TPU v7x, 16 devices: a whole 2x2x2 slice. The times are simulated.
16 devices in a mesh: ep: 16 (over z, y, x, core).
Axes of the slice: x: 2, y: 2, z: 2, core: 2. Of those that a mesh axis runs over, the one named last changes fastest.
Arguments:
- x_tokens: bfloat16 [131072, 384], P('ep')
- w_router: float32 [384, 32], replicated
- expert_idx: int32 [131072], P('ep')
- w_in: bfloat16 [32, 384, 1536], P('ep')
- w_out: bfloat16 [32, 1536, 384], P('ep')
- grad_y: bfloat16 [131072, 384], P('ep')
Outputs:
- output 1: bfloat16 [131072, 384], P('ep')
- output 2: float32 [32, 384, 1536], P('ep')
- output 3: float32 [32, 1536, 384], P('ep')
- output 4: float32 [384, 32], replicated
- output 5: float32 [], replicated
- output 6: float32 [], replicated
All inputs are finite; a program needn't handle non-finite values.
Results may differ from a plain program's by a relative error of at most 0.0126676.
Values are sent between devices in bfloat16 or wider.
A program may use at most 1 GiB of HBM per device.

v0:
```python
import jax
import jax.numpy as jnp
from jax import lax
from jax.sharding import PartitionSpec as P

AUX_WEIGHT = 0.01
Z_WEIGHT = 0.001


def route_slots(idx_group, num_experts, capacity):
    tokens = idx_group.shape[0]
    n_slots = num_experts * capacity
    onehot = (idx_group[:, None] == jnp.arange(num_experts, dtype=jnp.int32)[None, :]).astype(jnp.int32)
    position = jnp.sum(jnp.cumsum(onehot, axis=0) * onehot, axis=1) - 1
    tok_slot = jnp.where(position < capacity, idx_group * capacity + position, n_slots)
    slot_tok = jnp.full((n_slots,), tokens, jnp.int32).at[tok_slot].set(jnp.arange(tokens, dtype=jnp.int32), mode='drop')
    return onehot.astype(jnp.float32), tok_slot, slot_tok


def gather_rows(source, row_index):
    return jnp.take(source, row_index, axis=0, mode='fill', fill_value=0)


def router_grad(router_prob, onehot, gate_val, d_gate, log_norm, aux_vec, z_coef):
    spread = jnp.sum(router_prob * aux_vec, axis=-1, keepdims=True)
    return ((gate_val * d_gate)[..., None] * (onehot - router_prob)
            + router_prob * (aux_vec - spread)
            + (z_coef * log_norm)[..., None] * router_prob)


def solution(mesh):
    n_dev = mesh.shape['ep']

    def expert_layer(x_tokens, w_router, expert_idx, w_in, w_out, grad_y):
        tokens, d_model = x_tokens.shape
        n_local = w_in.shape[0]
        num_experts = n_local * n_dev
        capacity = (5 * tokens + 4 * num_experts - 1) // (4 * num_experts)
        total_tok = tokens * n_dev
        onehot, tok_slot, slot_tok = route_slots(expert_idx, num_experts, capacity)
        logits = jnp.dot(x_tokens, w_router, preferred_element_type=jnp.float32)
        router_prob = jax.nn.softmax(logits, axis=-1)
        log_norm = jax.nn.logsumexp(logits, axis=-1)
        gate_val = jnp.sum(router_prob * onehot, axis=-1)
        route_stats = jnp.concatenate([jnp.sum(onehot, axis=0), jnp.sum(router_prob, axis=0), jnp.sum(log_norm * log_norm)[None]])
        route_stats = lax.psum(route_stats, 'ep')

        sent_rows = gather_rows(x_tokens, slot_tok).reshape(n_dev, n_local, capacity, d_model)
        recv_rows = lax.all_to_all(sent_rows, 'ep', 0, 0, tiled=True)
        pre_act = jnp.einsum('pecd,edf->pecf', recv_rows, w_in, preferred_element_type=jnp.float32)
        hidden = jnp.maximum(pre_act, 0.0).astype(jnp.bfloat16)
        expert_out = jnp.einsum('pecf,efd->pecd', hidden, w_out, preferred_element_type=jnp.float32).astype(jnp.bfloat16)
        back_out = lax.all_to_all(expert_out, 'ep', 0, 0, tiled=True).reshape(num_experts * capacity, d_model)
        out_tok = gather_rows(back_out, tok_slot)
        gy_f32 = grad_y.astype(jnp.float32)
        d_gate = jnp.sum(out_tok.astype(jnp.float32) * gy_f32, axis=-1)

        scaled = (gate_val[:, None] * gy_f32).astype(jnp.bfloat16)
        sent_grad = gather_rows(scaled, slot_tok).reshape(n_dev, n_local, capacity, d_model)
        recv_grad = lax.all_to_all(sent_grad, 'ep', 0, 0, tiled=True)
        d_hidden = jnp.einsum('pecd,efd->pecf', recv_grad, w_out, preferred_element_type=jnp.float32)
        d_pre = jnp.where(hidden > 0, d_hidden, 0.0).astype(jnp.bfloat16)
        grad_w_out = jnp.einsum('pecf,pecd->efd', hidden, recv_grad, preferred_element_type=jnp.float32)
        grad_w_in = jnp.einsum('pecd,pecf->edf', recv_rows, d_pre, preferred_element_type=jnp.float32)
        d_rows = jnp.einsum('pecf,edf->pecd', d_pre, w_in, preferred_element_type=jnp.float32).astype(jnp.bfloat16)
        back_grad = lax.all_to_all(d_rows, 'ep', 0, 0, tiled=True).reshape(num_experts * capacity, d_model)
        dx_expert = gather_rows(back_grad, tok_slot)

        load_frac = route_stats[:num_experts] / total_tok
        mean_prob = route_stats[num_experts:2 * num_experts] / total_tok
        aux_loss = AUX_WEIGHT * num_experts * jnp.sum(load_frac * mean_prob)
        z_loss = Z_WEIGHT * route_stats[2 * num_experts] / total_tok
        aux_vec = AUX_WEIGHT * num_experts * load_frac / total_tok
        d_logits = router_grad(router_prob, onehot, gate_val, d_gate, log_norm, aux_vec, 2.0 * Z_WEIGHT / total_tok)
        dx_router = jnp.einsum('se,de->sd', d_logits, w_router)
        grad_x = (dx_expert.astype(jnp.float32) + dx_router).astype(jnp.bfloat16)
        grad_w_router = lax.psum(jnp.einsum('sd,se->de', x_tokens, d_logits, preferred_element_type=jnp.float32), 'ep')
        return grad_x, grad_w_in, grad_w_out, grad_w_router, aux_loss, z_loss

    return jax.shard_map(expert_layer, mesh=mesh,
                         in_specs=(P('ep', None), P(None, None), P('ep'), P('ep', None, None), P('ep', None, None), P('ep', None)),
                         out_specs=(P('ep', None), P('ep', None, None), P('ep', None, None), P(None, None), P(), P()),
                         check_vma=False)
```

profile of v0, /device:TPU:0, one launch (start us, length us, event | category | flops | bytes accessed | tf_op | source)
XLA Modules:
  0.0 869.1 jit_solution(8668346064062468521)
XLA Ops:
  2.6 17.1 %reduce-window.6 = s32[32,64,128]{2,1,0:T(8,128)S(1)} reduce-window(s32[32,64,128]{2,1,0:T(8,128)} %fusion.28, s32[]{:T(128)} %constant.18.clone.1), window={size=1x1x128 pad=0_0x0_0x127_0}, to_apply=%region_0.0 | reduce-window | flops 33292288 | bytes 2097156 | tf_op jit(solution)/shard_map/reduce-window
  23.5 30.5 %scatter_custom_fusion = s32[10240]{0:T(1024)S(1)} fusion(s32[8192]{0:T(1024)S(1)} %get-tuple-element.13, s32[8192]{0:T(1024)S(1)} %iota.11, s32[]{:T(128)} %constant.17.clone.1), kind=kCustom, calls=%fused_computation.67 | custom fusion | bytes 40964 | tf_op jit(solution)/shard_map/scatter | solution.py:16
  54.1 43.9 %gather_fusion = bf16[10240,384]{1,0:T(8,128)(2,1)} fusion(bf16[8192,384]{1,0:T(8,128)(2,1)} %param.10, s32[10240]{0:T(1024)S(1)} %fusion.41), kind=kCustom, calls=%fused_computation.clone | custom fusion | bytes 15769600 | tf_op jit(solution)/shard_map/jit(_take)/gather | solution.py:21
  98.0 5.4 broadcast_select_fusion.1
  103.4 97.2 %all_to_all.20 = bf16[16,2,320,384]{3,2,1,0:T(8,128)(2,1)S(1)} all-to-all(bf16[16,2,320,384]{3,2,1,0:T(8,128)(2,1)S(1)} %bitcast.68), channel_id=1, replica_groups=mesh['ep'=16] {'ep'}, dimensions={0} | all-to-all | bytes 15728640 | tf_op jit(solution)/shard_map/all_to_all | solution.py:49
  203.7 20.4 %maximum_convert_fusion = bf16[2,16,320,1536]{3,2,1,0:T(8,128)(2,1)} fusion(bf16[16,2,320,384]{3,2,1,0:T(8,128)(2,1)S(1)} %all_to_all.20, bf16[2,384,1536]{2,1,0:T(8,128)(2,1)S(1)} %copy-done.20), kind=kOutput, calls=%fused_computation.7 | convolution fusion | flops 12111052800 | bytes 41680896 | tf_op jit(solution)/shard_map/pecd,edf->pecf/dot_general | solution.py:50
  224.0 24.3 %convert_bitcast_fusion = bf16[16,2,320,384]{3,2,0,1:T(8,128)(2,1)} fusion(bf16[2,16,320,1536]{3,2,1,0:T(8,128)(2,1)} %maximum_convert_fusion, bf16[2,1536,384]{2,1,0:T(8,128)(2,1)S(1)} %copy-done), kind=kOutput, calls=%fused_computation.20 | convolution fusion | flops 12083527680 | bytes 41680896 | tf_op jit(solution)/shard_map/pecf,efd->pecd/dot_general | solution.py:52
  248.3 7.4 copy.19
  259.2 4.8 fusion.47
  267.4 119.0 %psum.14 = f32[65]{0:T(128)S(1)} all-reduce(f32[65]{0:T(128)S(1)} %pad_maximum_fusion), channel_id=1, replica_groups=mesh['ep'=16] {'ep'}, use_global_device_ids=true, to_apply=%region_12.15 | all-reduce | flops 65 | bytes 520 | tf_op jit(solution)/shard_map/psum | solution.py:46
  390.2 36.8 %gather_fusion.3 = bf16[8192,384]{1,0:T(8,128)(2,1)} fusion(bf16[10240,384]{1,0:T(8,128)(2,1)} %bitcast.14, s32[8192]{0:T(1024)S(1)} %broadcast_clamp_fusion), kind=kCustom, calls=%fused_computation.3.clone | custom fusion | bytes 12615680 | tf_op jit(solution)/shard_map/jit(_take)/gather | solution.py:21
  427.0 10.2 %fusion.8 = (f32[8192]{0:T(1024)S(1)}, bf16[8192,384]{1,0:T(8,128)(2,1)}) fusion(bf16[8192,384]{1,0:T(8,128)(2,1)} %param.15, bf16[8192,384]{1,0:T(8,128)(2,1)} %gather_fusion.3, pred[8192]{0:T(1024)(128)(4,1)S(1)} %get-tuple-element.12, f32[8192]{0:T(1024)} %get-tuple-element.9), kind=kLoop, calls=%fused_computation.17 | loop fusion | flops 22011904 | bytes 18948096 | tf_op jit(solution)/shard_map/reduce_sum | solution.py:56
  437.2 43.9 %gather_fusion.1 = bf16[10240,384]{1,0:T(8,128)(2,1)} fusion(bf16[8192,384]{1,0:T(8,128)(2,1)} %get-tuple-element.15, s32[10240]{0:T(1024)S(1)} %fusion.41), kind=kCustom, calls=%fused_computation.2.clone | custom fusion | bytes 15769600 | tf_op jit(solution)/shard_map/jit(_take)/gather | solution.py:21
  481.2 5.4 broadcast_select_fusion
  486.6 95.2 %all_to_all.21 = bf16[16,2,320,384]{3,2,1,0:T(8,128)(2,1)} all-to-all(bf16[16,2,320,384]{3,2,1,0:T(8,128)(2,1)S(1)} %bitcast.67), channel_id=1, replica_groups=mesh['ep'=16] {'ep'}, dimensions={0} | all-to-all | bytes 15728640 | tf_op jit(solution)/shard_map/all_to_all | solution.py:60
  581.8 30.9 %fusion = bf16[16,2,320,1536]{3,2,0,1:T(8,128)(2,1)} fusion(bf16[2,16,320,1536]{3,2,1,0:T(8,128)(2,1)} %maximum_convert_fusion, bf16[16,2,320,384]{3,2,1,0:T(8,128)(2,1)} %all_to_all.21, bf16[2,1536,384]{2,1,0:T(8,128)(2,1)S(1)} %copy-done), kind=kOutput, calls=%fused_computation.6 | convolution fusion | flops 12126781440 | bytes 73138176 | tf_op jit(solution)/shard_map/pecd,efd->pecf/dot_general | solution.py:61
  612.7 24.9 %convert_bitcast_fusion.1 = bf16[16,2,320,384]{3,2,0,1:T(8,128)(2,1)} fusion(bf16[16,2,320,1536]{3,2,0,1:T(8,128)(2,1)} %fusion, bf16[2,384,1536]{2,1,0:T(8,128)(2,1)} %param.13), kind=kOutput, calls=%fused_computation.21 | convolution fusion | flops 12083527680 | bytes 41680896 | tf_op jit(solution)/shard_map/pecf,edf->pecd/dot_general | solution.py:65
  637.6 7.5 copy.18
  650.7 3.9 convolution_bitcast_fusion
  654.6 122.0 %psum.15 = f32[384,32]{0,1:T(8,128)} all-reduce(f32[384,32]{0,1:T(8,128)S(1)} %convolution_bitcast_fusion), channel_id=1, replica_groups=mesh['ep'=16] {'ep'}, use_global_device_ids=true, to_apply=%region_14.17 | all-reduce | flops 12288 | bytes 98304 | tf_op jit(solution)/shard_map/psum | solution.py:77
  776.6 20.7 %fusion.14 = f32[2,384,1536]{2,1,0:T(8,128)} fusion(bf16[16,2,320,384]{3,2,1,0:T(8,128)(2,1)} %copy-done.2, bf16[16,2,320,1536]{3,2,0,1:T(8,128)(2,1)} %fusion), kind=kOutput, calls=%fused_computation.26 | convolution fusion | flops 12079595520 | bytes 44040192 | tf_op jit(solution)/shard_map/pecd,pecf->edf/dot_general | solution.py:64
  797.3 24.2 %fusion.17 = f32[2,1536,384]{2,1,0:T(8,128)} fusion(bf16[16,2,320,384]{3,2,1,0:T(8,128)(2,1)} %all_to_all.21, bf16[2,16,320,1536]{3,2,1,0:T(8,128)(2,1)} %maximum_convert_fusion), kind=kOutput, calls=%fused_computation.27 | convolution fusion | flops 12079595520 | bytes 44040192 | tf_op jit(solution)/shard_map/pecf,pecd->efd/dot_general | solution.py:63
  821.5 36.9 %gather_fusion.2 = bf16[8192,384]{1,0:T(8,128)(2,1)} fusion(bf16[10240,384]{1,0:T(8,128)(2,1)} %bitcast.11, s32[8192]{0:T(1024)S(1)} %copy-done.5), kind=kCustom, calls=%fused_computation.1.clone | custom fusion | bytes 12615680 | tf_op jit(solution)/shard_map/jit(_take)/gather | solution.py:21
  858.4 7.9 add_convert_fusion
  (65 shorter events, 23.8 us)
Async XLA Ops:
  0.6 223.4 %copy-start = (bf16[2,1536,384]{2,1,0:T(8,128)(2,1)S(1)}, bf16[2,1536,384]{2,1,0:T(8,128)(2,1)}, u32[]{:S(2)}) copy-start(bf16[2,1536,384]{2,1,0:T(8,128)(2,1)} %param.14) | copy-start | bytes 7077892
  23.5 74.4 %copy-start.9 = (s32[8192]{0:T(1024)}, s32[8192]{0:T(1024)S(1)}, u32[]{:S(2)}) copy-start(s32[8192]{0:T(1024)S(1)} %get-tuple-element.13) | copy-start | bytes 98308
  23.5 403.5 %copy-start.12 = (pred[8192]{0:T(1024)(128)(4,1)}, pred[8192]{0:T(1024)(128)(4,1)S(1)}, u32[]{:S(2)}) copy-start(pred[8192]{0:T(1024)(128)(4,1)S(1)} %get-tuple-element.12) | copy-start | bytes 24580
  54.0 43.9 %copy-start.10 = (pred[10240]{0:T(1024)(128)(4,1)}, pred[10240]{0:T(1024)(128)(4,1)S(1)}, u32[]{:S(2)}) copy-start(pred[10240]{0:T(1024)(128)(4,1)S(1)} %compare_and_fusion) | copy-start | bytes 30724
  103.4 100.3 %copy-start.20 = (bf16[2,384,1536]{2,1,0:T(8,128)(2,1)S(1)}, bf16[2,384,1536]{2,1,0:T(8,128)(2,1)}, u32[]{:S(2)}) copy-start(bf16[2,384,1536]{2,1,0:T(8,128)(2,1)} %param.13) | copy-start | bytes 7077892
  200.6 3.1 copy-start.2
  255.7 134.4 %all-to-all-start.3 = ((bf16[16,2,320,384]{3,2,1,0:T(8,128)(2,1)}), bf16[16,2,320,384]{3,2,1,0:T(8,128)(2,1)}, u32[]{:S(2)}, u32[]{:S(2)}) async-start(bf16[16,2,320,384]{3,2,1,0:T(8,128)(2,1)} %copy.19), calls=%async_computation.3 | async-start | bytes 15728640 | tf_op jit(solution)/shard_map/all_to_all | solution.py:53
  259.2 5.7 copy-start.3
  264.2 0.6 copy-start.7
  386.3 0.5 copy-start.18
  387.5 0.8 copy-start.16
  388.3 38.7 %copy-start.4 = (s32[8192]{0:T(1024)}, s32[8192]{0:T(1024)S(1)}, u32[]{:S(2)}) copy-start(s32[8192]{0:T(1024)S(1)} %broadcast_clamp_fusion) | copy-start | bytes 98308
  645.0 3.7 copy-start.19
  645.0 5.6 copy-start.6
  645.0 5.7 copy-start.8
  645.0 5.7 copy-start.13
  645.0 5.7 copy-start.14
  645.0 5.7 copy-start.17
  645.0 176.5 %all-to-all-start.2 = ((bf16[16,2,320,384]{3,2,1,0:T(8,128)(2,1)}), bf16[16,2,320,384]{3,2,1,0:T(8,128)(2,1)}, u32[]{:S(2)}, u32[]{:S(2)}) async-start(bf16[16,2,320,384]{3,2,1,0:T(8,128)(2,1)} %copy.18), calls=%async_computation.2 | async-start | bytes 15728640 | tf_op jit(solution)/shard_map/all_to_all | solution.py:66
  650.7 146.6 %copy-start.15 = (f32[8192]{0:T(1024)}, f32[8192]{0:T(1024)S(1)}, u32[]{:S(2)}) copy-start(f32[8192]{0:T(1024)S(1)} %mul.79) | copy-start | bytes 98308
  797.3 24.3 %copy-start.5 = (s32[8192]{0:T(1024)S(1)}, s32[8192]{0:T(1024)}, u32[]{:S(2)}) copy-start(s32[8192]{0:T(1024)} %copy-done.4) | copy-start | bytes 98308
  821.5 36.9 %copy-start.11 = (f32[384,32]{0,1:T(8,128)S(1)}, f32[384,32]{0,1:T(8,128)}, u32[]{:S(2)}) copy-start(f32[384,32]{0,1:T(8,128)} %param.11) | copy-start | bytes 147460
  858.4 7.9 copy-start.1
where the time goes:
time: 876 us; the launch traced here: 869 us
  blocking collectives  433 us (49%)
  local copies, waits for them, and re-layouts  213 us (24%)
  matrix products  162 us (18%)
  other arithmetic  49 us (6%)
    gather x4, local copies, waits for them, and re-layouts, gather_rows(): return jnp.take(source, row_index, axis=0, mode='fill', fill_value=0)  161 us
    psum x1, blocking collectives, expert_layer(): lax.psum(jnp.einsum('sd,se->de', x_tokens, d_logits, preferred_element_ty...  122 us
    psum x1, blocking collectives, expert_layer(): route_stats = lax.psum(route_stats, 'ep')  119 us
    all_to_all x1, blocking collectives, expert_layer(): recv_rows = lax.all_to_all(sent_rows, 'ep', 0, 0, tiled=True)  97.2 us
    all_to_all x1, blocking collectives, expert_layer(): recv_grad = lax.all_to_all(sent_grad, 'ep', 0, 0, tiled=True)  95.2 us
    dot_general x1, matrix products, expert_layer(): jnp.einsum('pecd,efd->pecf', recv_grad, w_out, preferred_element_type=jnp...  30.9 us
    scatter x1, local copies, waits for them, and re-layouts, route_slots(): jnp.full((n_slots,), tokens, jnp.int32).at[tok_slot]  30.5 us
    dot_general x1, matrix products, expert_layer(): jnp.einsum('pecf,edf->pecd', d_pre, w_in, preferred_element_type=jnp.floa...  24.9 us
  transfers between devices with their start and end apart: 2, of which 0 were waited for; matrix products, arithmetic and copies ran while one was open for 7% of the time, Pallas kernels for 0%

commit v1 on v0

--- a/solution.py
+++ b/solution.py
@@ -1,10 +1,16 @@
+import functools
+
 import jax
 import jax.numpy as jnp
 from jax import lax
+from jax.experimental import pallas as pl
+from jax.experimental.pallas import tpu as pltpu
 from jax.sharding import PartitionSpec as P
 
 AUX_WEIGHT = 0.01
 Z_WEIGHT = 0.001
+MESH = pl.DeviceIdType.MESH
+F_CHUNK = 512
 
 
 def route_slots(idx_group, num_experts, capacity):
@@ -28,6 +34,189 @@
             + (z_coef * log_norm)[..., None] * router_prob)
 
 
+def nt_dot(a, b):
+    return lax.dot_general(a, b, (((1,), (1,)), ((), ())), preferred_element_type=jnp.float32)
+
+
+def exchange_kernel(n, n_local, xd_ref, gate_ref, w_in_ref, w_out_ref,
+                    gw_in_ref, gw_out_t_ref, back_ref, g_back_ref,
+                    xr, gate_r, g_s,
+                    fwd_send, fwd_recv, gate_send, gate_recv,
+                    ret_send, ret_recv, g_send, g_recv, loc_sem):
+    me = lax.axis_index('ep')
+    cap, d_model = xr.shape[3], xr.shape[4]
+    d_ff = w_in_ref.shape[2]
+
+    def peer_of(k):
+        out = 0
+        bit = 1
+        while bit < n:
+            mine = (me // bit) % 2
+            flip = (k // bit) % 2
+            out = out + bit * (mine + flip - 2 * mine * flip)
+            bit *= 2
+        return out
+
+    half = n // 2
+
+    def rel_of(j):
+        return (j % half) * 2 + j // half
+
+    def fwd_copy(k, e, peer):
+        return pltpu.make_async_remote_copy(
+            src_ref=xd_ref.at[peer, e], dst_ref=xr.at[k, e],
+            send_sem=fwd_send.at[k * n_local + e], recv_sem=fwd_recv.at[k * n_local + e],
+            device_id=(peer,), device_id_type=MESH)
+
+    def gate_copy(k, peer):
+        return pltpu.make_async_remote_copy(
+            src_ref=gate_ref.at[peer], dst_ref=gate_r.at[k],
+            send_sem=gate_send.at[k], recv_sem=gate_recv.at[k],
+            device_id=(peer,), device_id_type=MESH)
+
+    def ret_copy(k, e, peer):
+        return pltpu.make_async_remote_copy(
+            src_ref=xr.at[k, e, 0], dst_ref=back_ref.at[me, e],
+            send_sem=ret_send.at[k * n_local + e], recv_sem=ret_recv.at[k * n_local + e],
+            device_id=(peer,), device_id_type=MESH)
+
+    def g_copy(k, peer):
+        return pltpu.make_async_remote_copy(
+            src_ref=g_s.at[k], dst_ref=g_back_ref.at[me],
+            send_sem=g_send.at[k], recv_sem=g_recv.at[k],
+            device_id=(peer,), device_id_type=MESH)
+
+    own_in = [pltpu.make_async_copy(xd_ref.at[me, e], xr.at[0, e], loc_sem.at[e]) for e in range(n_local)]
+    own_gate = pltpu.make_async_copy(gate_ref.at[me], gate_r.at[0], loc_sem.at[n_local])
+    for c in own_in:
+        c.start()
+    own_gate.start()
+
+    def issue(j, carry):
+        k = rel_of(j)
+        peer = peer_of(k)
+        gate_copy(k, peer).start()
+        for e in range(n_local):
+            fwd_copy(k, e, peer).start()
+        return carry
+
+    lax.fori_loop(1, n, issue, 0)
+
+    gw_in_ref[...] = jnp.zeros_like(gw_in_ref)
+    gw_out_t_ref[...] = jnp.zeros_like(gw_out_t_ref)
+    g_s[...] = jnp.zeros_like(g_s)
+    for c in own_in:
+        c.wait()
+    own_gate.wait()
+
+    lanes = gate_r.shape[2]
+
+    def tile(k, e):
+        eye = (lax.broadcasted_iota(jnp.int32, (cap, lanes), 0)
+               == lax.broadcasted_iota(jnp.int32, (cap, lanes), 1))
+        rows = xr[k, e, 0]
+        dy = xr[k, e, 1].astype(jnp.float32)
+        gate_row = gate_r[k, pl.ds(e, 1), :]
+        gate_col = jnp.sum(jnp.where(eye, gate_row, 0.0), axis=1, keepdims=True)
+        grad = (gate_col * dy).astype(jnp.bfloat16)
+        rows_t = rows.T
+        grad_t = grad.T
+        out = jnp.zeros((cap, d_model), jnp.float32)
+        d_rows = jnp.zeros((cap, d_model), jnp.float32)
+        for f in range(0, d_ff, F_CHUNK):
+            fs = pl.ds(f, F_CHUNK)
+            w_a = w_in_ref[e, :, fs]
+            w_b = w_out_ref[e, fs, :]
+            pre = jnp.dot(rows, w_a, preferred_element_type=jnp.float32)
+            hid = jnp.maximum(pre, 0.0).astype(jnp.bfloat16)
+            out = out + jnp.dot(hid, w_b, preferred_element_type=jnp.float32)
+            d_hid = nt_dot(grad, w_b)
+            d_pre = jnp.where(hid.astype(jnp.float32) > 0, d_hid, 0.0).astype(jnp.bfloat16)
+            gw_out_t_ref[e, :, fs] += jnp.dot(grad_t, hid, preferred_element_type=jnp.float32)
+            gw_in_ref[e, :, fs] += jnp.dot(rows_t, d_pre, preferred_element_type=jnp.float32)
+            d_rows = d_rows + nt_dot(d_pre, w_a)
+        out = out.astype(jnp.bfloat16).astype(jnp.float32)
+        g_col = jnp.sum(out * dy, axis=1, keepdims=True)
+        g_s[k, pl.ds(e, 1), :] = jnp.sum(jnp.where(eye, g_col, 0.0), axis=0, keepdims=True)
+        xr[k, e, 0] = d_rows.astype(jnp.bfloat16)
+
+    def step(t, carry):
+        j = t // n_local
+        e = t % n_local
+        k = rel_of(j)
+        peer = peer_of(k)
+
+        @pl.when(j > 0)
+        def _():
+            @pl.when(e == 0)
+            def _():
+                gate_copy(k, peer).wait_recv()
+            fwd_copy(k, e, peer).wait_recv()
+
+        tile(k, e)
+
+        @pl.when(j > 0)
+        def _():
+            ret_copy(k, e, peer).start()
+
+            @pl.when(e == n_local - 1)
+            def _():
+                g_copy(k, peer).start()
+        return carry
+
+    lax.fori_loop(0, n * n_local, step, 0)
+
+    own_out = [pltpu.make_async_copy(xr.at[0, e, 0], back_ref.at[me, e], loc_sem.at[e]) for e in range(n_local)]
+    own_g = pltpu.make_async_copy(g_s.at[0], g_back_ref.at[me], loc_sem.at[n_local])
+    for c in own_out:
+        c.start()
+    own_g.start()
+    for c in own_out:
+        c.wait()
+    own_g.wait()
+
+    def drain(j, carry):
+        k = rel_of(j)
+        peer = peer_of(k)
+        gate_copy(k, peer).wait_send()
+        g_copy(k, peer).wait()
+        for e in range(n_local):
+            fwd_copy(k, e, peer).wait_send()
+            ret_copy(k, e, peer).wait()
+        return carry
+
+    lax.fori_loop(1, n, drain, 0)
+
+
+def exchange(xd, gates, w_in, w_out, n_dev):
+    n_local, d_model, d_ff = w_in.shape
+    cap = xd.shape[3]
+    lanes = gates.shape[2]
+    any_spec = pl.BlockSpec(memory_space=pl.ANY)
+    vmem_spec = pl.BlockSpec(memory_space=pltpu.VMEM)
+    pairs = n_dev * n_local
+    dma = pltpu.SemaphoreType.DMA
+    return pl.pallas_call(
+        functools.partial(exchange_kernel, n_dev, n_local),
+        out_shape=(jax.ShapeDtypeStruct((n_local, d_model, d_ff), jnp.float32),
+                   jax.ShapeDtypeStruct((n_local, d_model, d_ff), jnp.float32),
+                   jax.ShapeDtypeStruct((n_dev, n_local, cap, d_model), jnp.bfloat16),
+                   jax.ShapeDtypeStruct((n_dev, 8, lanes), jnp.float32)),
+        in_specs=[any_spec, any_spec, vmem_spec, vmem_spec],
+        out_specs=(vmem_spec, vmem_spec, any_spec, any_spec),
+        scratch_shapes=[
+            pltpu.VMEM((n_dev, n_local, 2, cap, d_model), jnp.bfloat16),
+            pltpu.VMEM((n_dev, 8, lanes), jnp.float32),
+            pltpu.VMEM((n_dev, 8, lanes), jnp.float32),
+            dma((pairs,)), dma((pairs,)), dma((n_dev,)), dma((n_dev,)),
+            dma((pairs,)), dma((pairs,)), dma((n_dev,)), dma((n_dev,)),
+            dma((n_local + 1,)),
+        ],
+        compiler_params=pltpu.CompilerParams(has_side_effects=True, vmem_limit_bytes=60 * 1024 * 1024),
+        name='exchange',
+    )(xd, gates, w_in, w_out)
+
+
 def solution(mesh):
     n_dev = mesh.shape['ep']
 
@@ -37,6 +226,7 @@
         num_experts = n_local * n_dev
         capacity = (5 * tokens + 4 * num_experts - 1) // (4 * num_experts)
         total_tok = tokens * n_dev
+        lanes = -(-capacity // 128) * 128
         onehot, tok_slot, slot_tok = route_slots(expert_idx, num_experts, capacity)
         logits = jnp.dot(x_tokens, w_router, preferred_element_type=jnp.float32)
         router_prob = jax.nn.softmax(logits, axis=-1)
@@ -45,26 +235,15 @@
         route_stats = jnp.concatenate([jnp.sum(onehot, axis=0), jnp.sum(router_prob, axis=0), jnp.sum(log_norm * log_norm)[None]])
         route_stats = lax.psum(route_stats, 'ep')
 
-        sent_rows = gather_rows(x_tokens, slot_tok).reshape(n_dev, n_local, capacity, d_model)
-        recv_rows = lax.all_to_all(sent_rows, 'ep', 0, 0, tiled=True)
-        pre_act = jnp.einsum('pecd,edf->pecf', recv_rows, w_in, preferred_element_type=jnp.float32)
-        hidden = jnp.maximum(pre_act, 0.0).astype(jnp.bfloat16)
-        expert_out = jnp.einsum('pecf,efd->pecd', hidden, w_out, preferred_element_type=jnp.float32).astype(jnp.bfloat16)
-        back_out = lax.all_to_all(expert_out, 'ep', 0, 0, tiled=True).reshape(num_experts * capacity, d_model)
-        out_tok = gather_rows(back_out, tok_slot)
-        gy_f32 = grad_y.astype(jnp.float32)
-        d_gate = jnp.sum(out_tok.astype(jnp.float32) * gy_f32, axis=-1)
-
-        scaled = (gate_val[:, None] * gy_f32).astype(jnp.bfloat16)
-        sent_grad = gather_rows(scaled, slot_tok).reshape(n_dev, n_local, capacity, d_model)
-        recv_grad = lax.all_to_all(sent_grad, 'ep', 0, 0, tiled=True)
-        d_hidden = jnp.einsum('pecd,efd->pecf', recv_grad, w_out, preferred_element_type=jnp.float32)
-        d_pre = jnp.where(hidden > 0, d_hidden, 0.0).astype(jnp.bfloat16)
-        grad_w_out = jnp.einsum('pecf,pecd->efd', hidden, recv_grad, preferred_element_type=jnp.float32)
-        grad_w_in = jnp.einsum('pecd,pecf->edf', recv_rows, d_pre, preferred_element_type=jnp.float32)
-        d_rows = jnp.einsum('pecf,edf->pecd', d_pre, w_in, preferred_element_type=jnp.float32).astype(jnp.bfloat16)
-        back_grad = lax.all_to_all(d_rows, 'ep', 0, 0, tiled=True).reshape(num_experts * capacity, d_model)
-        dx_expert = gather_rows(back_grad, tok_slot)
+        slot_shape = (n_dev, n_local, 1, capacity, d_model)
+        xd = jnp.concatenate([gather_rows(x_tokens, slot_tok).reshape(slot_shape),
+                              gather_rows(grad_y, slot_tok).reshape(slot_shape)], axis=2)
+        gate_slot = gather_rows(gate_val, slot_tok).reshape(n_dev, n_local, capacity)
+        gates = jnp.pad(gate_slot, ((0, 0), (0, 8 - n_local), (0, lanes - capacity)))
+        grad_w_in, grad_w_out_t, back, g_back = exchange(xd, gates, w_in, w_out, n_dev)
+        grad_w_out = jnp.swapaxes(grad_w_out_t, 1, 2)
+        d_gate = gather_rows(g_back[:, :n_local, :capacity].reshape(num_experts * capacity), tok_slot)
+        dx_expert = gather_rows(back.reshape(num_experts * capacity, d_model), tok_slot)
 
         load_frac = route_stats[:num_experts] / total_tok
         mean_prob = route_stats[num_experts:2 * num_experts] / total_tok

time: 876 us -> 714 us (0.82)
  blocking collectives: 433 us -> 68.9 us
  Pallas kernels: 0 us -> 326 us
  matrix products: 162 us -> 13.6 us
  local copies, waits for them, and re-layouts: 213 us -> 272 us
  other arithmetic: 49 us -> 29.3 us
    pallas_call x0 -> x1, Pallas kernels: none -> 326 us  [exchange(): pl.pallas_call(functools.partial(exchange_kernel, n_dev, n_local), out_sh...]
    all_to_all x2 -> x0, blocking collectives: 192 us -> none  [the longest x1 97.2 us: expert_layer(): recv_rows = lax.all_to_all(sent_rows, 'ep', 0, 0, tiled=True)]
    dot_general x6 -> x0, matrix products: 145 us -> none  [the longest x1 30.9 us: expert_layer(): jnp.einsum('pecd,efd->pecf', recv_grad, w_out, preferred_element_type=jnp...]
    psum x1, blocking collectives: 122 us -> 34.3 us  [expert_layer(): lax.psum(jnp.einsum('sd,se->de', x_tokens, d_logits, preferred_element_ty...]
    psum x1, blocking collectives: 119 us -> 34.6 us  [expert_layer(): route_stats = lax.psum(route_stats, 'ep')]
    gather x4 -> x5, local copies, waits for them, and re-layouts: 161 us -> 227 us  [gather_rows(): return jnp.take(source, row_index, axis=0, mode='fill', fill_value=0)]
    convert_element_type x2 -> x0, local copies, waits for them, and re-layouts: 14.8 us -> none  [the longest x1 7.45 us: expert_layer(): jnp.einsum('pecf,edf->pecd', d_pre, w_in, preferred_element_type=jnp.floa...]
    reduce_sum x1 -> x0, other arithmetic: 10.2 us -> none  [expert_layer(): d_gate = jnp.sum(out_tok.astype(jnp.float32) * gy_f32, axis=-1)]
  transfers between devices with their start and end apart: 2 -> 0, of which waited for: 0 -> 0; matrix products, arithmetic and copies ran while one was open for 7% -> 0% of each run, Pallas kernels for 0% -> 0%
where the time goes in v1:
time: 714 us; the launch traced here: 713 us
  Pallas kernels  326 us (46%)
  local copies, waits for them, and re-layouts  272 us (38%)
  blocking collectives  68.9 us (10%)
  other arithmetic  29.3 us (4%)
  matrix products  13.6 us (2%)
    pallas_call x1, Pallas kernels, exchange(): pl.pallas_call(functools.partial(exchange_kernel, n_dev, n_local), out_sh...  326 us
    gather x5, local copies, waits for them, and re-layouts, gather_rows(): return jnp.take(source, row_index, axis=0, mode='fill', fill_value=0)  227 us
    psum x1, blocking collectives, expert_layer(): route_stats = lax.psum(route_stats, 'ep')  34.6 us
    psum x1, blocking collectives, expert_layer(): lax.psum(jnp.einsum('sd,se->de', x_tokens, d_logits, preferred_element_ty...  34.3 us
    scatter x1, local copies, waits for them, and re-layouts, route_slots(): jnp.full((n_slots,), tokens, jnp.int32).at[tok_slot]  30.5 us

profile of v1, /device:TPU:0, one launch (start us, length us, event | category | flops | bytes accessed | tf_op | source)
XLA Modules:
  0.0 713.4 jit_solution(9216125412592835898)
XLA Ops:
  0.7 0.9 fusion.2
  1.6 9.5 %reduce-window.6 = s32[32,64,128]{2,1,0:T(8,128)S(1)} reduce-window(s32[32,64,128]{2,1,0:T(8,128)S(1)} %fusion.2, s32[]{:T(128)} %constant.48.clone.1), window={size=1x1x128 pad=0_0x0_0x127_0}, to_apply=%region_0.0 | reduce-window | flops 33292288 | bytes 2097156 | tf_op jit(solution)/shard_map/reduce-window
  11.1 0.9 slice_reduce_fusion
  12.6 0.8 fusion.1
  13.4 30.5 %scatter_custom_fusion = s32[10240]{0:T(1024)S(1)} fusion(s32[8192]{0:T(1024)S(1)} %get-tuple-element.34, s32[8192]{0:T(1024)S(1)} %iota.11, s32[]{:T(128)} %constant.59.clone.1), kind=kCustom, calls=%fused_computation.47 | custom fusion | bytes 40964 | tf_op jit(solution)/shard_map/scatter | solution.py:22
  43.9 4.8 fusion.21
  50.2 0.7 pad_maximum_fusion.1
  50.9 34.6 %psum.14 = f32[65]{0:T(128)S(1)} all-reduce(f32[65]{0:T(128)S(1)} %pad_maximum_fusion.1), channel_id=1, replica_groups=mesh['ep'=16] {'ep'}, use_global_device_ids=true, to_apply=%region_11.13 | all-reduce | flops 65 | bytes 520 | tf_op jit(solution)/shard_map/psum | solution.py:236
  86.8 0.7 multiply_reduce_fusion.3
  88.6 56.8 %gather_fusion = f32[10240]{0:T(1024)S(1)} fusion(f32[8192]{0:T(1024)S(1)} %get-tuple-element.28, s32[10240]{0:T(1024)S(1)} %fusion.15), kind=kCustom, calls=%fused_computation.2 | custom fusion | bytes 122880 | tf_op jit(solution)/shard_map/jit(_take)/gather | solution.py:27
  145.5 0.7 pad.4.gate_ref
  146.2 43.9 %gather_fusion.4 = bf16[10240,384]{1,0:T(8,128)(2,1)} fusion(bf16[8192,384]{1,0:T(8,128)(2,1)} %param.13, s32[10240]{0:T(1024)S(1)} %fusion.15), kind=kCustom, calls=%fused_computation.1.clone | custom fusion | bytes 15769600 | tf_op jit(solution)/shard_map/jit(_take)/gather | solution.py:27
  190.1 43.9 %gather_fusion.3 = bf16[10240,384]{1,0:T(8,128)(2,1)} fusion(bf16[8192,384]{1,0:T(8,128)(2,1)} %param.8, s32[10240]{0:T(1024)S(1)} %fusion.15), kind=kCustom, calls=%fused_computation.clone | custom fusion | bytes 15769600 | tf_op jit(solution)/shard_map/jit(_take)/gather | solution.py:27
  234.0 7.4 %broadcast_select_fusion.1 = (bf16[10240,384]{1,0:T(8,128)(2,1)S(1)}, bf16[10240,384]{1,0:T(8,128)(2,1)S(1)}) fusion(bf16[10240,384]{1,0:T(8,128)(2,1)} %gather_fusion.3, pred[10240]{0:T(1024)(128)(4,1)S(1)} %get-tuple-element.36, bf16[10240,384]{1,0:T(8,128)(2,1)} %gather_fusion.4), kind=kLoop, calls=%fused_computation.9 | loop fusion | flops 7864320 | bytes 31467520 | tf_op jit(solution)/shard_map/jit(_take)/select_n | solution.py:27
  241.3 6.8 pad_maximum_fusion.xd_ref
  248.1 325.6 %exchange.1 = (f32[2,384,1536]{2,1,0:T(8,128)}, f32[2,384,1536]{2,1,0:T(8,128)}, bf16[16,2,320,384]{3,2,1,0:T(8,128)(2,1)}, f32[16,8,384]{2,1,0:T(8,128)}) custom-call(bf16[16,2,2,320,384]{4,3,2,1,0:T(8,128)(2,1)} %pad_maximum_fusion.xd_ref, f32[16,8,384]{2,1,0:T(8,128)} %pad.4.gate_ref, bf16[2,384,1536]{2,1,0:T(8,128)(2,1)} %w_in_ref.1, ...), custom_call_target="tpu_custom_call" | custom-call | tf_op jit(solution)/shard_map/exchange/pallas_call | solution.py:199
  573.7 36.8 %gather_fusion.1 = bf16[8192,384]{1,0:T(8,128)(2,1)} fusion(bf16[10240,384]{1,0:T(8,128)(2,1)} %bitcast.30, s32[8192]{0:T(1024)S(1)} %get-tuple-element.33), kind=kCustom, calls=%fused_computation.3 | custom fusion | bytes 12615680 | tf_op jit(solution)/shard_map/jit(_take)/gather | solution.py:27
  610.6 0.9 slice.20
  611.6 45.5 %gather_fusion.2 = f32[8192]{0:T(1024)S(1)} fusion(f32[10240]{0:T(1024)S(1)} %reshape.87, s32[8192]{0:T(1024)S(1)} %get-tuple-element.33), kind=kCustom, calls=%fused_computation.4 | custom fusion | bytes 98304 | tf_op jit(solution)/shard_map/jit(_take)/gather | solution.py:27
  657.2 7.7 %add_convert_fusion = bf16[8192,384]{1,0:T(8,128)(2,1)} fusion(f32[384,32]{0,1:T(8,128)S(1)} %copy-done, bf16[8192,384]{1,0:T(8,128)(2,1)} %gather_fusion.1, pred[8192]{0:T(1024)(128)(4,1)S(1)} %get-tuple-element.32, f32[8192]{0:T(1024)S(1)} %get-tuple-element.37, f32[8192]{0:T(1024)S(1)} %get-tuple-element.27, f32[32]{0:T(128)S(1)} %get-tuple-element.42, ...), kind=kOutput, calls=%fused_computation.7 | convolution fusion | flops 217055232 | bytes 13885568 | tf_op jit(solution)/shard_map/se,de->sd/dot_general | solution.py:254
  664.9 1.1 convolution_bitcast_fusion
  666.0 34.3 %psum.15 = f32[384,32]{0,1:T(8,128)} all-reduce(f32[384,32]{0,1:T(8,128)S(1)} %convolution_bitcast_fusion), channel_id=1, replica_groups=mesh['ep'=16] {'ep'}, use_global_device_ids=true, to_apply=%region_13.15 | all-reduce | flops 12288 | bytes 98304 | tf_op jit(solution)/shard_map/psum | solution.py:256
  700.3 6.0 copy.13
  706.3 4.8 copy.17
  (24 shorter events, 3.4 us)
Async XLA Ops:
  0.6 43.3 %copy-start = (f32[384,32]{0,1:T(8,128)S(1)}, f32[384,32]{0,1:T(8,128)}, u32[]{:S(2)}) copy-start(f32[384,32]{0,1:T(8,128)} %param.9) | copy-start | bytes 147460
  0.6 12.0 %copy-start.1 = (s32[8192]{0:T(1024)S(1)}, s32[8192]{0:T(1024)}, u32[]{:S(2)}) copy-start(s32[8192]{0:T(1024)} %param.10) | copy-start | bytes 98308
  611.6 53.2 %slice-start = ((s8[6291456]{0:T(1024)(128)(4,1)}), s8[2097152]{0:T(1024)(128)(4,1)S(1)}, s32[]{:S(2)}) async-start(s8[6291456]{0:T(1024)(128)(4,1)} %bitcast.28), calls=%async_computation | async-start | bytes 4194304
  657.2 7.7 %slice-start.1 = ((s8[6291456]{0:T(1024)(128)(4,1)}), s8[4194304]{0:T(1024)(128)(4,1)S(1)}, s32[]{:S(2)}) async-start(s8[6291456]{0:T(1024)(128)(4,1)} %bitcast.28), calls=%async_computation.1 | async-start | bytes 8388608

commit v2 on v1

--- a/solution.py
+++ b/solution.py
@@ -11,51 +11,282 @@
 Z_WEIGHT = 0.001
 MESH = pl.DeviceIdType.MESH
 F_CHUNK = 512
-
-
-def route_slots(idx_group, num_experts, capacity):
-    tokens = idx_group.shape[0]
-    n_slots = num_experts * capacity
-    onehot = (idx_group[:, None] == jnp.arange(num_experts, dtype=jnp.int32)[None, :]).astype(jnp.int32)
-    position = jnp.sum(jnp.cumsum(onehot, axis=0) * onehot, axis=1) - 1
-    tok_slot = jnp.where(position < capacity, idx_group * capacity + position, n_slots)
-    slot_tok = jnp.full((n_slots,), tokens, jnp.int32).at[tok_slot].set(jnp.arange(tokens, dtype=jnp.int32), mode='drop')
-    return onehot.astype(jnp.float32), tok_slot, slot_tok
-
-
-def gather_rows(source, row_index):
-    return jnp.take(source, row_index, axis=0, mode='fill', fill_value=0)
-
-
-def router_grad(router_prob, onehot, gate_val, d_gate, log_norm, aux_vec, z_coef):
-    spread = jnp.sum(router_prob * aux_vec, axis=-1, keepdims=True)
-    return ((gate_val * d_gate)[..., None] * (onehot - router_prob)
-            + router_prob * (aux_vec - spread)
-            + (z_coef * log_norm)[..., None] * router_prob)
+TOKEN_BLOCK = 256
+UNROLL = 16
+
+
+def route_slots(onehot, idx_group, capacity):
+    tokens, num_experts = onehot.shape
+    blocks = tokens // TOKEN_BLOCK
+    chosen = onehot.reshape(blocks, TOKEN_BLOCK, num_experts)
+    lower = jnp.tril(jnp.ones((TOKEN_BLOCK, TOKEN_BLOCK), jnp.bfloat16))
+    within = jnp.einsum('ij,bje->bie', lower, chosen.astype(jnp.bfloat16), preferred_element_type=jnp.float32)
+    totals = within[:, -1, :]
+    before = (jnp.arange(blocks)[:, None] > jnp.arange(blocks)[None, :]).astype(jnp.float32)
+    base = jnp.sum(before[:, :, None] * totals[None, :, :], axis=1)
+    position = jnp.sum((within + base[:, None, :]) * chosen, axis=-1).reshape(tokens).astype(jnp.int32) - 1
+    return jnp.where(position < capacity, idx_group * capacity + position, num_experts * capacity), base[-1] + totals[-1]
+
+
+def dispatch_kernel(blocks, capacity, slot_ref, x_ref, dy_ref, gate_ref, xd_ref, gates_ref, table, stage):
+    step = pl.program_id(0)
+    d_model = x_ref.shape[1]
+    cols = d_model // 128
+    lanes = gates_ref.shape[2]
+    n_local = xd_ref.shape[1]
+
+    @pl.when(step == 0)
+    def _():
+        def clear(i, carry):
+            table[pl.ds(pl.multiple_of(i * 512, 512), 512), :] = jnp.zeros((512, 128), jnp.float32)
+            return carry
+        lax.fori_loop(0, table.shape[0] // 512, clear, 0)
+
+    @pl.when(step < blocks)
+    def _():
+        for c in range(cols):
+            stage[pl.ds(c, TOKEN_BLOCK, stride=8), :] = x_ref[:, c * 128:(c + 1) * 128].astype(jnp.float32)
+            stage[pl.ds(cols + c, TOKEN_BLOCK, stride=8), :] = dy_ref[:, c * 128:(c + 1) * 128].astype(jnp.float32)
+        stage[pl.ds(2 * cols, TOKEN_BLOCK, stride=8), :] = gate_ref[...]
+
+        def place(i, carry):
+            for u in range(UNROLL):
+                t = i * UNROLL + u
+                slot = slot_ref[step * TOKEN_BLOCK + t]
+                table[pl.ds(pl.multiple_of(slot * 8, 8), 8), :] = stage[pl.ds(pl.multiple_of(t * 8, 8), 8), :]
+            return carry
+        lax.fori_loop(0, TOKEN_BLOCK // UNROLL, place, 0)
+
+    @pl.when(step >= blocks)
+    def _():
+        dst = step - blocks
+        gates_ref[...] = jnp.zeros_like(gates_ref)
+        for e in range(n_local):
+            first = (dst * n_local + e) * (capacity * 8)
+            for c in range(cols):
+                xd_ref[0, e, 0, :, c * 128:(c + 1) * 128] = table[pl.ds(first + c, capacity, stride=8), :].astype(jnp.bfloat16)
+                xd_ref[0, e, 1, :, c * 128:(c + 1) * 128] = table[pl.ds(first + cols + c, capacity, stride=8), :].astype(jnp.bfloat16)
+            gate = table[pl.ds(first + 2 * cols, capacity, stride=8), :]
+            row = lax.broadcasted_iota(jnp.int32, (capacity, 128), 0)
+            lane = lax.broadcasted_iota(jnp.int32, (capacity, 128), 1)
+            for c in range(lanes // 128):
+                gates_ref[0, e:e + 1, c * 128:(c + 1) * 128] = jnp.sum(
+                    jnp.where(row == lane + c * 128, gate, 0.0), axis=0, keepdims=True)
+
+
+def dispatch(tok_slot, x_tokens, grad_y, gate_rows, n_dev, n_local, capacity, lanes):
+    tokens, d_model = x_tokens.shape
+    blocks = tokens // TOKEN_BLOCK
+    n_slots = n_dev * n_local * capacity
+    table_rows = -(-(n_slots + 1) * 8 // 512) * 512
+    tok = lambda i: (jnp.minimum(i, blocks - 1), 0)
+    dst = lambda i: jnp.maximum(i - blocks, 0)
+    return pl.pallas_call(
+        functools.partial(dispatch_kernel, blocks, capacity),
+        grid=(blocks + n_dev,),
+        out_shape=(jax.ShapeDtypeStruct((n_dev, n_local, 2, capacity, d_model), jnp.bfloat16),
+                   jax.ShapeDtypeStruct((n_dev, 8, lanes), jnp.float32)),
+        in_specs=[pl.BlockSpec(memory_space=pltpu.SMEM),
+                  pl.BlockSpec((TOKEN_BLOCK, d_model), tok),
+                  pl.BlockSpec((TOKEN_BLOCK, d_model), tok),
+                  pl.BlockSpec((TOKEN_BLOCK, 128), tok)],
+        out_specs=(pl.BlockSpec((1, n_local, 2, capacity, d_model), lambda i: (dst(i), 0, 0, 0, 0)),
+                   pl.BlockSpec((1, 8, lanes), lambda i: (dst(i), 0, 0))),
+        scratch_shapes=[pltpu.VMEM((table_rows, 128), jnp.float32),
+                        pltpu.VMEM((TOKEN_BLOCK * 8, 128), jnp.float32)],
+        compiler_params=pltpu.CompilerParams(dimension_semantics=('arbitrary',), vmem_limit_bytes=60 * 1024 * 1024),
+        name='dispatch',
+    )(tok_slot, x_tokens, grad_y, gate_rows)
+
+
+def split3(v):
+    hi = v.astype(jnp.bfloat16)
+    rest = v - hi.astype(jnp.float32)
+    mid = rest.astype(jnp.bfloat16)
+    low = (rest - mid.astype(jnp.float32)).astype(jnp.bfloat16)
+    return hi, mid, low
+
+
+def combine_kernel(sources, capacity, slot_ref, back_ref, g_ref, x_ref, ohg_ref, p_ref, zp_ref, aux_ref, wr_t_ref, gwi_ref, gwo_t_ref,
+                   gx_ref, gwr_ref, gwi_out_ref, gwo_out_ref, table, stage):
+    step = pl.program_id(0)
+    d_model = x_ref.shape[1]
+    cols = d_model // 128
+    n_local = back_ref.shape[1]
+    num_experts = p_ref.shape[1]
+    n_slots = sources * n_local * capacity
+    gwi_out_ref[...] = gwi_ref[...]
+    gwo_out_ref[0] = gwo_t_ref[0].T
+
+    @pl.when(step == 0)
+    def _():
+        table[pl.ds(n_slots * 8, 8), :] = jnp.zeros((8, 128), jnp.float32)
+        gwr_ref[...] = jnp.zeros_like(gwr_ref)
+
+    @pl.when(step < sources)
+    def _():
+        lanes = g_ref.shape[2]
+        eye = (lax.broadcasted_iota(jnp.int32, (capacity, lanes), 0)
+               == lax.broadcasted_iota(jnp.int32, (capacity, lanes), 1))
+        for e in range(n_local):
+            first = (step * n_local + e) * (capacity * 8)
+            for c in range(cols):
+                table[pl.ds(first + c, capacity, stride=8), :] = back_ref[0, e, :, c * 128:(c + 1) * 128].astype(jnp.float32)
+            g_col = jnp.sum(jnp.where(eye, g_ref[0, e:e + 1, :], 0.0), axis=1, keepdims=True)
+            table[pl.ds(first + cols, capacity, stride=8), :] = jnp.broadcast_to(g_col, (capacity, 128))
+
+    @pl.when(step >= sources)
+    def _():
+        block = step - sources
+
+        def pick(i, carry):
+            for u in range(UNROLL):
+                t = i * UNROLL + u
+                slot = slot_ref[block * TOKEN_BLOCK + t]
+                stage[pl.ds(pl.multiple_of(t * 8, 8), 8), :] = table[pl.ds(pl.multiple_of(slot * 8, 8), 8), :]
+            return carry
+        lax.fori_loop(0, TOKEN_BLOCK // UNROLL, pick, 0)
+        g_tok = stage[pl.ds(cols, TOKEN_BLOCK, stride=8), :][:, :num_experts]
+        prob = p_ref[...]
+        aux_vec = aux_ref[0:1, :]
+        spread = jnp.sum(prob * aux_vec, axis=1, keepdims=True)
+        d_logits = g_tok * ohg_ref[...] + prob * (aux_vec - spread) + zp_ref[...]
+        hi, mid, low = split3(d_logits)
+        left = jnp.concatenate([hi, mid, hi, low, mid, hi], axis=1)
+        dx_router = jnp.dot(left, wr_t_ref[...], preferred_element_type=jnp.float32)
+        for c in range(cols):
+            part = slice(c * 128, (c + 1) * 128)
+            gx_ref[:, part] = (stage[pl.ds(c, TOKEN_BLOCK, stride=8), :] + dx_router[:, part]).astype(jnp.bfloat16)
+        parts = jnp.concatenate([hi, mid, low, jnp.zeros_like(hi)], axis=1)
+        gwr_ref[...] += lax.dot_general(parts, x_ref[...], (((0,), (0,)), ((), ())), preferred_element_type=jnp.float32)
+
+
+def combine(tok_slot, back, g_back, x_tokens, ohg, prob, zp, aux_vec, w_router, gw_in, gw_out_t):
+    n_dev, n_local, capacity, d_model = back.shape
+    tokens = x_tokens.shape[0]
+    num_experts = prob.shape[1]
+    d_ff = gw_in.shape[2]
+    blocks = tokens // TOKEN_BLOCK
+    steps = n_dev + blocks
+    lanes = g_back.shape[2]
+    n_slots = n_dev * n_local * capacity
+    round_bf16 = lambda v: lax.reduce_precision(v, 8, 7)
+    w_hi = round_bf16(w_router.T)
+    w_mid = round_bf16(w_router.T - w_hi)
+    w_low = w_router.T - w_hi - w_mid
+    wr_t = jnp.concatenate([w_hi, w_hi, w_mid, w_hi, w_mid, w_low], axis=0).astype(jnp.bfloat16)
+    gw_in_rows = gw_in.reshape(n_local * d_model, d_ff)
+    in_rows = n_local * d_model // steps
+    out_cols = d_ff // 128
+    src = lambda i: jnp.minimum(i, n_dev - 1)
+    tok = lambda i: (jnp.maximum(i - n_dev, 0), 0)
+    flip = lambda i: jnp.minimum(i, n_local * out_cols - 1)
+    gx, gwr, gw_in_out, gw_out = pl.pallas_call(
+        functools.partial(combine_kernel, n_dev, capacity),
+        grid=(steps,),
+        out_shape=(jax.ShapeDtypeStruct((tokens, d_model), jnp.bfloat16),
+                   jax.ShapeDtypeStruct((4 * num_experts, d_model), jnp.float32),
+                   jax.ShapeDtypeStruct((n_local * d_model, d_ff), jnp.float32),
+                   jax.ShapeDtypeStruct((n_local, d_ff, d_model), jnp.float32)),
+        in_specs=[pl.BlockSpec(memory_space=pltpu.SMEM),
+                  pl.BlockSpec((1, n_local, capacity, d_model), lambda i: (src(i), 0, 0, 0)),
+                  pl.BlockSpec((1, 8, lanes), lambda i: (src(i), 0, 0)),
+                  pl.BlockSpec((TOKEN_BLOCK, d_model), tok),
+                  pl.BlockSpec((TOKEN_BLOCK, num_experts), tok),
+                  pl.BlockSpec((TOKEN_BLOCK, num_experts), tok),
+                  pl.BlockSpec((TOKEN_BLOCK, num_experts), tok),
+                  pl.BlockSpec((8, num_experts), lambda i: (0, 0)),
+                  pl.BlockSpec((6 * num_experts, d_model), lambda i: (0, 0)),
+                  pl.BlockSpec((in_rows, d_ff), lambda i: (i, 0)),
+                  pl.BlockSpec((1, d_model, 128), lambda i: (flip(i) // out_cols, 0, flip(i) % out_cols))],
+        out_specs=(pl.BlockSpec((TOKEN_BLOCK, d_model), tok),
+                   pl.BlockSpec((4 * num_experts, d_model), lambda i: (0, 0)),
+                   pl.BlockSpec((in_rows, d_ff), lambda i: (i, 0)),
+                   pl.BlockSpec((1, 128, d_model), lambda i: (flip(i) // out_cols, flip(i) % out_cols, 0))),
+        scratch_shapes=[pltpu.VMEM(((n_slots + 1) * 8, 128), jnp.float32),
+                        pltpu.VMEM((TOKEN_BLOCK * 8, 128), jnp.float32)],
+        compiler_params=pltpu.CompilerParams(dimension_semantics=('arbitrary',), vmem_limit_bytes=60 * 1024 * 1024),
+        name='combine',
+    )(tok_slot, back, g_back, x_tokens, ohg, prob, zp, jnp.broadcast_to(aux_vec, (8, num_experts)), wr_t, gw_in_rows, gw_out_t)
+    part = gwr.reshape(4, num_experts, d_model)
+    return gx, (part[0] + part[1] + part[2]).T, gw_in_out.reshape(n_local, d_model, d_ff), gw_out
+
+
+def flip_bits(me, k, n):
+    out = 0
+    bit = 1
+    while bit < n:
+        mine = (me // bit) % 2
+        flip = (k // bit) % 2
+        out = out + bit * (mine + flip - 2 * mine * flip)
+        bit *= 2
+    return out
+
+
+def total_kernel(n, part_ref, out_ref, inbox, mine, a_send, a_recv, b_send, b_recv):
+    me = lax.axis_index('ep')
+
+    def scatter(k):
+        peer = flip_bits(me, k, n)
+        return pltpu.make_async_remote_copy(src_ref=part_ref.at[peer], dst_ref=inbox.at[me], send_sem=a_send.at[k],
+                                            recv_sem=a_recv.at[k], device_id=(peer,), device_id_type=MESH)
+
+    def spread(k):
+        peer = flip_bits(me, k, n)
+        return pltpu.make_async_remote_copy(src_ref=mine, dst_ref=out_ref.at[me], send_sem=b_send.at[k],
+                                            recv_sem=b_recv.at[k], device_id=(peer,), device_id_type=MESH)
+
+    for k in range(1, n):
+        scatter(k).start()
+    inbox[me] = part_ref[me]
+    for k in range(1, n):
+        scatter(k).wait_recv()
+    total = inbox[0]
+    for i in range(1, n):
+        total = total + inbox[i]
+    mine[...] = total
+    out_ref[me] = total
+    for k in range(1, n):
+        spread(k).start()
+    for k in range(1, n):
+        scatter(k).wait_send()
+        spread(k).wait()
+
+
+def total(part, n_dev):
+    rows, cols = part.shape
+    piece = rows * cols // (n_dev * 128)
+    chunks = jnp.pad(part.reshape(n_dev, piece, 128), ((0, 0), (0, -piece % 8), (0, 0)))
+    dma = pltpu.SemaphoreType.DMA
+    vmem_spec = pl.BlockSpec(memory_space=pltpu.VMEM)
+    out = pl.pallas_call(
+        functools.partial(total_kernel, n_dev),
+        out_shape=jax.ShapeDtypeStruct(chunks.shape, jnp.float32),
+        in_specs=[vmem_spec],
+        out_specs=vmem_spec,
+        scratch_shapes=[pltpu.VMEM(chunks.shape, jnp.float32), pltpu.VMEM(chunks.shape[1:], jnp.float32),
+                        dma((n_dev,)), dma((n_dev,)), dma((n_dev,)), dma((n_dev,))],
+        compiler_params=pltpu.CompilerParams(has_side_effects=True),
+        name='total',
+    )(chunks)
+    return out[:, :piece].reshape(rows, cols)
 
 
 def nt_dot(a, b):
     return lax.dot_general(a, b, (((1,), (1,)), ((), ())), preferred_element_type=jnp.float32)
 
 
-def exchange_kernel(n, n_local, xd_ref, gate_ref, w_in_ref, w_out_ref,
-                    gw_in_ref, gw_out_t_ref, back_ref, g_back_ref,
-                    xr, gate_r, g_s,
+def exchange_kernel(n, n_local, xd_ref, gate_ref, stat_ref, w_in_ref, w_out_ref,
+                    gw_in_ref, gw_out_t_ref, back_ref, g_back_ref, stat_out_ref,
+                    xr, gate_r, g_s, stat_r,
                     fwd_send, fwd_recv, gate_send, gate_recv,
-                    ret_send, ret_recv, g_send, g_recv, loc_sem):
+                    ret_send, ret_recv, g_send, g_recv, stat_send, stat_recv, loc_sem):
     me = lax.axis_index('ep')
     cap, d_model = xr.shape[3], xr.shape[4]
     d_ff = w_in_ref.shape[2]
 
     def peer_of(k):
-        out = 0
-        bit = 1
-        while bit < n:
-            mine = (me // bit) % 2
-            flip = (k // bit) % 2
-            out = out + bit * (mine + flip - 2 * mine * flip)
-            bit *= 2
-        return out
+        return flip_bits(me, k, n)
 
     half = n // 2
 
@@ -86,6 +317,12 @@
             send_sem=g_send.at[k], recv_sem=g_recv.at[k],
             device_id=(peer,), device_id_type=MESH)
 
+    def stat_copy(k, peer):
+        return pltpu.make_async_remote_copy(
+            src_ref=stat_ref, dst_ref=stat_r.at[me],
+            send_sem=stat_send.at[k], recv_sem=stat_recv.at[k],
+            device_id=(peer,), device_id_type=MESH)
+
     own_in = [pltpu.make_async_copy(xd_ref.at[me, e], xr.at[0, e], loc_sem.at[e]) for e in range(n_local)]
     own_gate = pltpu.make_async_copy(gate_ref.at[me], gate_r.at[0], loc_sem.at[n_local])
     for c in own_in:
@@ -96,6 +333,7 @@
         k = rel_of(j)
         peer = peer_of(k)
         gate_copy(k, peer).start()
+        stat_copy(k, peer).start()
         for e in range(n_local):
             fwd_copy(k, e, peer).start()
         return carry
@@ -105,6 +343,7 @@
     gw_in_ref[...] = jnp.zeros_like(gw_in_ref)
     gw_out_t_ref[...] = jnp.zeros_like(gw_out_t_ref)
     g_s[...] = jnp.zeros_like(g_s)
+    stat_r[me] = stat_ref[...]
     for c in own_in:
         c.wait()
     own_gate.wait()
@@ -179,6 +418,7 @@
         k = rel_of(j)
         peer = peer_of(k)
         gate_copy(k, peer).wait_send()
+        stat_copy(k, peer).wait()
         g_copy(k, peer).wait()
         for e in range(n_local):
             fwd_copy(k, e, peer).wait_send()
@@ -186,9 +426,13 @@
         return carry
 
     lax.fori_loop(1, n, drain, 0)
-
-
-def exchange(xd, gates, w_in, w_out, n_dev):
+    stat = stat_r[0]
+    for i in range(1, n):
+        stat = stat + stat_r[i]
+    stat_out_ref[...] = stat
+
+
+def exchange(xd, gates, stats, w_in, w_out, n_dev):
     n_local, d_model, d_ff = w_in.shape
     cap = xd.shape[3]
     lanes = gates.shape[2]
@@ -201,20 +445,22 @@
         out_shape=(jax.ShapeDtypeStruct((n_local, d_model, d_ff), jnp.float32),
                    jax.ShapeDtypeStruct((n_local, d_model, d_ff), jnp.float32),
                    jax.ShapeDtypeStruct((n_dev, n_local, cap, d_model), jnp.bfloat16),
-                   jax.ShapeDtypeStruct((n_dev, 8, lanes), jnp.float32)),
-        in_specs=[any_spec, any_spec, vmem_spec, vmem_spec],
-        out_specs=(vmem_spec, vmem_spec, any_spec, any_spec),
+                   jax.ShapeDtypeStruct((n_dev, 8, lanes), jnp.float32),
+                   jax.ShapeDtypeStruct(stats.shape, jnp.float32)),
+        in_specs=[any_spec, any_spec, vmem_spec, vmem_spec, vmem_spec],
+        out_specs=(vmem_spec, vmem_spec, any_spec, any_spec, vmem_spec),
         scratch_shapes=[
             pltpu.VMEM((n_dev, n_local, 2, cap, d_model), jnp.bfloat16),
             pltpu.VMEM((n_dev, 8, lanes), jnp.float32),
             pltpu.VMEM((n_dev, 8, lanes), jnp.float32),
+            pltpu.VMEM((n_dev,) + stats.shape, jnp.float32),
             dma((pairs,)), dma((pairs,)), dma((n_dev,)), dma((n_dev,)),
             dma((pairs,)), dma((pairs,)), dma((n_dev,)), dma((n_dev,)),
-            dma((n_local + 1,)),
+            dma((n_dev,)), dma((n_dev,)), dma((n_local + 1,)),
         ],
         compiler_params=pltpu.CompilerParams(has_side_effects=True, vmem_limit_bytes=60 * 1024 * 1024),
         name='exchange',
-    )(xd, gates, w_in, w_out)
+    )(xd, gates, stats, w_in, w_out)
 
 
 def solution(mesh):
@@ -227,33 +473,26 @@
         capacity = (5 * tokens + 4 * num_experts - 1) // (4 * num_experts)
         total_tok = tokens * n_dev
         lanes = -(-capacity // 128) * 128
-        onehot, tok_slot, slot_tok = route_slots(expert_idx, num_experts, capacity)
+        onehot = (expert_idx[:, None] == jnp.arange(num_experts, dtype=jnp.int32)[None, :]).astype(jnp.float32)
+        tok_slot, load = route_slots(onehot, expert_idx, capacity)
         logits = jnp.dot(x_tokens, w_router, preferred_element_type=jnp.float32)
         router_prob = jax.nn.softmax(logits, axis=-1)
-        log_norm = jax.nn.logsumexp(logits, axis=-1)
-        gate_val = jnp.sum(router_prob * onehot, axis=-1)
-        route_stats = jnp.concatenate([jnp.sum(onehot, axis=0), jnp.sum(router_prob, axis=0), jnp.sum(log_norm * log_norm)[None]])
-        route_stats = lax.psum(route_stats, 'ep')
-
-        slot_shape = (n_dev, n_local, 1, capacity, d_model)
-        xd = jnp.concatenate([gather_rows(x_tokens, slot_tok).reshape(slot_shape),
-                              gather_rows(grad_y, slot_tok).reshape(slot_shape)], axis=2)
-        gate_slot = gather_rows(gate_val, slot_tok).reshape(n_dev, n_local, capacity)
-        gates = jnp.pad(gate_slot, ((0, 0), (0, 8 - n_local), (0, lanes - capacity)))
-        grad_w_in, grad_w_out_t, back, g_back = exchange(xd, gates, w_in, w_out, n_dev)
-        grad_w_out = jnp.swapaxes(grad_w_out_t, 1, 2)
-        d_gate = gather_rows(g_back[:, :n_local, :capacity].reshape(num_experts * capacity), tok_slot)
-        dx_expert = gather_rows(back.reshape(num_experts * capacity, d_model), tok_slot)
-
-        load_frac = route_stats[:num_experts] / total_tok
-        mean_prob = route_stats[num_experts:2 * num_experts] / total_tok
+        log_norm = jax.nn.logsumexp(logits, axis=-1, keepdims=True)
+        gate_val = jnp.sum(router_prob * onehot, axis=-1, keepdims=True)
+        stats = jnp.concatenate([load, jnp.sum(router_prob, axis=0), jnp.sum(log_norm * log_norm)[None]])
+        stats = jnp.pad(stats[None], ((0, 7), (0, 128 - stats.shape[0])))
+        xd, gates = dispatch(tok_slot, x_tokens, grad_y, jnp.broadcast_to(gate_val, (tokens, 128)), n_dev, n_local, capacity, lanes)
+        gw_in, gw_out_t, back, g_back, stats = exchange(xd, gates, stats, w_in, w_out, n_dev)
+
+        load_frac = stats[0, :num_experts] / total_tok
+        mean_prob = stats[0, num_experts:2 * num_experts] / total_tok
         aux_loss = AUX_WEIGHT * num_experts * jnp.sum(load_frac * mean_prob)
-        z_loss = Z_WEIGHT * route_stats[2 * num_experts] / total_tok
+        z_loss = Z_WEIGHT * stats[0, 2 * num_experts] / total_tok
         aux_vec = AUX_WEIGHT * num_experts * load_frac / total_tok
-        d_logits = router_grad(router_prob, onehot, gate_val, d_gate, log_norm, aux_vec, 2.0 * Z_WEIGHT / total_tok)
-        dx_router = jnp.einsum('se,de->sd', d_logits, w_router)
-        grad_x = (dx_expert.astype(jnp.float32) + dx_router).astype(jnp.bfloat16)
-        grad_w_router = lax.psum(jnp.einsum('sd,se->de', x_tokens, d_logits, preferred_element_type=jnp.float32), 'ep')
+        ohg = gate_val * (onehot - router_prob)
+        zp = (2.0 * Z_WEIGHT / total_tok * log_norm) * router_prob
+        grad_x, part, grad_w_in, grad_w_out = combine(tok_slot, back, g_back, x_tokens, ohg, router_prob, zp, aux_vec, w_router, gw_in, gw_out_t)
+        grad_w_router = total(part, n_dev)
         return grad_x, grad_w_in, grad_w_out, grad_w_router, aux_loss, z_loss
 
     return jax.shard_map(expert_layer, mesh=mesh,

time: 714 us -> 492 us (0.69)
  local copies, waits for them, and re-layouts: 272 us -> 11.7 us
  Pallas kernels: 326 us -> 440 us
  blocking collectives: 68.9 us -> 0 us
  matrix products: 13.6 us -> 5.15 us
    gather x5 -> x0, local copies, waits for them, and re-layouts: 227 us -> none  [gather_rows(): return jnp.take(source, row_index, axis=0, mode='fill', fill_value=0)]
    pallas_call x0 -> x3, Pallas kernels: none -> 112 us  [the longest x1 53.2 us: combine(): pl.pallas_call(functools.partial(combine_kernel, n_dev, capacity), grid=(...]
    psum x2 -> x0, blocking collectives: 68.9 us -> none  [the longest x1 34.6 us: expert_layer(): route_stats = lax.psum(route_stats, 'ep')]
    scatter x1 -> x0, local copies, waits for them, and re-layouts: 30.5 us -> none  [route_slots(): jnp.full((n_slots,), tokens, jnp.int32).at[tok_slot]]
    unnamed x10, local copies, waits for them, and re-layouts: 10.9 us -> 0.76 us
    another operation x3 -> x0, other arithmetic: 10.1 us -> none
    mul x2, other arithmetic: 0.63 us -> 10.5 us  [the longest x1 5.6 us: expert_layer(): zp = 2.0 * Z_WEIGHT / total_tok * log_norm * router_prob]
    dot_general x2 -> x1, matrix products: 8.79 us -> 0.33 us  [route_slots(): jnp.einsum('ij,bje->bie', lower, chosen.astype(jnp.bfloat16), preferred_e...]
where the time goes in v2:
time: 492 us; the launch traced here: 490 us
  Pallas kernels  440 us (89%)
  other arithmetic  28 us (6%)
  local copies, waits for them, and re-layouts  11.7 us (2%)
  matrix products  5.15 us (1%)
    pallas_call x1, Pallas kernels, exchange(): pl.pallas_call(functools.partial(exchange_kernel, n_dev, n_local), out_sh...  329 us
    pallas_call x1, Pallas kernels, combine(): pl.pallas_call(functools.partial(combine_kernel, n_dev, capacity), grid=(...  53.2 us
    pallas_call x1, Pallas kernels, dispatch(): pl.pallas_call(functools.partial(dispatch_kernel, blocks, capacity), grid...  44.5 us
    pallas_call x1, Pallas kernels, total(): pl.pallas_call(functools.partial(total_kernel, n_dev), out_shape=jax.Shap...  13.9 us

profile of v2, /device:TPU:0, one launch (start us, length us, event | category | flops | bytes accessed | tf_op | source)
XLA Modules:
  0.0 489.6 jit_solution(247174552769244428)
XLA Ops:
  0.6 0.8 eq.22
  1.4 0.8 constant_dynamic-update-slice_fusion.4
  2.2 0.8 constant_dynamic-update-slice_fusion.3
  3.0 0.8 constant_dynamic-update-slice_fusion.2
  3.8 0.8 constant_dynamic-update-slice_fusion.1
  4.7 0.8 constant_dynamic-update-slice_fusion
  5.5 0.8 fusion.9.wr_t_ref
  7.8 1.4 add_select_fusion.slot_ref
  9.2 4.8 fusion.16
  14.9 2.7 copy.18
  17.6 4.2 fusion.1
  21.9 5.6 %broadcast_multiply_fusion = (f32[8192,32]{1,0:T(8,128)}, f32[8192,32]{1,0:T(8,128)S(1)}) fusion(f32[8192]{0:T(1024)S(1)} %get-tuple-element.51, f32[8192]{0:T(1024)S(1)} %fusion.1, f32[8192,32]{1,0:T(8,128)S(1)} %copy-done.1, f32[8192]{0:T(1024)S(1)} %get-tuple-element.54), kind=kLoop, calls=%fused_computation.6 | loop fusion | flops 786432 | bytes 3244032 | tf_op jit(solution)/shard_map/mul | solution.py:493
  27.5 2.6 fusion.14
  31.3 4.9 %subtract_multiply_fusion.ohg_ref = f32[8192,32]{1,0:T(8,128)} fusion(f32[8192,32]{1,0:T(8,128)S(1)} %get-tuple-element.49.p_ref, f32[8192]{0:T(1024)S(1)} %get-tuple-element.47, s32[8192]{0:T(1024)S(1)} %copy-done.2), kind=kLoop, calls=%fused_computation | loop fusion | flops 1048576 | bytes 2162688 | tf_op jit(solution)/shard_map/mul | solution.py:492
  36.3 2.6 broadcast_in_dim.42.gate_ref
  38.9 44.5 %dispatch.1 = (bf16[16,2,2,320,384]{4,3,2,1,0:T(8,128)(2,1)}, f32[16,8,384]{2,1,0:T(8,128)}) custom-call(s32[8192]{0:T(1024)} %add_select_fusion.slot_ref, bf16[8192,384]{1,0:T(8,128)(2,1)} %x_ref.3, bf16[8192,384]{1,0:T(8,128)(2,1)} %dy_ref.1, f32[8192,128]{1,0:T(8,128)} %broadcast_in_dim.42.gate_ref), custom_call_target="tpu_custom_call" | custom-call | tf_op jit(solution)/shard_map/dispatch/pallas_call | solution.py:84
  83.4 328.9 %exchange.1 = (f32[2,384,1536]{2,1,0:T(8,128)}, f32[2,384,1536]{2,1,0:T(8,128)}, bf16[16,2,320,384]{3,2,1,0:T(8,128)(2,1)}, f32[16,8,384]{2,1,0:T(8,128)}, f32[8,128]{1,0:T(8,128)}) custom-call(bf16[16,2,2,320,384]{4,3,2,1,0:T(8,128)(2,1)} %get-tuple-element.17.xd_ref, f32[16,8,384]{2,1,0:T(8,128)} %get-tuple-element.18.gate_ref, f32[8,128]{1,0:T(8,128)} %pad.8.stat_ref, ...), custom_call_target="tpu_custom_call" | custom-call | tf_op jit(solution)/shard_map/exchange/pallas_call | solution.py:443
  412.3 1.3 slice.44
  414.2 1.4 multiply_reduce_fusion.2
  416.8 53.2 %combine.1 = (bf16[8192,384]{1,0:T(8,128)(2,1)}, f32[128,384]{1,0:T(8,128)}, f32[768,1536]{1,0:T(8,128)}, f32[2,1536,384]{2,1,0:T(8,128)}) custom-call(s32[8192]{0:T(1024)} %add_select_fusion.slot_ref, bf16[16,2,320,384]{3,2,1,0:T(8,128)(2,1)} %get-tuple-element.19.back_ref, f32[16,8,384]{2,1,0:T(8,128)} %get-tuple-element.20.g_ref, ...), custom_call_target="tpu_custom_call" | custom-call | tf_op jit(solution)/shard_map/combine/pallas_call | solution.py:184
  470.0 0.9 add_bitcast_fusion
  471.7 13.9 %total.1 = f32[16,8,128]{2,1,0:T(8,128)} custom-call(f32[16,8,128]{2,1,0:T(8,128)} %pad.9.part_ref), custom_call_target="tpu_custom_call" | custom-call | tf_op jit(solution)/shard_map/total/pallas_call | solution.py:262
  485.6 0.9 reshape.98
  486.6 0.7 copy.20
  (26 shorter events, 5.1 us)
Async XLA Ops:
  6.3 7.8 %copy-start.3 = (bf16[192,384]{1,0:T(8,128)(2,1)}, bf16[192,384]{1,0:T(8,128)(2,1)S(1)}, u32[]{:S(2)}) copy-start(bf16[192,384]{1,0:T(8,128)(2,1)S(1)} %fusion.9.wr_t_ref) | copy-start | bytes 442372
  17.6 4.2 copy-start.1
  21.8 5.6 %copy-start.2 = (s32[8192]{0:T(1024)S(1)}, s32[8192]{0:T(1024)}, u32[]{:S(2)}) copy-start(s32[8192]{0:T(1024)} %param.8) | copy-start | bytes 98308
  27.5 8.8 %copy-start = (f32[8192,32]{1,0:T(8,128)}, f32[8192,32]{1,0:T(8,128)S(1)}, u32[]{:S(2)}) copy-start(f32[8192,32]{1,0:T(8,128)S(1)} %get-tuple-element.49.p_ref) | copy-start | bytes 3145732

commit v3 on v2

--- a/solution.py
+++ b/solution.py
@@ -276,6 +276,25 @@
     return lax.dot_general(a, b, (((1,), (1,)), ((), ())), preferred_element_type=jnp.float32)
 
 
+def tile_at(t):
+    quarter = t // 4
+    edge = (7 - quarter) // 7 + quarter // 7
+    turn = (t + 4) % 8
+    piece = (1 - edge) * (turn // 2) + edge * (t % 4)
+    stage = (t + 4) // 8
+    chip = stage * (7 - stage) // 2 + stage // 4
+    chip = chip + (1 - edge) * (turn % 2) * (7 - 2 * chip)
+    return chip * 2 + piece // 2, piece % 2
+
+
+def link_sets(n, n_local):
+    assert n == 16
+    pieces = []
+    for chips in ((3, 4), (5, 2), (6, 1), (7,)):
+        pieces.append([[(chip * 2 + c, e) for c in range(2) for e in range(n_local)] for chip in chips])
+    return pieces
+
+
 def exchange_kernel(n, n_local, xd_ref, gate_ref, stat_ref, w_in_ref, w_out_ref,
                     gw_in_ref, gw_out_t_ref, back_ref, g_back_ref, stat_out_ref,
                     xr, gate_r, g_s, stat_r,
@@ -288,58 +307,82 @@
     def peer_of(k):
         return flip_bits(me, k, n)
 
-    half = n // 2
-
-    def rel_of(j):
-        return (j % half) * 2 + j // half
-
-    def fwd_copy(k, e, peer):
+    def fwd_copy(k, e, part):
+        sem = (k * n_local + e) * 2 + part
+        peer = peer_of(k)
         return pltpu.make_async_remote_copy(
-            src_ref=xd_ref.at[peer, e], dst_ref=xr.at[k, e],
-            send_sem=fwd_send.at[k * n_local + e], recv_sem=fwd_recv.at[k * n_local + e],
+            src_ref=xd_ref.at[peer, e, part], dst_ref=xr.at[k, e, part],
+            send_sem=fwd_send.at[sem], recv_sem=fwd_recv.at[sem],
             device_id=(peer,), device_id_type=MESH)
 
-    def gate_copy(k, peer):
+    def gate_copy(k):
+        peer = peer_of(k)
         return pltpu.make_async_remote_copy(
             src_ref=gate_ref.at[peer], dst_ref=gate_r.at[k],
             send_sem=gate_send.at[k], recv_sem=gate_recv.at[k],
             device_id=(peer,), device_id_type=MESH)
 
-    def ret_copy(k, e, peer):
+    def stat_copy(k):
+        return pltpu.make_async_remote_copy(
+            src_ref=stat_ref, dst_ref=stat_r.at[me],
+            send_sem=stat_send.at[k], recv_sem=stat_recv.at[k],
+            device_id=(peer_of(k),), device_id_type=MESH)
+
+    def ret_copy(k, e):
+        sem = k * n_local + e
         return pltpu.make_async_remote_copy(
             src_ref=xr.at[k, e, 0], dst_ref=back_ref.at[me, e],
-            send_sem=ret_send.at[k * n_local + e], recv_sem=ret_recv.at[k * n_local + e],
-            device_id=(peer,), device_id_type=MESH)
-
-    def g_copy(k, peer):
+            send_sem=ret_send.at[sem], recv_sem=ret_recv.at[sem],
+            device_id=(peer_of(k),), device_id_type=MESH)
+
+    def g_copy(k):
         return pltpu.make_async_remote_copy(
             src_ref=g_s.at[k], dst_ref=g_back_ref.at[me],
             send_sem=g_send.at[k], recv_sem=g_recv.at[k],
-            device_id=(peer,), device_id_type=MESH)
-
-    def stat_copy(k, peer):
-        return pltpu.make_async_remote_copy(
-            src_ref=stat_ref, dst_ref=stat_r.at[me],
-            send_sem=stat_send.at[k], recv_sem=stat_recv.at[k],
-            device_id=(peer,), device_id_type=MESH)
-
+            device_id=(peer_of(k),), device_id_type=MESH)
+
+    sets = link_sets(n, n_local)
+
+    def interleave(queues):
+        return [queue[i] for i in range(len(queues[0])) for queue in queues]
+
+    def send_rows(queues):
+        for k, e in interleave(queues):
+            if e == 0:
+                gate_copy(k).start()
+                stat_copy(k).start()
+            for part in range(2):
+                fwd_copy(k, e, part).start()
+
+    def rows_left(queues):
+        for queue in queues:
+            for i, (k, e) in enumerate(queue):
+                fwd_copy(k, e, 0).wait_send()
+                if i < len(queue) - 1:
+                    fwd_copy(k, e, 1).wait_send()
+
+    def send_grads(queues):
+        for k, e in interleave(queues):
+            ret_copy(k, e).start()
+            if e == n_local - 1:
+                g_copy(k).start()
+
+    def grads_left(queues):
+        for queue in queues:
+            for k, e in queue[:-1]:
+                ret_copy(k, e).wait_send()
+
+    near = [[(1, e) for e in range(n_local)]]
     own_in = [pltpu.make_async_copy(xd_ref.at[me, e], xr.at[0, e], loc_sem.at[e]) for e in range(n_local)]
     own_gate = pltpu.make_async_copy(gate_ref.at[me], gate_r.at[0], loc_sem.at[n_local])
+    own_out = [pltpu.make_async_copy(xr.at[0, e, 0], back_ref.at[me, e], loc_sem.at[e]) for e in range(n_local)]
+    own_g = pltpu.make_async_copy(g_s.at[0], g_back_ref.at[me], loc_sem.at[n_local])
+
+    send_rows(sets[0])
+    send_rows(near)
     for c in own_in:
         c.start()
     own_gate.start()
-
-    def issue(j, carry):
-        k = rel_of(j)
-        peer = peer_of(k)
-        gate_copy(k, peer).start()
-        stat_copy(k, peer).start()
-        for e in range(n_local):
-            fwd_copy(k, e, peer).start()
-        return carry
-
-    lax.fori_loop(1, n, issue, 0)
-
     gw_in_ref[...] = jnp.zeros_like(gw_in_ref)
     gw_out_t_ref[...] = jnp.zeros_like(gw_out_t_ref)
     g_s[...] = jnp.zeros_like(g_s)
@@ -379,50 +422,84 @@
         g_s[k, pl.ds(e, 1), :] = jnp.sum(jnp.where(eye, g_col, 0.0), axis=0, keepdims=True)
         xr[k, e, 0] = d_rows.astype(jnp.bfloat16)
 
+    order = [(0, e) for e in range(n_local)] + near[0]
+    first = []
+    for queues in sets:
+        first.append(len(order))
+        order = order + interleave(queues)
+    assert order == [tile_at(t) for t in range(len(order))]
+
+    def own_back():
+        send_grads(near)
+        for c in own_out:
+            c.start()
+        own_g.start()
+
+    def after_rows(done, then):
+        def run():
+            rows_left(sets[done])
+            then()
+        return run
+
+    def after_grads(done, then):
+        def run():
+            grads_left(sets[done])
+            then()
+        return run
+
+    events = {
+        first[0]: own_back,
+        first[1] - 2: after_rows(0, lambda: send_rows(sets[1])),
+        first[2] - 2: after_rows(1, lambda: send_grads(sets[0])),
+        first[2]: after_grads(0, lambda: send_rows(sets[2])),
+        first[3] - 2: after_rows(2, lambda: send_grads(sets[1])),
+        first[3]: after_grads(1, lambda: send_rows(sets[3])),
+        len(order) - 1: after_rows(3, lambda: send_grads(sets[2])),
+    }
+
     def step(t, carry):
-        j = t // n_local
-        e = t % n_local
-        k = rel_of(j)
-        peer = peer_of(k)
-
-        @pl.when(j > 0)
+        k, e = tile_at(t)
+        for at, run in events.items():
+            pl.when(t == at)(run)
+
+        @pl.when(t >= n_local)
         def _():
             @pl.when(e == 0)
             def _():
-                gate_copy(k, peer).wait_recv()
-            fwd_copy(k, e, peer).wait_recv()
+                gate_copy(k).wait_recv()
+            for part in range(2):
+                fwd_copy(k, e, part).wait_recv()
 
         tile(k, e)
-
-        @pl.when(j > 0)
-        def _():
-            ret_copy(k, e, peer).start()
-
-            @pl.when(e == n_local - 1)
-            def _():
-                g_copy(k, peer).start()
         return carry
 
-    lax.fori_loop(0, n * n_local, step, 0)
-
-    own_out = [pltpu.make_async_copy(xr.at[0, e, 0], back_ref.at[me, e], loc_sem.at[e]) for e in range(n_local)]
-    own_g = pltpu.make_async_copy(g_s.at[0], g_back_ref.at[me], loc_sem.at[n_local])
-    for c in own_out:
-        c.start()
-    own_g.start()
+    lax.fori_loop(0, len(order), step, 0)
+    grads_left(sets[2])
+    send_grads(sets[3])
+
+    for queues in sets:
+        for queue in queues:
+            k, e = queue[-1]
+            fwd_copy(k, e, 1).wait_send()
+            if queues is not sets[3]:
+                ret_copy(k, e).wait_send()
+    grads_left(sets[3])
+    for queue in sets[3]:
+        ret_copy(*queue[-1]).wait_send()
+    for k, e in near[0]:
+        for part in range(2):
+            fwd_copy(k, e, part).wait_send()
+        ret_copy(k, e).wait_send()
     for c in own_out:
         c.wait()
     own_g.wait()
 
-    def drain(j, carry):
-        k = rel_of(j)
-        peer = peer_of(k)
-        gate_copy(k, peer).wait_send()
-        stat_copy(k, peer).wait()
-        g_copy(k, peer).wait()
+    def drain(k, carry):
+        gate_copy(k).wait_send()
+        stat_copy(k).wait()
+        g_copy(k).wait()
         for e in range(n_local):
-            fwd_copy(k, e, peer).wait_send()
-            ret_copy(k, e, peer).wait()
+            ret_copy(k, e).wait_recv()
         return carry
 
     lax.fori_loop(1, n, drain, 0)
@@ -454,7 +531,7 @@
             pltpu.VMEM((n_dev, 8, lanes), jnp.float32),
             pltpu.VMEM((n_dev, 8, lanes), jnp.float32),
             pltpu.VMEM((n_dev,) + stats.shape, jnp.float32),
-            dma((pairs,)), dma((pairs,)), dma((n_dev,)), dma((n_dev,)),
+            dma((2 * pairs,)), dma((2 * pairs,)), dma((n_dev,)), dma((n_dev,)),
             dma((pairs,)), dma((pairs,)), dma((n_dev,)), dma((n_dev,)),
             dma((n_dev,)), dma((n_dev,)), dma((n_local + 1,)),
         ],

time: 492 us -> 439 us (0.89)
  Pallas kernels: 440 us -> 387 us
    pallas_call x1, Pallas kernels: 329 us -> 278 us  [exchange(): pl.pallas_call(functools.partial(exchange_kernel, n_dev, n_local), out_sh...]
where the time goes in v3:
time: 439 us; the launch traced here: 437 us
  Pallas kernels  387 us (88%)
  other arithmetic  28 us (6%)
  local copies, waits for them, and re-layouts  11.7 us (3%)
  matrix products  5.15 us (1%)
    pallas_call x1, Pallas kernels, exchange(): pl.pallas_call(functools.partial(exchange_kernel, n_dev, n_local), out_sh...  278 us
    pallas_call x1, Pallas kernels, combine(): pl.pallas_call(functools.partial(combine_kernel, n_dev, capacity), grid=(...  53.2 us
    pallas_call x1, Pallas kernels, dispatch(): pl.pallas_call(functools.partial(dispatch_kernel, blocks, capacity), grid...  44.5 us
    pallas_call x1, Pallas kernels, total(): pl.pallas_call(functools.partial(total_kernel, n_dev), out_shape=jax.Shap...  12.2 us

profile of v3, /device:TPU:0, one launch (start us, length us, event | category | flops | bytes accessed | tf_op | source)
XLA Modules:
  0.0 436.6 jit_solution(6463884169630296802)
XLA Ops:
  0.6 0.8 eq.22
  1.4 0.8 constant_dynamic-update-slice_fusion.4
  2.2 0.8 constant_dynamic-update-slice_fusion.3
  3.0 0.8 constant_dynamic-update-slice_fusion.2
  3.8 0.8 constant_dynamic-update-slice_fusion.1
  4.7 0.8 constant_dynamic-update-slice_fusion
  5.5 0.8 fusion.9.wr_t_ref
  7.8 1.4 add_select_fusion.slot_ref
  9.2 4.8 %fusion.16 = (f32[8192]{0:T(1024)S(1)}, f32[8192,32]{0,1:T(8,128)S(1)}) fusion(bf16[8192,384]{1,0:T(8,128)(2,1)} %x_ref.3, f32[384,32]{0,1:T(8,128)} %param.7), kind=kOutput, calls=%fused_computation.49 | convolution fusion | flops 201580544 | bytes 7421952 | tf_op jit(solution)/shard_map/dot_general | solution.py:555
  14.9 2.7 copy.18
  17.6 4.2 fusion.1
  21.9 5.6 %broadcast_multiply_fusion = (f32[8192,32]{1,0:T(8,128)}, f32[8192,32]{1,0:T(8,128)S(1)}) fusion(f32[8192]{0:T(1024)S(1)} %get-tuple-element.51, f32[8192]{0:T(1024)S(1)} %fusion.1, f32[8192,32]{1,0:T(8,128)S(1)} %copy-done.1, f32[8192]{0:T(1024)S(1)} %get-tuple-element.54), kind=kLoop, calls=%fused_computation.6 | loop fusion | flops 786432 | bytes 3244032 | tf_op jit(solution)/shard_map/mul | solution.py:570
  27.5 2.6 fusion.14
  31.3 4.9 %subtract_multiply_fusion.ohg_ref = f32[8192,32]{1,0:T(8,128)} fusion(f32[8192,32]{1,0:T(8,128)S(1)} %get-tuple-element.49.p_ref, f32[8192]{0:T(1024)S(1)} %get-tuple-element.47, s32[8192]{0:T(1024)S(1)} %copy-done.2), kind=kLoop, calls=%fused_computation | loop fusion | flops 1048576 | bytes 2162688 | tf_op jit(solution)/shard_map/mul | solution.py:569
  36.3 2.6 broadcast_in_dim.42.gate_ref
  38.9 44.5 %dispatch.1 = (bf16[16,2,2,320,384]{4,3,2,1,0:T(8,128)(2,1)}, f32[16,8,384]{2,1,0:T(8,128)}) custom-call(s32[8192]{0:T(1024)} %add_select_fusion.slot_ref, bf16[8192,384]{1,0:T(8,128)(2,1)} %x_ref.3, bf16[8192,384]{1,0:T(8,128)(2,1)} %dy_ref.1, f32[8192,128]{1,0:T(8,128)} %broadcast_in_dim.42.gate_ref), custom_call_target="tpu_custom_call" | custom-call | tf_op jit(solution)/shard_map/dispatch/pallas_call | solution.py:84
  83.4 277.6 %exchange.1 = (f32[2,384,1536]{2,1,0:T(8,128)}, f32[2,384,1536]{2,1,0:T(8,128)}, bf16[16,2,320,384]{3,2,1,0:T(8,128)(2,1)}, f32[16,8,384]{2,1,0:T(8,128)}, f32[8,128]{1,0:T(8,128)}) custom-call(bf16[16,2,2,320,384]{4,3,2,1,0:T(8,128)(2,1)} %get-tuple-element.17.xd_ref, f32[16,8,384]{2,1,0:T(8,128)} %get-tuple-element.18.gate_ref, f32[8,128]{1,0:T(8,128)} %pad.8.stat_ref, ...), custom_call_target="tpu_custom_call" | custom-call | tf_op jit(solution)/shard_map/exchange/pallas_call | solution.py:520
  361.0 1.3 slice.44
  362.9 1.4 multiply_reduce_fusion.2
  365.5 53.2 %combine.1 = (bf16[8192,384]{1,0:T(8,128)(2,1)}, f32[128,384]{1,0:T(8,128)}, f32[768,1536]{1,0:T(8,128)}, f32[2,1536,384]{2,1,0:T(8,128)}) custom-call(s32[8192]{0:T(1024)} %add_select_fusion.slot_ref, bf16[16,2,320,384]{3,2,1,0:T(8,128)(2,1)} %get-tuple-element.19.back_ref, f32[16,8,384]{2,1,0:T(8,128)} %get-tuple-element.20.g_ref, ...), custom_call_target="tpu_custom_call" | custom-call | tf_op jit(solution)/shard_map/combine/pallas_call | solution.py:184
  418.7 0.9 add_bitcast_fusion
  420.4 12.2 %total.1 = f32[16,8,128]{2,1,0:T(8,128)} custom-call(f32[16,8,128]{2,1,0:T(8,128)} %pad.9.part_ref), custom_call_target="tpu_custom_call" | custom-call | tf_op jit(solution)/shard_map/total/pallas_call | solution.py:262
  432.6 0.9 reshape.98
  433.6 0.7 copy.20
  (26 shorter events, 5.1 us)
Async XLA Ops:
  6.3 7.8 %copy-start.3 = (bf16[192,384]{1,0:T(8,128)(2,1)}, bf16[192,384]{1,0:T(8,128)(2,1)S(1)}, u32[]{:S(2)}) copy-start(bf16[192,384]{1,0:T(8,128)(2,1)S(1)} %fusion.9.wr_t_ref) | copy-start | bytes 442372
  17.6 4.2 copy-start.1
  21.8 5.6 %copy-start.2 = (s32[8192]{0:T(1024)S(1)}, s32[8192]{0:T(1024)}, u32[]{:S(2)}) copy-start(s32[8192]{0:T(1024)} %param.8) | copy-start | bytes 98308
  27.5 8.8 %copy-start = (f32[8192,32]{1,0:T(8,128)}, f32[8192,32]{1,0:T(8,128)S(1)}, u32[]{:S(2)}) copy-start(f32[8192,32]{1,0:T(8,128)S(1)} %get-tuple-element.49.p_ref) | copy-start | bytes 3145732

commit v4 on v3

--- a/solution.py
+++ b/solution.py
@@ -26,77 +26,6 @@
     base = jnp.sum(before[:, :, None] * totals[None, :, :], axis=1)
     position = jnp.sum((within + base[:, None, :]) * chosen, axis=-1).reshape(tokens).astype(jnp.int32) - 1
     return jnp.where(position < capacity, idx_group * capacity + position, num_experts * capacity), base[-1] + totals[-1]
-
-
-def dispatch_kernel(blocks, capacity, slot_ref, x_ref, dy_ref, gate_ref, xd_ref, gates_ref, table, stage):
-    step = pl.program_id(0)
-    d_model = x_ref.shape[1]
-    cols = d_model // 128
-    lanes = gates_ref.shape[2]
-    n_local = xd_ref.shape[1]
-
-    @pl.when(step == 0)
-    def _():
-        def clear(i, carry):
-            table[pl.ds(pl.multiple_of(i * 512, 512), 512), :] = jnp.zeros((512, 128), jnp.float32)
-            return carry
-        lax.fori_loop(0, table.shape[0] // 512, clear, 0)
-
-    @pl.when(step < blocks)
-    def _():
-        for c in range(cols):
-            stage[pl.ds(c, TOKEN_BLOCK, stride=8), :] = x_ref[:, c * 128:(c + 1) * 128].astype(jnp.float32)
-            stage[pl.ds(cols + c, TOKEN_BLOCK, stride=8), :] = dy_ref[:, c * 128:(c + 1) * 128].astype(jnp.float32)
-        stage[pl.ds(2 * cols, TOKEN_BLOCK, stride=8), :] = gate_ref[...]
-
-        def place(i, carry):
-            for u in range(UNROLL):
-                t = i * UNROLL + u
-                slot = slot_ref[step * TOKEN_BLOCK + t]
-                table[pl.ds(pl.multiple_of(slot * 8, 8), 8), :] = stage[pl.ds(pl.multiple_of(t * 8, 8), 8), :]
-            return carry
-        lax.fori_loop(0, TOKEN_BLOCK // UNROLL, place, 0)
-
-    @pl.when(step >= blocks)
-    def _():
-        dst = step - blocks
-        gates_ref[...] = jnp.zeros_like(gates_ref)
-        for e in range(n_local):
-            first = (dst * n_local + e) * (capacity * 8)
-            for c in range(cols):
-                xd_ref[0, e, 0, :, c * 128:(c + 1) * 128] = table[pl.ds(first + c, capacity, stride=8), :].astype(jnp.bfloat16)
-                xd_ref[0, e, 1, :, c * 128:(c + 1) * 128] = table[pl.ds(first + cols + c, capacity, stride=8), :].astype(jnp.bfloat16)
-            gate = table[pl.ds(first + 2 * cols, capacity, stride=8), :]
-            row = lax.broadcasted_iota(jnp.int32, (capacity, 128), 0)
-            lane = lax.broadcasted_iota(jnp.int32, (capacity, 128), 1)
-            for c in range(lanes // 128):
-                gates_ref[0, e:e + 1, c * 128:(c + 1) * 128] = jnp.sum(
-                    jnp.where(row == lane + c * 128, gate, 0.0), axis=0, keepdims=True)
-
-
-def dispatch(tok_slot, x_tokens, grad_y, gate_rows, n_dev, n_local, capacity, lanes):
-    tokens, d_model = x_tokens.shape
-    blocks = tokens // TOKEN_BLOCK
-    n_slots = n_dev * n_local * capacity
-    table_rows = -(-(n_slots + 1) * 8 // 512) * 512
-    tok = lambda i: (jnp.minimum(i, blocks - 1), 0)
-    dst = lambda i: jnp.maximum(i - blocks, 0)
-    return pl.pallas_call(
-        functools.partial(dispatch_kernel, blocks, capacity),
-        grid=(blocks + n_dev,),
-        out_shape=(jax.ShapeDtypeStruct((n_dev, n_local, 2, capacity, d_model), jnp.bfloat16),
-                   jax.ShapeDtypeStruct((n_dev, 8, lanes), jnp.float32)),
-        in_specs=[pl.BlockSpec(memory_space=pltpu.SMEM),
-                  pl.BlockSpec((TOKEN_BLOCK, d_model), tok),
-                  pl.BlockSpec((TOKEN_BLOCK, d_model), tok),
-                  pl.BlockSpec((TOKEN_BLOCK, 128), tok)],
-        out_specs=(pl.BlockSpec((1, n_local, 2, capacity, d_model), lambda i: (dst(i), 0, 0, 0, 0)),
-                   pl.BlockSpec((1, 8, lanes), lambda i: (dst(i), 0, 0))),
-        scratch_shapes=[pltpu.VMEM((table_rows, 128), jnp.float32),
-                        pltpu.VMEM((TOKEN_BLOCK * 8, 128), jnp.float32)],
-        compiler_params=pltpu.CompilerParams(dimension_semantics=('arbitrary',), vmem_limit_bytes=60 * 1024 * 1024),
-        name='dispatch',
-    )(tok_slot, x_tokens, grad_y, gate_rows)
 
 
 def split3(v):
@@ -295,32 +224,32 @@
     return pieces
 
 
-def exchange_kernel(n, n_local, xd_ref, gate_ref, stat_ref, w_in_ref, w_out_ref,
+def exchange_kernel(n, n_local, cap, x_ref, dy_ref, slot_ref, gate_ref, stat_ref, w_in_ref, w_out_ref,
                     gw_in_ref, gw_out_t_ref, back_ref, g_back_ref, stat_out_ref,
-                    xr, gate_r, g_s, stat_r,
+                    table, w_a_all, w_b_all, staged, packed, gate_acc, xr, gate_s, gate_r, g_s, stat_r,
                     fwd_send, fwd_recv, gate_send, gate_recv,
                     ret_send, ret_recv, g_send, g_recv, stat_send, stat_recv, loc_sem):
     me = lax.axis_index('ep')
-    cap, d_model = xr.shape[3], xr.shape[4]
+    d_model = x_ref.shape[1]
     d_ff = w_in_ref.shape[2]
+    lanes = gate_r.shape[2]
+    chunks, chunk_tok = slot_ref.shape
 
     def peer_of(k):
         return flip_bits(me, k, n)
 
-    def fwd_copy(k, e, part):
+    def fwd_copy(k, e, part, src):
         sem = (k * n_local + e) * 2 + part
-        peer = peer_of(k)
         return pltpu.make_async_remote_copy(
-            src_ref=xd_ref.at[peer, e, part], dst_ref=xr.at[k, e, part],
+            src_ref=src.at[part], dst_ref=xr.at[k, e, part],
             send_sem=fwd_send.at[sem], recv_sem=fwd_recv.at[sem],
-            device_id=(peer,), device_id_type=MESH)
+            device_id=(peer_of(k),), device_id_type=MESH)
 
     def gate_copy(k):
-        peer = peer_of(k)
         return pltpu.make_async_remote_copy(
-            src_ref=gate_ref.at[peer], dst_ref=gate_r.at[k],
+            src_ref=gate_s.at[k], dst_ref=gate_r.at[k],
             send_sem=gate_send.at[k], recv_sem=gate_recv.at[k],
-            device_id=(peer,), device_id_type=MESH)
+            device_id=(peer_of(k),), device_id_type=MESH)
 
     def stat_copy(k):
         return pltpu.make_async_remote_copy(
@@ -346,20 +275,27 @@
     def interleave(queues):
         return [queue[i] for i in range(len(queues[0])) for queue in queues]
 
-    def send_rows(queues):
-        for k, e in interleave(queues):
-            if e == 0:
-                gate_copy(k).start()
-                stat_copy(k).start()
-            for part in range(2):
-                fwd_copy(k, e, part).start()
-
-    def rows_left(queues):
-        for queue in queues:
-            for i, (k, e) in enumerate(queue):
-                fwd_copy(k, e, 0).wait_send()
-                if i < len(queue) - 1:
-                    fwd_copy(k, e, 1).wait_send()
+    near = [[(1, e) for e in range(n_local)]]
+    order = [(0, e) for e in range(n_local)] + near[0]
+    first = []
+    for queues in sets:
+        first.append(len(order))
+        order = order + interleave(queues)
+    assert order == [tile_at(t) for t in range(len(order))]
+
+    def rows_sent(k, e, part):
+        fwd_copy(k, e, part, staged.at[0, 0]).wait_send()
+
+    def rows_left(i):
+        for queue in sets[i]:
+            for j, (k, e) in enumerate(queue):
+                rows_sent(k, e, 0)
+                if j < len(queue) - 1:
+                    rows_sent(k, e, 1)
+
+    def rows_done(i):
+        for queue in sets[i]:
+            rows_sent(*queue[-1], 1)
 
     def send_grads(queues):
         for k, e in interleave(queues):
@@ -367,35 +303,63 @@
             if e == n_local - 1:
                 g_copy(k).start()
 
-    def grads_left(queues):
-        for queue in queues:
+    def grads_left(i):
+        for queue in sets[i]:
             for k, e in queue[:-1]:
                 ret_copy(k, e).wait_send()
 
-    near = [[(1, e) for e in range(n_local)]]
-    own_in = [pltpu.make_async_copy(xd_ref.at[me, e], xr.at[0, e], loc_sem.at[e]) for e in range(n_local)]
-    own_gate = pltpu.make_async_copy(gate_ref.at[me], gate_r.at[0], loc_sem.at[n_local])
-    own_out = [pltpu.make_async_copy(xr.at[0, e, 0], back_ref.at[me, e], loc_sem.at[e]) for e in range(n_local)]
-    own_g = pltpu.make_async_copy(g_s.at[0], g_back_ref.at[me], loc_sem.at[n_local])
-
-    send_rows(sets[0])
-    send_rows(near)
-    for c in own_in:
-        c.start()
-    own_gate.start()
-    gw_in_ref[...] = jnp.zeros_like(gw_in_ref)
-    gw_out_t_ref[...] = jnp.zeros_like(gw_out_t_ref)
-    g_s[...] = jnp.zeros_like(g_s)
-    stat_r[me] = stat_ref[...]
-    for c in own_in:
-        c.wait()
-    own_gate.wait()
-
-    lanes = gate_r.shape[2]
+    eye = (lax.broadcasted_iota(jnp.int32, (cap, lanes), 0)
+           == lax.broadcasted_iota(jnp.int32, (cap, lanes), 1))
+
+    def pack(k, e, dst):
+        base = (peer_of(k) * n_local + e) * cap
+        packed[...] = jnp.zeros_like(packed)
+        gate_acc[...] = jnp.zeros_like(gate_acc)
+        own_row = lax.broadcasted_iota(jnp.int32, (cap, chunk_tok), 0)
+
+        def chunk(c, carry):
+            hit = own_row == slot_ref[pl.ds(c, 1), :] - base
+            start = pl.multiple_of(c * chunk_tok, chunk_tok)
+            packed[...] += jnp.dot(jnp.where(hit, 1.0, 0.0).astype(jnp.bfloat16), table[pl.ds(start, chunk_tok), :],
+                                   preferred_element_type=jnp.float32)
+            picked = jnp.where(hit, gate_ref[pl.ds(c, 1), :], 0.0)
+            for i in range(chunk_tok // 128):
+                gate_acc[...] += picked[:, i * 128:(i + 1) * 128]
+            return carry
+
+        lax.fori_loop(0, chunks, chunk, 0)
+        dst[0] = packed[:, :d_model].astype(jnp.bfloat16)
+        dst[1] = packed[:, d_model:].astype(jnp.bfloat16)
+        gate_col = jnp.sum(gate_acc[...], axis=1, keepdims=True)
+        gate_s[k, pl.ds(e, 1), :] = jnp.sum(jnp.where(eye, gate_col, 0.0), axis=0, keepdims=True)
+
+    def send_piece(k, e, src):
+        for part in range(2):
+            fwd_copy(k, e, part, src).start()
+
+        @pl.when(e == n_local - 1)
+        def _():
+            gate_copy(k).start()
+            stat_copy(k).start()
+
+    def make_pieces(i, lo, hi, send):
+        def body(j, carry):
+            k, e = tile_at(first[i] + j)
+            buf = staged.at[i % 2, j]
+            pack(k, e, buf)
+            if send:
+                send_piece(k, e, buf)
+            return carry
+        lax.fori_loop(lo, hi, body, 0)
+
+    def send_pieces(i, lo, hi):
+        def body(j, carry):
+            k, e = tile_at(first[i] + j)
+            send_piece(k, e, staged.at[i % 2, j])
+            return carry
+        lax.fori_loop(lo, hi, body, 0)
 
     def tile(k, e):
-        eye = (lax.broadcasted_iota(jnp.int32, (cap, lanes), 0)
-               == lax.broadcasted_iota(jnp.int32, (cap, lanes), 1))
         rows = xr[k, e, 0]
         dy = xr[k, e, 1].astype(jnp.float32)
         gate_row = gate_r[k, pl.ds(e, 1), :]
@@ -407,8 +371,8 @@
         d_rows = jnp.zeros((cap, d_model), jnp.float32)
         for f in range(0, d_ff, F_CHUNK):
             fs = pl.ds(f, F_CHUNK)
-            w_a = w_in_ref[e, :, fs]
-            w_b = w_out_ref[e, fs, :]
+            w_a = w_a_all[e, :, fs]
+            w_b = w_b_all[e, fs, :]
             pre = jnp.dot(rows, w_a, preferred_element_type=jnp.float32)
             hid = jnp.maximum(pre, 0.0).astype(jnp.bfloat16)
             out = out + jnp.dot(hid, w_b, preferred_element_type=jnp.float32)
@@ -422,73 +386,107 @@
         g_s[k, pl.ds(e, 1), :] = jnp.sum(jnp.where(eye, g_col, 0.0), axis=0, keepdims=True)
         xr[k, e, 0] = d_rows.astype(jnp.bfloat16)
 
-    order = [(0, e) for e in range(n_local)] + near[0]
-    first = []
-    for queues in sets:
-        first.append(len(order))
-        order = order + interleave(queues)
-    assert order == [tile_at(t) for t in range(len(order))]
-
-    def own_back():
-        send_grads(near)
-        for c in own_out:
-            c.start()
-        own_g.start()
-
-    def after_rows(done, then):
-        def run():
-            rows_left(sets[done])
-            then()
-        return run
-
-    def after_grads(done, then):
-        def run():
-            grads_left(sets[done])
-            then()
-        return run
-
-    events = {
-        first[0]: own_back,
-        first[1] - 2: after_rows(0, lambda: send_rows(sets[1])),
-        first[2] - 2: after_rows(1, lambda: send_grads(sets[0])),
-        first[2]: after_grads(0, lambda: send_rows(sets[2])),
-        first[3] - 2: after_rows(2, lambda: send_grads(sets[1])),
-        first[3]: after_grads(1, lambda: send_rows(sets[3])),
-        len(order) - 1: after_rows(3, lambda: send_grads(sets[2])),
-    }
-
-    def step(t, carry):
-        k, e = tile_at(t)
-        for at, run in events.items():
-            pl.when(t == at)(run)
-
-        @pl.when(t >= n_local)
-        def _():
-            @pl.when(e == 0)
+    def tiles(lo, hi, events=None):
+        def body(t, carry):
+            for at, run in (events or {}).items():
+                pl.when(t == at)(run)
+            k, e = tile_at(t)
+
+            @pl.when(t >= n_local)
             def _():
-                gate_copy(k).wait_recv()
-            for part in range(2):
-                fwd_copy(k, e, part).wait_recv()
-
-        tile(k, e)
+                @pl.when(e == 0)
+                def _():
+                    gate_copy(k).wait_recv()
+                for part in range(2):
+                    fwd_copy(k, e, part, staged.at[0, 0]).wait_recv()
+
+            tile(k, e)
+            return carry
+        lax.fori_loop(lo, hi, body, 0)
+
+    load_x = pltpu.make_async_copy(x_ref, table.at[:, pl.ds(0, d_model)], loc_sem.at[0])
+    load_dy = pltpu.make_async_copy(dy_ref, table.at[:, pl.ds(d_model, d_model)], loc_sem.at[1])
+    load_a = pltpu.make_async_copy(w_in_ref, w_a_all, loc_sem.at[2])
+    load_b = pltpu.make_async_copy(w_out_ref, w_b_all, loc_sem.at[3])
+    for c in (load_x, load_dy, load_a, load_b):
+        c.start()
+    gate_s[...] = jnp.zeros_like(gate_s)
+    g_s[...] = jnp.zeros_like(g_s)
+    stat_r[me] = stat_ref[...]
+    load_x.wait()
+    load_dy.wait()
+
+    make_pieces(0, 0, 8, True)
+    make_pieces(1, 0, 2, False)
+    rows_left(0)
+    send_pieces(1, 0, 2)
+    make_pieces(1, 2, 8, True)
+    gw_in_ref[...] = jnp.zeros_like(gw_in_ref)
+    gw_out_t_ref[...] = jnp.zeros_like(gw_out_t_ref)
+    load_a.wait()
+    load_b.wait()
+    tiles(first[0], first[1])
+    rows_left(1)
+    send_grads(sets[0])
+    rows_done(0)
+    make_pieces(2, 0, 4, False)
+    grads_left(0)
+    send_pieces(2, 0, 4)
+    make_pieces(2, 4, 8, True)
+    tiles(first[1], first[2])
+    rows_done(1)
+    make_pieces(3, 0, 2, False)
+    rows_left(2)
+    send_grads(sets[1])
+    make_pieces(3, 2, 4, False)
+
+    def start_last():
+        grads_left(1)
+        send_pieces(3, 0, 4)
+
+    tiles(first[2], first[3], {first[3] - 2: start_last})
+    rows_done(2)
+
+    def near_piece(j, carry):
+        k, e = tile_at(n_local + j)
+        pack(k, e, staged.at[0, j])
+        send_piece(k, e, staged.at[0, j])
         return carry
 
-    lax.fori_loop(0, len(order), step, 0)
-    grads_left(sets[2])
+    lax.fori_loop(0, n_local, near_piece, 0)
+
+    def own_piece(j, carry):
+        pack(0, j, xr.at[0, j])
+        return carry
+
+    lax.fori_loop(0, n_local, own_piece, 0)
+    gate_r[0] = gate_s[0]
+    tiles(0, first[0])
+    own_out = [pltpu.make_async_copy(xr.at[0, e, 0], back_ref.at[me, e], loc_sem.at[e]) for e in range(n_local)]
+    own_g = pltpu.make_async_copy(g_s.at[0], g_back_ref.at[me], loc_sem.at[n_local])
+    send_grads(near)
+    for c in own_out:
+        c.start()
+    own_g.start()
+
+    def start_third():
+        rows_left(3)
+        send_grads(sets[2])
+
+    tiles(first[3], len(order), {len(order) - 1: start_third})
+    grads_left(2)
     send_grads(sets[3])
 
-    for queues in sets:
-        for queue in queues:
-            k, e = queue[-1]
-            fwd_copy(k, e, 1).wait_send()
-            if queues is not sets[3]:
-                ret_copy(k, e).wait_send()
-    grads_left(sets[3])
+    rows_done(3)
+    for i in range(3):
+        for queue in sets[i]:
+            ret_copy(*queue[-1]).wait_send()
+    grads_left(3)
     for queue in sets[3]:
         ret_copy(*queue[-1]).wait_send()
     for k, e in near[0]:
         for part in range(2):
-            fwd_copy(k, e, part).wait_send()
+            rows_sent(k, e, part)
         ret_copy(k, e).wait_send()
     for c in own_out:
         c.wait()
@@ -509,35 +507,40 @@
     stat_out_ref[...] = stat
 
 
-def exchange(xd, gates, stats, w_in, w_out, n_dev):
+def exchange(x_tokens, grad_y, tok_slot, gate_val, stats, w_in, w_out, n_dev, cap, lanes):
     n_local, d_model, d_ff = w_in.shape
-    cap = xd.shape[3]
-    lanes = gates.shape[2]
+    tokens = x_tokens.shape[0]
     any_spec = pl.BlockSpec(memory_space=pl.ANY)
     vmem_spec = pl.BlockSpec(memory_space=pltpu.VMEM)
     pairs = n_dev * n_local
     dma = pltpu.SemaphoreType.DMA
+    small = pltpu.VMEM((n_dev, 8, lanes), jnp.float32)
     return pl.pallas_call(
-        functools.partial(exchange_kernel, n_dev, n_local),
+        functools.partial(exchange_kernel, n_dev, n_local, cap),
         out_shape=(jax.ShapeDtypeStruct((n_local, d_model, d_ff), jnp.float32),
                    jax.ShapeDtypeStruct((n_local, d_model, d_ff), jnp.float32),
                    jax.ShapeDtypeStruct((n_dev, n_local, cap, d_model), jnp.bfloat16),
                    jax.ShapeDtypeStruct((n_dev, 8, lanes), jnp.float32),
                    jax.ShapeDtypeStruct(stats.shape, jnp.float32)),
-        in_specs=[any_spec, any_spec, vmem_spec, vmem_spec, vmem_spec],
+        in_specs=[any_spec, any_spec, vmem_spec, vmem_spec, vmem_spec, any_spec, any_spec],
         out_specs=(vmem_spec, vmem_spec, any_spec, any_spec, vmem_spec),
         scratch_shapes=[
+            pltpu.VMEM((tokens, 2 * d_model), jnp.bfloat16),
+            pltpu.VMEM(w_in.shape, jnp.bfloat16),
+            pltpu.VMEM(w_out.shape, jnp.bfloat16),
+            pltpu.VMEM((2, 8, 2, cap, d_model), jnp.bfloat16),
+            pltpu.VMEM((cap, 2 * d_model), jnp.float32),
+            pltpu.VMEM((cap, 128), jnp.float32),
             pltpu.VMEM((n_dev, n_local, 2, cap, d_model), jnp.bfloat16),
-            pltpu.VMEM((n_dev, 8, lanes), jnp.float32),
-            pltpu.VMEM((n_dev, 8, lanes), jnp.float32),
+            small, small, small,
             pltpu.VMEM((n_dev,) + stats.shape, jnp.float32),
             dma((2 * pairs,)), dma((2 * pairs,)), dma((n_dev,)), dma((n_dev,)),
             dma((pairs,)), dma((pairs,)), dma((n_dev,)), dma((n_dev,)),
-            dma((n_dev,)), dma((n_dev,)), dma((n_local + 1,)),
+            dma((n_dev,)), dma((n_dev,)), dma((4,)),
         ],
-        compiler_params=pltpu.CompilerParams(has_side_effects=True, vmem_limit_bytes=60 * 1024 * 1024),
+        compiler_params=pltpu.CompilerParams(has_side_effects=True, vmem_limit_bytes=63 * 1024 * 1024),
         name='exchange',
-    )(xd, gates, stats, w_in, w_out)
+    )(x_tokens, grad_y, tok_slot.reshape(-1, 512), gate_val.reshape(-1, 512), stats, w_in, w_out)
 
 
 def solution(mesh):
@@ -558,8 +561,7 @@
         gate_val = jnp.sum(router_prob * onehot, axis=-1, keepdims=True)
         stats = jnp.concatenate([load, jnp.sum(router_prob, axis=0), jnp.sum(log_norm * log_norm)[None]])
         stats = jnp.pad(stats[None], ((0, 7), (0, 128 - stats.shape[0])))
-        xd, gates = dispatch(tok_slot, x_tokens, grad_y, jnp.broadcast_to(gate_val, (tokens, 128)), n_dev, n_local, capacity, lanes)
-        gw_in, gw_out_t, back, g_back, stats = exchange(xd, gates, stats, w_in, w_out, n_dev)
+        gw_in, gw_out_t, back, g_back, stats = exchange(x_tokens, grad_y, tok_slot, gate_val, stats, w_in, w_out, n_dev, capacity, lanes)
 
         load_frac = stats[0, :num_experts] / total_tok
         mean_prob = stats[0, num_experts:2 * num_experts] / total_tok

time: 439 us -> 560 us (1.28)
  Pallas kernels: 387 us -> 504 us
    pallas_call x2 -> x1, Pallas kernels: 322 us -> 439 us  [exchange(): pl.pallas_call(functools.partial(exchange_kernel, n_dev, n_local, cap), o...]
where the time goes in v4:
time: 560 us; the launch traced here: 557 us
  Pallas kernels  504 us (90%)
  other arithmetic  31.8 us (6%)
  local copies, waits for them, and re-layouts  12.3 us (2%)
    pallas_call x1, Pallas kernels, exchange(): pl.pallas_call(functools.partial(exchange_kernel, n_dev, n_local, cap), o...  439 us
    pallas_call x1, Pallas kernels, combine(): pl.pallas_call(functools.partial(combine_kernel, n_dev, capacity), grid=(...  53.2 us
    pallas_call x1, Pallas kernels, total(): pl.pallas_call(functools.partial(total_kernel, n_dev), out_shape=jax.Shap...  11.3 us

profile of v4, /device:TPU:0, one launch (start us, length us, event | category | flops | bytes accessed | tf_op | source)
XLA Modules:
  0.0 557.2 jit_solution(12019055761459128340)
XLA Ops:
  0.6 0.8 eq.22
  1.4 0.8 constant_dynamic-update-slice_fusion.4
  2.2 0.8 constant_dynamic-update-slice_fusion.3
  3.0 0.8 constant_dynamic-update-slice_fusion.2
  3.8 0.8 constant_dynamic-update-slice_fusion.1
  4.7 0.8 constant_dynamic-update-slice_fusion
  5.5 0.8 fusion.9.wr_t_ref
  7.8 0.8 add_select_fusion.slot_ref
  9.2 4.8 fusion.16
  14.9 2.7 copy.18
  17.6 4.2 fusion.1
  21.9 5.6 %broadcast_multiply_fusion = (f32[8192,32]{1,0:T(8,128)}, f32[8192,32]{1,0:T(8,128)S(1)}) fusion(f32[8192]{0:T(1024)S(1)} %get-tuple-element.47, f32[8192]{0:T(1024)S(1)} %fusion.1, f32[8192,32]{1,0:T(8,128)S(1)} %copy-done.1, f32[8192]{0:T(1024)S(1)} %get-tuple-element.50), kind=kLoop, calls=%fused_computation.6 | loop fusion | flops 786432 | bytes 3244032 | tf_op jit(solution)/shard_map/mul | solution.py:572
  27.5 2.0 copy-done
  29.6 2.5 fusion.14
  32.1 0.7 maximum_bitcast_fusion
  34.0 9.4 %subtract_multiply_fusion.ohg_ref = f32[8192,32]{1,0:T(8,128)} fusion(f32[8192,32]{1,0:T(8,128)} %copy-done, f32[8192]{0:T(1024)S(1)} %get-tuple-element.43, s32[8192]{0:T(1024)S(1)} %copy-done.2), kind=kLoop, calls=%fused_computation | loop fusion | flops 1048576 | bytes 2162688 | tf_op jit(solution)/shard_map/mul | solution.py:571
  43.4 439.1 %exchange.1 = (f32[2,384,1536]{2,1,0:T(8,128)}, f32[2,384,1536]{2,1,0:T(8,128)}, bf16[16,2,320,384]{3,2,1,0:T(8,128)(2,1)}, f32[16,8,384]{2,1,0:T(8,128)}, f32[8,128]{1,0:T(8,128)}) custom-call(bf16[8192,384]{1,0:T(8,128)(2,1)} %x_ref.3, bf16[8192,384]{1,0:T(8,128)(2,1)} %dy_ref.1, s32[16,512]{1,0:T(8,128)} %reshape.98.slot_ref, ...), custom_call_target="tpu_custom_call" | custom-call | tf_op jit(solution)/shard_map/exchange/pallas_call | solution.py:518
  482.5 1.3 slice.44
  484.4 1.4 multiply_reduce_fusion.2
  487.1 53.2 %combine.1 = (bf16[8192,384]{1,0:T(8,128)(2,1)}, f32[128,384]{1,0:T(8,128)}, f32[768,1536]{1,0:T(8,128)}, f32[2,1536,384]{2,1,0:T(8,128)}) custom-call(s32[8192]{0:T(1024)} %copy-done.3, bf16[16,2,320,384]{3,2,1,0:T(8,128)(2,1)} %get-tuple-element.15.back_ref, f32[16,8,384]{2,1,0:T(8,128)} %get-tuple-element.16.g_ref, bf16[8192,384]{1,0:T(8,128)(2,1)} %x_ref.3, ...), custom_call_target="tpu_custom_call" | custom-call | tf_op jit(solution)/shard_map/combine/pallas_call | solution.py:113
  540.2 0.9 add_bitcast_fusion
  542.0 11.3 %total.1 = f32[16,8,128]{2,1,0:T(8,128)} custom-call(f32[16,8,128]{2,1,0:T(8,128)} %pad.9.part_ref), custom_call_target="tpu_custom_call" | custom-call | tf_op jit(solution)/shard_map/total/pallas_call | solution.py:191
  553.3 0.9 reshape.102
  554.2 0.7 copy.20
  (28 shorter events, 5.6 us)
Async XLA Ops:
  6.3 7.8 %copy-start.4 = (bf16[192,384]{1,0:T(8,128)(2,1)}, bf16[192,384]{1,0:T(8,128)(2,1)S(1)}, u32[]{:S(2)}) copy-start(bf16[192,384]{1,0:T(8,128)(2,1)S(1)} %fusion.9.wr_t_ref) | copy-start | bytes 442372
  8.6 5.7 %copy-start.3 = (s32[8192]{0:T(1024)}, s32[8192]{0:T(1024)S(1)}, u32[]{:S(2)}) copy-start(s32[8192]{0:T(1024)S(1)} %add_select_fusion.slot_ref) | copy-start | bytes 98308
  17.6 4.2 copy-start.1
  21.9 7.7 %copy-start.2 = (s32[8192]{0:T(1024)S(1)}, s32[8192]{0:T(1024)}, u32[]{:S(2)}) copy-start(s32[8192]{0:T(1024)} %param.8) | copy-start | bytes 98308
  27.5 2.0 copy-start

commit v5 on v3

--- a/solution.py
+++ b/solution.py
@@ -13,90 +13,16 @@
 F_CHUNK = 512
 TOKEN_BLOCK = 256
 UNROLL = 16
-
-
-def route_slots(onehot, idx_group, capacity):
-    tokens, num_experts = onehot.shape
-    blocks = tokens // TOKEN_BLOCK
-    chosen = onehot.reshape(blocks, TOKEN_BLOCK, num_experts)
-    lower = jnp.tril(jnp.ones((TOKEN_BLOCK, TOKEN_BLOCK), jnp.bfloat16))
-    within = jnp.einsum('ij,bje->bie', lower, chosen.astype(jnp.bfloat16), preferred_element_type=jnp.float32)
-    totals = within[:, -1, :]
-    before = (jnp.arange(blocks)[:, None] > jnp.arange(blocks)[None, :]).astype(jnp.float32)
-    base = jnp.sum(before[:, :, None] * totals[None, :, :], axis=1)
-    position = jnp.sum((within + base[:, None, :]) * chosen, axis=-1).reshape(tokens).astype(jnp.int32) - 1
-    return jnp.where(position < capacity, idx_group * capacity + position, num_experts * capacity), base[-1] + totals[-1]
-
-
-def dispatch_kernel(blocks, capacity, slot_ref, x_ref, dy_ref, gate_ref, xd_ref, gates_ref, table, stage):
-    step = pl.program_id(0)
-    d_model = x_ref.shape[1]
-    cols = d_model // 128
-    lanes = gates_ref.shape[2]
-    n_local = xd_ref.shape[1]
-
-    @pl.when(step == 0)
-    def _():
-        def clear(i, carry):
-            table[pl.ds(pl.multiple_of(i * 512, 512), 512), :] = jnp.zeros((512, 128), jnp.float32)
-            return carry
-        lax.fori_loop(0, table.shape[0] // 512, clear, 0)
-
-    @pl.when(step < blocks)
-    def _():
-        for c in range(cols):
-            stage[pl.ds(c, TOKEN_BLOCK, stride=8), :] = x_ref[:, c * 128:(c + 1) * 128].astype(jnp.float32)
-            stage[pl.ds(cols + c, TOKEN_BLOCK, stride=8), :] = dy_ref[:, c * 128:(c + 1) * 128].astype(jnp.float32)
-        stage[pl.ds(2 * cols, TOKEN_BLOCK, stride=8), :] = gate_ref[...]
-
-        def place(i, carry):
-            for u in range(UNROLL):
-                t = i * UNROLL + u
-                slot = slot_ref[step * TOKEN_BLOCK + t]
-                table[pl.ds(pl.multiple_of(slot * 8, 8), 8), :] = stage[pl.ds(pl.multiple_of(t * 8, 8), 8), :]
-            return carry
-        lax.fori_loop(0, TOKEN_BLOCK // UNROLL, place, 0)
-
-    @pl.when(step >= blocks)
-    def _():
-        dst = step - blocks
-        gates_ref[...] = jnp.zeros_like(gates_ref)
-        for e in range(n_local):
-            first = (dst * n_local + e) * (capacity * 8)
-            for c in range(cols):
-                xd_ref[0, e, 0, :, c * 128:(c + 1) * 128] = table[pl.ds(first + c, capacity, stride=8), :].astype(jnp.bfloat16)
-                xd_ref[0, e, 1, :, c * 128:(c + 1) * 128] = table[pl.ds(first + cols + c, capacity, stride=8), :].astype(jnp.bfloat16)
-            gate = table[pl.ds(first + 2 * cols, capacity, stride=8), :]
-            row = lax.broadcasted_iota(jnp.int32, (capacity, 128), 0)
-            lane = lax.broadcasted_iota(jnp.int32, (capacity, 128), 1)
-            for c in range(lanes // 128):
-                gates_ref[0, e:e + 1, c * 128:(c + 1) * 128] = jnp.sum(
-                    jnp.where(row == lane + c * 128, gate, 0.0), axis=0, keepdims=True)
-
-
-def dispatch(tok_slot, x_tokens, grad_y, gate_rows, n_dev, n_local, capacity, lanes):
-    tokens, d_model = x_tokens.shape
-    blocks = tokens // TOKEN_BLOCK
-    n_slots = n_dev * n_local * capacity
-    table_rows = -(-(n_slots + 1) * 8 // 512) * 512
-    tok = lambda i: (jnp.minimum(i, blocks - 1), 0)
-    dst = lambda i: jnp.maximum(i - blocks, 0)
-    return pl.pallas_call(
-        functools.partial(dispatch_kernel, blocks, capacity),
-        grid=(blocks + n_dev,),
-        out_shape=(jax.ShapeDtypeStruct((n_dev, n_local, 2, capacity, d_model), jnp.bfloat16),
-                   jax.ShapeDtypeStruct((n_dev, 8, lanes), jnp.float32)),
-        in_specs=[pl.BlockSpec(memory_space=pltpu.SMEM),
-                  pl.BlockSpec((TOKEN_BLOCK, d_model), tok),
-                  pl.BlockSpec((TOKEN_BLOCK, d_model), tok),
-                  pl.BlockSpec((TOKEN_BLOCK, 128), tok)],
-        out_specs=(pl.BlockSpec((1, n_local, 2, capacity, d_model), lambda i: (dst(i), 0, 0, 0, 0)),
-                   pl.BlockSpec((1, 8, lanes), lambda i: (dst(i), 0, 0))),
-        scratch_shapes=[pltpu.VMEM((table_rows, 128), jnp.float32),
-                        pltpu.VMEM((TOKEN_BLOCK * 8, 128), jnp.float32)],
-        compiler_params=pltpu.CompilerParams(dimension_semantics=('arbitrary',), vmem_limit_bytes=60 * 1024 * 1024),
-        name='dispatch',
-    )(tok_slot, x_tokens, grad_y, gate_rows)
+ROW_TOKENS = 1024
+GROUP = 2
+
+
+def nt_dot(a, b):
+    return lax.dot_general(a, b, (((1,), (1,)), ((), ())), preferred_element_type=jnp.float32)
+
+
+def eye_mask(rows, cols):
+    return lax.broadcasted_iota(jnp.int32, (rows, cols), 0) == lax.broadcasted_iota(jnp.int32, (rows, cols), 1)
 
 
 def split3(v):
@@ -107,13 +33,173 @@
     return hi, mid, low
 
 
-def combine_kernel(sources, capacity, slot_ref, back_ref, g_ref, x_ref, ohg_ref, p_ref, zp_ref, aux_ref, wr_t_ref, gwi_ref, gwo_t_ref,
-                   gx_ref, gwr_ref, gwi_out_ref, gwo_out_ref, table, stage):
+def split_weights(w):
+    round_bf16 = lambda v: lax.reduce_precision(v, 8, 7)
+    hi = round_bf16(w)
+    mid = round_bf16(w - hi)
+    return hi, mid, w - hi - mid
+
+
+def route_kernel(capacity, x_ref, idx_ref, wr_ref, prob_ref, slot_ref, gate_ref, norm_ref, stat_ref, seen, load, prob_sum, z_sum):
     step = pl.program_id(0)
-    d_model = x_ref.shape[1]
+    num_experts, block = prob_ref.shape
+
+    @pl.when(step == 0)
+    def _():
+        seen[...] = jnp.zeros_like(seen)
+        prob_sum[...] = jnp.zeros_like(prob_sum)
+        z_sum[...] = jnp.zeros_like(z_sum)
+
+    parts = nt_dot(wr_ref[...], x_ref[...])
+    logits = parts[:num_experts] + parts[num_experts:2 * num_experts] + parts[2 * num_experts:]
+    top = jnp.max(logits, axis=0, keepdims=True)
+    shifted = jnp.exp(logits - top)
+    scale = jnp.sum(shifted, axis=0, keepdims=True)
+    prob = shifted / scale
+    log_norm = top + jnp.log(scale)
+    idx = idx_ref[pl.ds(step, 1), :]
+    chosen = jnp.where(lax.broadcasted_iota(jnp.int32, (num_experts, block), 0) == idx, 1.0, 0.0)
+    prob_ref[...] = prob
+    gate_ref[pl.ds(step, 1), :] = jnp.sum(prob * chosen, axis=0, keepdims=True)
+    norm_ref[pl.ds(step, 1), :] = log_norm
+    squares = log_norm * log_norm
+    for i in range(0, block, 128):
+        prob_sum[...] += prob[:, i:i + 128]
+        z_sum[0:1, :] += squares[:, i:i + 128]
+    upto = jnp.where(lax.broadcasted_iota(jnp.int32, (TOKEN_BLOCK, TOKEN_BLOCK), 0)
+                     <= lax.broadcasted_iota(jnp.int32, (TOKEN_BLOCK, TOKEN_BLOCK), 1), 1.0, 0.0).astype(jnp.bfloat16)
+    before = seen[:, 0:1]
+    slots = []
+    for i in range(0, block, TOKEN_BLOCK):
+        part = chosen[:, i:i + TOKEN_BLOCK]
+        count = jnp.dot(part.astype(jnp.bfloat16), upto, preferred_element_type=jnp.float32) + before
+        position = jnp.sum(part * count, axis=0, keepdims=True).astype(jnp.int32) - 1
+        slots.append(jnp.where(position < capacity, idx[:, i:i + TOKEN_BLOCK] * capacity + position, num_experts * capacity))
+        before = count[:, TOKEN_BLOCK - 1:TOKEN_BLOCK]
+    slot_ref[pl.ds(step, 1), :] = jnp.concatenate(slots, axis=1)
+    seen[...] = jnp.broadcast_to(before, seen.shape)
+
+    @pl.when(step == pl.num_programs(0) - 1)
+    def _():
+        row = lax.broadcasted_iota(jnp.int32, (num_experts, 128), 0)
+        lane = lax.broadcasted_iota(jnp.int32, (num_experts, 128), 1)
+        probs = jnp.sum(prob_sum[...], axis=1, keepdims=True)
+        stat_ref[...] = jnp.zeros_like(stat_ref)
+        total = jnp.sum(jnp.where(row == lane, seen[...], 0.0) + jnp.where(row + num_experts == lane, probs, 0.0),
+                        axis=0, keepdims=True)
+        squares = jnp.sum(z_sum[0:1, :], axis=1, keepdims=True)
+        stat_ref[0:1, :] = total + jnp.where(lane[0:1, :] == 2 * num_experts, squares, 0.0)
+
+
+def route(x_tokens, idx_rows, w_router, capacity):
+    tokens, d_model = x_tokens.shape
+    num_experts = w_router.shape[1]
+    steps, block = idx_rows.shape
+    wr = jnp.concatenate(split_weights(w_router.T), axis=0).astype(jnp.bfloat16)
+    rows = lambda dtype: jax.ShapeDtypeStruct((steps, block), dtype)
+    whole = pl.BlockSpec((steps, block), lambda i: (0, 0))
+    return pl.pallas_call(
+        functools.partial(route_kernel, capacity),
+        grid=(steps,),
+        out_shape=(jax.ShapeDtypeStruct((num_experts, tokens), jnp.float32), rows(jnp.int32), rows(jnp.float32), rows(jnp.float32),
+                   jax.ShapeDtypeStruct((8, 128), jnp.float32)),
+        in_specs=[pl.BlockSpec((block, d_model), lambda i: (i, 0)), whole,
+                  pl.BlockSpec((3 * num_experts, d_model), lambda i: (0, 0))],
+        out_specs=(pl.BlockSpec((num_experts, block), lambda i: (0, i)), whole, whole, whole,
+                   pl.BlockSpec((8, 128), lambda i: (0, 0))),
+        scratch_shapes=[pltpu.VMEM((num_experts, 128), jnp.float32), pltpu.VMEM((num_experts, 128), jnp.float32),
+                        pltpu.VMEM((num_experts, 128), jnp.float32), pltpu.VMEM((8, 128), jnp.float32)],
+        compiler_params=pltpu.CompilerParams(dimension_semantics=('arbitrary',)),
+        name='route',
+    )(x_tokens, idx_rows, wr)
+
+
+def dispatch_kernel(steps, capacity, slot_ref, x_ref, dy_ref, gate_ref, xd_ref, gates_ref, table, stage):
+    step = pl.program_id(0)
+    block, d_model = x_ref.shape
     cols = d_model // 128
-    n_local = back_ref.shape[1]
-    num_experts = p_ref.shape[1]
+    lanes = gates_ref.shape[2]
+    group, n_local = xd_ref.shape[:2]
+
+    @pl.when(step == 0)
+    def _():
+        def clear(i, carry):
+            table[pl.ds(pl.multiple_of(i * 512, 512), 512), :] = jnp.zeros((512, 128), jnp.float32)
+            return carry
+        lax.fori_loop(0, table.shape[0] // 512, clear, 0)
+
+    @pl.when(step < steps)
+    def _():
+        for c in range(cols):
+            stage[pl.ds(c, block, stride=8), :] = x_ref[:, c * 128:(c + 1) * 128].astype(jnp.float32)
+            stage[pl.ds(cols + c, block, stride=8), :] = dy_ref[:, c * 128:(c + 1) * 128].astype(jnp.float32)
+        eye = eye_mask(128, 128)
+        gate_row = gate_ref[pl.ds(step, 1), :]
+        for i in range(0, block, 128):
+            gate = jnp.sum(jnp.where(eye, gate_row[:, i:i + 128], 0.0), axis=1, keepdims=True)
+            stage[pl.ds(i * 8 + 2 * cols, 128, stride=8), :] = jnp.broadcast_to(gate, (128, 128))
+
+        def place(i, carry):
+            for u in range(UNROLL):
+                t = i * UNROLL + u
+                slot = slot_ref[step, t]
+                table[pl.ds(pl.multiple_of(slot * 8, 8), 8), :] = stage[pl.ds(pl.multiple_of(t * 8, 8), 8), :]
+            return carry
+        lax.fori_loop(0, block // UNROLL, place, 0)
+
+    @pl.when(step >= steps)
+    def _():
+        gates_ref[...] = jnp.zeros_like(gates_ref)
+        row = lax.broadcasted_iota(jnp.int32, (capacity, 128), 0)
+        lane = lax.broadcasted_iota(jnp.int32, (capacity, 128), 1)
+
+        def unload(i, carry):
+            d = i // n_local
+            e = i % n_local
+            first = (((step - steps) * group + d) * n_local + e) * (capacity * 8)
+            for c in range(cols):
+                xd_ref[d, e, 0, :, c * 128:(c + 1) * 128] = table[pl.ds(first + c, capacity, stride=8), :].astype(jnp.bfloat16)
+                xd_ref[d, e, 1, :, c * 128:(c + 1) * 128] = table[pl.ds(first + cols + c, capacity, stride=8), :].astype(jnp.bfloat16)
+            gate = table[pl.ds(first + 2 * cols, capacity, stride=8), :]
+            gates_ref[d, pl.ds(e, 1), :] = jnp.concatenate([
+                jnp.sum(jnp.where(row == lane + c * 128, gate, 0.0), axis=0, keepdims=True)
+                for c in range(lanes // 128)], axis=1)
+            return carry
+        lax.fori_loop(0, group * n_local, unload, 0)
+
+
+def dispatch(slot_rows, x_tokens, grad_y, gate_rows, n_dev, n_local, capacity, lanes):
+    tokens, d_model = x_tokens.shape
+    steps, block = slot_rows.shape
+    n_slots = n_dev * n_local * capacity
+    table_rows = -(-(n_slots + 1) * 8 // 512) * 512
+    tok = lambda i: (jnp.minimum(i, steps - 1), 0)
+    dst = lambda i: jnp.maximum(i - steps, 0)
+    return pl.pallas_call(
+        functools.partial(dispatch_kernel, steps, capacity),
+        grid=(steps + n_dev // GROUP,),
+        out_shape=(jax.ShapeDtypeStruct((n_dev, n_local, 2, capacity, d_model), jnp.bfloat16),
+                   jax.ShapeDtypeStruct((n_dev, 8, lanes), jnp.float32)),
+        in_specs=[pl.BlockSpec(memory_space=pltpu.SMEM),
+                  pl.BlockSpec((block, d_model), tok),
+                  pl.BlockSpec((block, d_model), tok),
+                  pl.BlockSpec((steps, block), lambda i: (0, 0))],
+        out_specs=(pl.BlockSpec((GROUP, n_local, 2, capacity, d_model), lambda i: (dst(i), 0, 0, 0, 0)),
+                   pl.BlockSpec((GROUP, 8, lanes), lambda i: (dst(i), 0, 0))),
+        scratch_shapes=[pltpu.VMEM((table_rows, 128), jnp.float32),
+                        pltpu.VMEM((block * 8, 128), jnp.float32)],
+        compiler_params=pltpu.CompilerParams(dimension_semantics=('arbitrary',), vmem_limit_bytes=62 * 1024 * 1024),
+        name='dispatch',
+    )(slot_rows, x_tokens, grad_y, gate_rows)
+
+
+def combine_kernel(fills, sources, capacity, z_coef, slot_ref, back_ref, g_ref, x_ref, prob_ref, gate_ref, norm_ref, idx_ref, aux_ref,
+                   wr_t_ref, gwi_ref, gwo_t_ref, gx_ref, gwr_ref, gwi_out_ref, gwo_out_ref, table, stage):
+    step = pl.program_id(0)
+    block, d_model = x_ref.shape
+    cols = d_model // 128
+    group, n_local = back_ref.shape[:2]
+    num_experts = prob_ref.shape[0]
     n_slots = sources * n_local * capacity
     gwi_out_ref[...] = gwi_ref[...]
     gwo_out_ref[0] = gwo_t_ref[0].T
@@ -123,92 +209,99 @@
         table[pl.ds(n_slots * 8, 8), :] = jnp.zeros((8, 128), jnp.float32)
         gwr_ref[...] = jnp.zeros_like(gwr_ref)
 
-    @pl.when(step < sources)
-    def _():
-        lanes = g_ref.shape[2]
-        eye = (lax.broadcasted_iota(jnp.int32, (capacity, lanes), 0)
-               == lax.broadcasted_iota(jnp.int32, (capacity, lanes), 1))
-        for e in range(n_local):
-            first = (step * n_local + e) * (capacity * 8)
+    @pl.when(step < fills)
+    def _():
+        eye = eye_mask(capacity, g_ref.shape[2])
+
+        def load(i, carry):
+            d = i // n_local
+            e = i % n_local
+            first = ((step * group + d) * n_local + e) * (capacity * 8)
             for c in range(cols):
-                table[pl.ds(first + c, capacity, stride=8), :] = back_ref[0, e, :, c * 128:(c + 1) * 128].astype(jnp.float32)
-            g_col = jnp.sum(jnp.where(eye, g_ref[0, e:e + 1, :], 0.0), axis=1, keepdims=True)
+                table[pl.ds(first + c, capacity, stride=8), :] = back_ref[d, e, :, c * 128:(c + 1) * 128].astype(jnp.float32)
+            g_col = jnp.sum(jnp.where(eye, g_ref[d, pl.ds(e, 1), :], 0.0), axis=1, keepdims=True)
             table[pl.ds(first + cols, capacity, stride=8), :] = jnp.broadcast_to(g_col, (capacity, 128))
-
-    @pl.when(step >= sources)
-    def _():
-        block = step - sources
+            return carry
+        lax.fori_loop(0, group * n_local, load, 0)
+
+    @pl.when(step >= fills)
+    def _():
+        part = step - fills
 
         def pick(i, carry):
             for u in range(UNROLL):
                 t = i * UNROLL + u
-                slot = slot_ref[block * TOKEN_BLOCK + t]
+                slot = slot_ref[part, t]
                 stage[pl.ds(pl.multiple_of(t * 8, 8), 8), :] = table[pl.ds(pl.multiple_of(slot * 8, 8), 8), :]
             return carry
-        lax.fori_loop(0, TOKEN_BLOCK // UNROLL, pick, 0)
-        g_tok = stage[pl.ds(cols, TOKEN_BLOCK, stride=8), :][:, :num_experts]
-        prob = p_ref[...]
-        aux_vec = aux_ref[0:1, :]
-        spread = jnp.sum(prob * aux_vec, axis=1, keepdims=True)
-        d_logits = g_tok * ohg_ref[...] + prob * (aux_vec - spread) + zp_ref[...]
+        lax.fori_loop(0, block // UNROLL, pick, 0)
+        eye = eye_mask(128, 128)
+        g_tok = jnp.concatenate([
+            jnp.sum(jnp.where(eye, stage[pl.ds(i * 8 + cols, 128, stride=8), :], 0.0), axis=0, keepdims=True)
+            for i in range(0, block, 128)], axis=1)
+        here = pl.ds(part, 1)
+        prob = prob_ref[...]
+        chosen = jnp.where(lax.broadcasted_iota(jnp.int32, (num_experts, block), 0) == idx_ref[here, :], 1.0, 0.0)
+        aux_vec = aux_ref[:, 0:1]
+        spread = jnp.sum(prob * aux_vec, axis=0, keepdims=True)
+        d_logits = ((gate_ref[here, :] * g_tok) * (chosen - prob) + prob * (aux_vec - spread)
+                    + (z_coef * norm_ref[here, :]) * prob)
         hi, mid, low = split3(d_logits)
-        left = jnp.concatenate([hi, mid, hi, low, mid, hi], axis=1)
-        dx_router = jnp.dot(left, wr_t_ref[...], preferred_element_type=jnp.float32)
+        gwr_ref[...] += jnp.dot(jnp.concatenate([hi, mid, low], axis=0), x_ref[...], preferred_element_type=jnp.float32)
+        left = jnp.concatenate([hi, mid, hi, low, mid, hi], axis=0)
+        dx_router = lax.dot_general(left, wr_t_ref[...], (((0,), (0,)), ((), ())), preferred_element_type=jnp.float32)
         for c in range(cols):
-            part = slice(c * 128, (c + 1) * 128)
-            gx_ref[:, part] = (stage[pl.ds(c, TOKEN_BLOCK, stride=8), :] + dx_router[:, part]).astype(jnp.bfloat16)
-        parts = jnp.concatenate([hi, mid, low, jnp.zeros_like(hi)], axis=1)
-        gwr_ref[...] += lax.dot_general(parts, x_ref[...], (((0,), (0,)), ((), ())), preferred_element_type=jnp.float32)
-
-
-def combine(tok_slot, back, g_back, x_tokens, ohg, prob, zp, aux_vec, w_router, gw_in, gw_out_t):
+            span = slice(c * 128, (c + 1) * 128)
+            gx_ref[:, span] = (stage[pl.ds(c, block, stride=8), :] + dx_router[:, span]).astype(jnp.bfloat16)
+
+
+def combine(slot_rows, back, g_back, x_tokens, prob, gate_rows, norm_rows, idx_rows, aux_vec, z_coef, w_router, gw_in, gw_out_t):
     n_dev, n_local, capacity, d_model = back.shape
     tokens = x_tokens.shape[0]
-    num_experts = prob.shape[1]
+    num_experts = prob.shape[0]
     d_ff = gw_in.shape[2]
-    blocks = tokens // TOKEN_BLOCK
-    steps = n_dev + blocks
+    blocks, block = slot_rows.shape
+    fills = n_dev // GROUP
+    steps = fills + blocks
     lanes = g_back.shape[2]
     n_slots = n_dev * n_local * capacity
-    round_bf16 = lambda v: lax.reduce_precision(v, 8, 7)
-    w_hi = round_bf16(w_router.T)
-    w_mid = round_bf16(w_router.T - w_hi)
-    w_low = w_router.T - w_hi - w_mid
+    w_hi, w_mid, w_low = split_weights(w_router.T)
     wr_t = jnp.concatenate([w_hi, w_hi, w_mid, w_hi, w_mid, w_low], axis=0).astype(jnp.bfloat16)
     gw_in_rows = gw_in.reshape(n_local * d_model, d_ff)
     in_rows = n_local * d_model // steps
-    out_cols = d_ff // 128
-    src = lambda i: jnp.minimum(i, n_dev - 1)
-    tok = lambda i: (jnp.maximum(i - n_dev, 0), 0)
+    out_cols = d_ff // 256
+    src = lambda i: jnp.minimum(i, fills - 1)
+    tok = lambda i: (jnp.maximum(i - fills, 0), 0)
     flip = lambda i: jnp.minimum(i, n_local * out_cols - 1)
+    rows = pl.BlockSpec((blocks, block), lambda i: (0, 0))
     gx, gwr, gw_in_out, gw_out = pl.pallas_call(
-        functools.partial(combine_kernel, n_dev, capacity),
+        functools.partial(combine_kernel, fills, n_dev, capacity, z_coef),
         grid=(steps,),
         out_shape=(jax.ShapeDtypeStruct((tokens, d_model), jnp.bfloat16),
-                   jax.ShapeDtypeStruct((4 * num_experts, d_model), jnp.float32),
+                   jax.ShapeDtypeStruct((3 * num_experts, d_model), jnp.float32),
                    jax.ShapeDtypeStruct((n_local * d_model, d_ff), jnp.float32),
                    jax.ShapeDtypeStruct((n_local, d_ff, d_model), jnp.float32)),
         in_specs=[pl.BlockSpec(memory_space=pltpu.SMEM),
-                  pl.BlockSpec((1, n_local, capacity, d_model), lambda i: (src(i), 0, 0, 0)),
-                  pl.BlockSpec((1, 8, lanes), lambda i: (src(i), 0, 0)),
-                  pl.BlockSpec((TOKEN_BLOCK, d_model), tok),
-                  pl.BlockSpec((TOKEN_BLOCK, num_experts), tok),
-                  pl.BlockSpec((TOKEN_BLOCK, num_experts), tok),
-                  pl.BlockSpec((TOKEN_BLOCK, num_experts), tok),
-                  pl.BlockSpec((8, num_experts), lambda i: (0, 0)),
+                  pl.BlockSpec((GROUP, n_local, capacity, d_model), lambda i: (src(i), 0, 0, 0)),
+                  pl.BlockSpec((GROUP, 8, lanes), lambda i: (src(i), 0, 0)),
+                  pl.BlockSpec((block, d_model), tok),
+                  pl.BlockSpec((num_experts, block), lambda i: (0, jnp.maximum(i - fills, 0))),
+                  rows, rows, rows,
+                  pl.BlockSpec((num_experts, 128), lambda i: (0, 0)),
                   pl.BlockSpec((6 * num_experts, d_model), lambda i: (0, 0)),
                   pl.BlockSpec((in_rows, d_ff), lambda i: (i, 0)),
-                  pl.BlockSpec((1, d_model, 128), lambda i: (flip(i) // out_cols, 0, flip(i) % out_cols))],
-        out_specs=(pl.BlockSpec((TOKEN_BLOCK, d_model), tok),
-                   pl.BlockSpec((4 * num_experts, d_model), lambda i: (0, 0)),
+                  pl.BlockSpec((1, d_model, 256), lambda i: (flip(i) // out_cols, 0, flip(i) % out_cols))],
+        out_specs=(pl.BlockSpec((block, d_model), tok),
+                   pl.BlockSpec((3 * num_experts, d_model), lambda i: (0, 0)),
                    pl.BlockSpec((in_rows, d_ff), lambda i: (i, 0)),
-                   pl.BlockSpec((1, 128, d_model), lambda i: (flip(i) // out_cols, flip(i) % out_cols, 0))),
+                   pl.BlockSpec((1, 256, d_model), lambda i: (flip(i) // out_cols, flip(i) % out_cols, 0))),
         scratch_shapes=[pltpu.VMEM(((n_slots + 1) * 8, 128), jnp.float32),
-                        pltpu.VMEM((TOKEN_BLOCK * 8, 128), jnp.float32)],
-        compiler_params=pltpu.CompilerParams(dimension_semantics=('arbitrary',), vmem_limit_bytes=60 * 1024 * 1024),
+                        pltpu.VMEM((block * 8, 128), jnp.float32)],
+        compiler_params=pltpu.CompilerParams(dimension_semantics=('arbitrary',), vmem_limit_bytes=63 * 1024 * 1024),
         name='combine',
-    )(tok_slot, back, g_back, x_tokens, ohg, prob, zp, jnp.broadcast_to(aux_vec, (8, num_experts)), wr_t, gw_in_rows, gw_out_t)
-    part = gwr.reshape(4, num_experts, d_model)
+    )(slot_rows, back, g_back, x_tokens, prob, gate_rows, norm_rows, idx_rows,
+      jnp.broadcast_to(aux_vec[:, None], (num_experts, 128)), wr_t, gw_in_rows, gw_out_t)
+    part = gwr.reshape(3, num_experts, d_model)
     return gx, (part[0] + part[1] + part[2]).T, gw_in_out.reshape(n_local, d_model, d_ff), gw_out
 
 
@@ -270,10 +363,6 @@
         name='total',
     )(chunks)
     return out[:, :piece].reshape(rows, cols)
-
-
-def nt_dot(a, b):
-    return lax.dot_general(a, b, (((1,), (1,)), ((), ())), preferred_element_type=jnp.float32)
 
 
 def tile_at(t):
@@ -550,15 +639,9 @@
         capacity = (5 * tokens + 4 * num_experts - 1) // (4 * num_experts)
         total_tok = tokens * n_dev
         lanes = -(-capacity // 128) * 128
-        onehot = (expert_idx[:, None] == jnp.arange(num_experts, dtype=jnp.int32)[None, :]).astype(jnp.float32)
-        tok_slot, load = route_slots(onehot, expert_idx, capacity)
-        logits = jnp.dot(x_tokens, w_router, preferred_element_type=jnp.float32)
-        router_prob = jax.nn.softmax(logits, axis=-1)
-        log_norm = jax.nn.logsumexp(logits, axis=-1, keepdims=True)
-        gate_val = jnp.sum(router_prob * onehot, axis=-1, keepdims=True)
-        stats = jnp.concatenate([load, jnp.sum(router_prob, axis=0), jnp.sum(log_norm * log_norm)[None]])
-        stats = jnp.pad(stats[None], ((0, 7), (0, 128 - stats.shape[0])))
-        xd, gates = dispatch(tok_slot, x_tokens, grad_y, jnp.broadcast_to(gate_val, (tokens, 128)), n_dev, n_local, capacity, lanes)
+        idx_rows = expert_idx.reshape(-1, ROW_TOKENS)
+        prob, slot_rows, gate_rows, norm_rows, stats = route(x_tokens, idx_rows, w_router, capacity)
+        xd, gates = dispatch(slot_rows, x_tokens, grad_y, gate_rows, n_dev, n_local, capacity, lanes)
         gw_in, gw_out_t, back, g_back, stats = exchange(xd, gates, stats, w_in, w_out, n_dev)
 
         load_frac = stats[0, :num_experts] / total_tok
@@ -566,9 +649,8 @@
         aux_loss = AUX_WEIGHT * num_experts * jnp.sum(load_frac * mean_prob)
         z_loss = Z_WEIGHT * stats[0, 2 * num_experts] / total_tok
         aux_vec = AUX_WEIGHT * num_experts * load_frac / total_tok
-        ohg = gate_val * (onehot - router_prob)
-        zp = (2.0 * Z_WEIGHT / total_tok * log_norm) * router_prob
-        grad_x, part, grad_w_in, grad_w_out = combine(tok_slot, back, g_back, x_tokens, ohg, router_prob, zp, aux_vec, w_router, gw_in, gw_out_t)
+        grad_x, part, grad_w_in, grad_w_out = combine(slot_rows, back, g_back, x_tokens, prob, gate_rows, norm_rows, idx_rows, aux_vec,
+                                                      2.0 * Z_WEIGHT / total_tok, w_router, gw_in, gw_out_t)
         grad_w_router = total(part, n_dev)
         return grad_x, grad_w_in, grad_w_out, grad_w_router, aux_loss, z_loss
 

time: 439 us -> 412 us (0.938)
  other arithmetic: 28 us -> 5.4 us
  Pallas kernels: 387 us -> 395 us
  local copies, waits for them, and re-layouts: 11.7 us -> 5.89 us
  matrix products: 5.15 us -> 0 us
    mul x2 -> x0, other arithmetic: 10.5 us -> none  [the longest x1 5.6 us: expert_layer(): zp = 2.0 * Z_WEIGHT / total_tok * log_norm * router_prob]
    reduce_sum x6 -> x0, other arithmetic: 8.16 us -> none  [the longest x1 4.22 us: expert_layer(): router_prob = jax.nn.softmax(logits, axis=-1)]
    pallas_call x2 -> x3, Pallas kernels: 97.7 us -> 105 us  [the longest x1 48.7 us: dispatch(): pl.pallas_call(functools.partial(dispatch_kernel, steps, capacity), grid=...]
    dot_general x2 -> x0, matrix products: 5.15 us -> none  [the longest x1 4.82 us: expert_layer(): logits = jnp.dot(x_tokens, w_router, preferred_element_type=jnp.float32)]
where the time goes in v5:
time: 412 us; the launch traced here: 410 us
  Pallas kernels  395 us (96%)
  local copies, waits for them, and re-layouts  5.89 us (1%)
  other arithmetic  5.4 us (1%)
  between operations  4.27 us (1%)
    pallas_call x1, Pallas kernels, exchange(): pl.pallas_call(functools.partial(exchange_kernel, n_dev, n_local), out_sh...  278 us
    pallas_call x1, Pallas kernels, dispatch(): pl.pallas_call(functools.partial(dispatch_kernel, steps, capacity), grid=...  48.7 us
    pallas_call x1, Pallas kernels, combine(): pl.pallas_call(functools.partial(combine_kernel, fills, n_dev, capacity,...  47.5 us
    pallas_call x1, Pallas kernels, total(): pl.pallas_call(functools.partial(total_kernel, n_dev), out_shape=jax.Shap...  12.2 us
    pallas_call x1, Pallas kernels, route(): pl.pallas_call(functools.partial(route_kernel, capacity), grid=(steps,),...  8.95 us

profile of v5, /device:TPU:0, one launch (start us, length us, event | category | flops | bytes accessed | tf_op | source)
XLA Modules:
  0.0 410.5 jit_solution(14826491540850006931)
XLA Ops:
  0.6 1.4 reshape.48.idx_ref
  2.0 0.8 constant_dynamic-update-slice_fusion.5
  2.8 0.8 constant_dynamic-update-slice_fusion.3
  3.7 0.8 constant_dynamic-update-slice_fusion
  4.5 0.0 copy-start
  4.5 0.7 pad_maximum_fusion.wr_ref
  5.2 8.9 %route.1 = (f32[32,8192]{1,0:T(8,128)}, s32[8,1024]{1,0:T(8,128)}, f32[8,1024]{1,0:T(8,128)}, f32[8,1024]{1,0:T(8,128)}, f32[8,128]{1,0:T(8,128)}) custom-call(bf16[8192,384]{1,0:T(8,128)(2,1)} %x_ref.5, s32[8,1024]{1,0:T(8,128)} %reshape.48.idx_ref, bf16[96,384]{1,0:T(8,128)(2,1)} %pad_maximum_fusion.wr_ref), custom_call_target="tpu_custom_call" | custom-call | tf_op jit(solution)/shard_map/route/pallas_call | solution.py:101
  14.1 48.7 %dispatch.1 = (bf16[16,2,2,320,384]{4,3,2,1,0:T(8,128)(2,1)}, f32[16,8,384]{2,1,0:T(8,128)}) custom-call(s32[8,1024]{1,0:T(8,128)} %get-tuple-element.22.slot_ref, bf16[8192,384]{1,0:T(8,128)(2,1)} %x_ref.5, bf16[8192,384]{1,0:T(8,128)(2,1)} %dy_ref.1, f32[8,1024]{1,0:T(8,128)} %get-tuple-element.23.gate_ref), custom_call_target="tpu_custom_call" | custom-call | tf_op jit(solution)/shard_map/dispatch/pallas_call | solution.py:178
  62.8 0.0 copy-done
  62.8 277.6 %exchange.1 = (f32[2,384,1536]{2,1,0:T(8,128)}, f32[2,384,1536]{2,1,0:T(8,128)}, bf16[16,2,320,384]{3,2,1,0:T(8,128)(2,1)}, f32[16,8,384]{2,1,0:T(8,128)}, f32[8,128]{1,0:T(8,128)}) custom-call(bf16[16,2,2,320,384]{4,3,2,1,0:T(8,128)(2,1)} %get-tuple-element.24.xd_ref, f32[16,8,384]{2,1,0:T(8,128)} %get-tuple-element.25.gate_ref, ...), custom_call_target="tpu_custom_call" | custom-call | tf_op jit(solution)/shard_map/exchange/pallas_call | solution.py:609
  340.4 1.3 slice.30
  342.3 1.4 multiply_reduce_fusion
  344.4 0.7 broadcast_in_dim.2.aux_ref
  345.1 47.5 %combine.1 = (bf16[8192,384]{1,0:T(8,128)(2,1)}, f32[96,384]{1,0:T(8,128)}, f32[768,1536]{1,0:T(8,128)}, f32[2,1536,384]{2,1,0:T(8,128)}) custom-call(s32[8,1024]{1,0:T(8,128)} %get-tuple-element.22.slot_ref, bf16[16,2,320,384]{3,2,1,0:T(8,128)(2,1)} %get-tuple-element.27.back_ref, f32[16,8,384]{2,1,0:T(8,128)} %get-tuple-element.28.g_ref, ...), custom_call_target="tpu_custom_call" | custom-call | tf_op jit(solution)/shard_map/combine/pallas_call | solution.py:277
  392.6 0.9 add_bitcast_fusion
  393.5 0.1 copy.14
  393.6 0.1 reshape.51
  393.7 0.6 pad.4.part_ref
  394.3 12.2 %total.1 = f32[16,8,128]{2,1,0:T(8,128)} custom-call(f32[16,8,128]{2,1,0:T(8,128)} %pad.4.part_ref), custom_call_target="tpu_custom_call" | custom-call | tf_op jit(solution)/shard_map/total/pallas_call | solution.py:355
  406.6 0.9 reshape.52
  407.5 0.7 copy.15
  (3 shorter events, 0.0 us)
Async XLA Ops:
  4.5 58.3 %copy-start = (bf16[192,384]{1,0:T(8,128)(2,1)}, bf16[192,384]{1,0:T(8,128)(2,1)S(1)}, u32[]{:S(2)}) copy-start(bf16[192,384]{1,0:T(8,128)(2,1)S(1)} %get-tuple-element.50.wr_t_ref) | copy-start | bytes 442372

commit v6 on v5

--- a/solution.py
+++ b/solution.py
@@ -12,7 +12,7 @@
 MESH = pl.DeviceIdType.MESH
 F_CHUNK = 512
 TOKEN_BLOCK = 256
-UNROLL = 16
+UNROLL = 32
 ROW_TOKENS = 1024
 GROUP = 2
 
@@ -33,13 +33,6 @@
     return hi, mid, low
 
 
-def split_weights(w):
-    round_bf16 = lambda v: lax.reduce_precision(v, 8, 7)
-    hi = round_bf16(w)
-    mid = round_bf16(w - hi)
-    return hi, mid, w - hi - mid
-
-
 def route_kernel(capacity, x_ref, idx_ref, wr_ref, prob_ref, slot_ref, gate_ref, norm_ref, stat_ref, seen, load, prob_sum, z_sum):
     step = pl.program_id(0)
     num_experts, block = prob_ref.shape
@@ -50,7 +43,7 @@
         prob_sum[...] = jnp.zeros_like(prob_sum)
         z_sum[...] = jnp.zeros_like(z_sum)
 
-    parts = nt_dot(wr_ref[...], x_ref[...])
+    parts = nt_dot(jnp.concatenate(split3(wr_ref[...]), axis=0), x_ref[...])
     logits = parts[:num_experts] + parts[num_experts:2 * num_experts] + parts[2 * num_experts:]
     top = jnp.max(logits, axis=0, keepdims=True)
     shifted = jnp.exp(logits - top)
@@ -74,7 +67,7 @@
         part = chosen[:, i:i + TOKEN_BLOCK]
         count = jnp.dot(part.astype(jnp.bfloat16), upto, preferred_element_type=jnp.float32) + before
         position = jnp.sum(part * count, axis=0, keepdims=True).astype(jnp.int32) - 1
-        slots.append(jnp.where(position < capacity, idx[:, i:i + TOKEN_BLOCK] * capacity + position, num_experts * capacity))
+        slots.append(8 * jnp.where(position < capacity, idx[:, i:i + TOKEN_BLOCK] * capacity + position, num_experts * capacity))
         before = count[:, TOKEN_BLOCK - 1:TOKEN_BLOCK]
     slot_ref[pl.ds(step, 1), :] = jnp.concatenate(slots, axis=1)
     seen[...] = jnp.broadcast_to(before, seen.shape)
@@ -95,7 +88,6 @@
     tokens, d_model = x_tokens.shape
     num_experts = w_router.shape[1]
     steps, block = idx_rows.shape
-    wr = jnp.concatenate(split_weights(w_router.T), axis=0).astype(jnp.bfloat16)
     rows = lambda dtype: jax.ShapeDtypeStruct((steps, block), dtype)
     whole = pl.BlockSpec((steps, block), lambda i: (0, 0))
     return pl.pallas_call(
@@ -104,14 +96,14 @@
         out_shape=(jax.ShapeDtypeStruct((num_experts, tokens), jnp.float32), rows(jnp.int32), rows(jnp.float32), rows(jnp.float32),
                    jax.ShapeDtypeStruct((8, 128), jnp.float32)),
         in_specs=[pl.BlockSpec((block, d_model), lambda i: (i, 0)), whole,
-                  pl.BlockSpec((3 * num_experts, d_model), lambda i: (0, 0))],
+                  pl.BlockSpec((num_experts, d_model), lambda i: (0, 0))],
         out_specs=(pl.BlockSpec((num_experts, block), lambda i: (0, i)), whole, whole, whole,
                    pl.BlockSpec((8, 128), lambda i: (0, 0))),
         scratch_shapes=[pltpu.VMEM((num_experts, 128), jnp.float32), pltpu.VMEM((num_experts, 128), jnp.float32),
                         pltpu.VMEM((num_experts, 128), jnp.float32), pltpu.VMEM((8, 128), jnp.float32)],
         compiler_params=pltpu.CompilerParams(dimension_semantics=('arbitrary',)),
         name='route',
-    )(x_tokens, idx_rows, wr)
+    )(x_tokens, idx_rows, w_router.T)
 
 
 def dispatch_kernel(steps, capacity, slot_ref, x_ref, dy_ref, gate_ref, xd_ref, gates_ref, table, stage):
@@ -142,8 +134,8 @@
         def place(i, carry):
             for u in range(UNROLL):
                 t = i * UNROLL + u
-                slot = slot_ref[step, t]
-                table[pl.ds(pl.multiple_of(slot * 8, 8), 8), :] = stage[pl.ds(pl.multiple_of(t * 8, 8), 8), :]
+                slot = slot_ref[step * block + t]
+                table[pl.ds(pl.multiple_of(slot, 8), 8), :] = stage[pl.ds(pl.multiple_of(t * 8, 8), 8), :]
             return carry
         lax.fori_loop(0, block // UNROLL, place, 0)
 
@@ -170,7 +162,7 @@
 
 def dispatch(slot_rows, x_tokens, grad_y, gate_rows, n_dev, n_local, capacity, lanes):
     tokens, d_model = x_tokens.shape
-    steps, block = slot_rows.shape
+    steps, block = gate_rows.shape
     n_slots = n_dev * n_local * capacity
     table_rows = -(-(n_slots + 1) * 8 // 512) * 512
     tok = lambda i: (jnp.minimum(i, steps - 1), 0)
@@ -231,8 +223,8 @@
         def pick(i, carry):
             for u in range(UNROLL):
                 t = i * UNROLL + u
-                slot = slot_ref[part, t]
-                stage[pl.ds(pl.multiple_of(t * 8, 8), 8), :] = table[pl.ds(pl.multiple_of(slot * 8, 8), 8), :]
+                slot = slot_ref[part * block + t]
+                stage[pl.ds(pl.multiple_of(t * 8, 8), 8), :] = table[pl.ds(pl.multiple_of(slot, 8), 8), :]
             return carry
         lax.fori_loop(0, block // UNROLL, pick, 0)
         eye = eye_mask(128, 128)
@@ -249,7 +241,9 @@
         hi, mid, low = split3(d_logits)
         gwr_ref[...] += jnp.dot(jnp.concatenate([hi, mid, low], axis=0), x_ref[...], preferred_element_type=jnp.float32)
         left = jnp.concatenate([hi, mid, hi, low, mid, hi], axis=0)
-        dx_router = lax.dot_general(left, wr_t_ref[...], (((0,), (0,)), ((), ())), preferred_element_type=jnp.float32)
+        w_hi, w_mid, w_low = split3(wr_t_ref[...])
+        right = jnp.concatenate([w_hi, w_hi, w_mid, w_hi, w_mid, w_low], axis=0)
+        dx_router = lax.dot_general(left, right, (((0,), (0,)), ((), ())), preferred_element_type=jnp.float32)
         for c in range(cols):
             span = slice(c * 128, (c + 1) * 128)
             gx_ref[:, span] = (stage[pl.ds(c, block, stride=8), :] + dx_router[:, span]).astype(jnp.bfloat16)
@@ -260,13 +254,11 @@
     tokens = x_tokens.shape[0]
     num_experts = prob.shape[0]
     d_ff = gw_in.shape[2]
-    blocks, block = slot_rows.shape
+    blocks, block = gate_rows.shape
     fills = n_dev // GROUP
     steps = fills + blocks
     lanes = g_back.shape[2]
     n_slots = n_dev * n_local * capacity
-    w_hi, w_mid, w_low = split_weights(w_router.T)
-    wr_t = jnp.concatenate([w_hi, w_hi, w_mid, w_hi, w_mid, w_low], axis=0).astype(jnp.bfloat16)
     gw_in_rows = gw_in.reshape(n_local * d_model, d_ff)
     in_rows = n_local * d_model // steps
     out_cols = d_ff // 256
@@ -288,7 +280,7 @@
                   pl.BlockSpec((num_experts, block), lambda i: (0, jnp.maximum(i - fills, 0))),
                   rows, rows, rows,
                   pl.BlockSpec((num_experts, 128), lambda i: (0, 0)),
-                  pl.BlockSpec((6 * num_experts, d_model), lambda i: (0, 0)),
+                  pl.BlockSpec((num_experts, d_model), lambda i: (0, 0)),
                   pl.BlockSpec((in_rows, d_ff), lambda i: (i, 0)),
                   pl.BlockSpec((1, d_model, 256), lambda i: (flip(i) // out_cols, 0, flip(i) % out_cols))],
         out_specs=(pl.BlockSpec((block, d_model), tok),
@@ -300,7 +292,7 @@
         compiler_params=pltpu.CompilerParams(dimension_semantics=('arbitrary',), vmem_limit_bytes=63 * 1024 * 1024),
         name='combine',
     )(slot_rows, back, g_back, x_tokens, prob, gate_rows, norm_rows, idx_rows,
-      jnp.broadcast_to(aux_vec[:, None], (num_experts, 128)), wr_t, gw_in_rows, gw_out_t)
+      jnp.broadcast_to(aux_vec[:, None], (num_experts, 128)), w_router.T, gw_in_rows, gw_out_t)
     part = gwr.reshape(3, num_experts, d_model)
     return gx, (part[0] + part[1] + part[2]).T, gw_in_out.reshape(n_local, d_model, d_ff), gw_out
 
@@ -384,9 +376,9 @@
     return pieces
 
 
-def exchange_kernel(n, n_local, xd_ref, gate_ref, stat_ref, w_in_ref, w_out_ref,
-                    gw_in_ref, gw_out_t_ref, back_ref, g_back_ref, stat_out_ref,
-                    xr, gate_r, g_s, stat_r,
+def exchange_kernel(n, n_local, xd_ref, gate_ref, stat_ref, w_in_hbm, w_out_hbm,
+                    gw_in_hbm, gw_out_t_hbm, back_ref, g_back_ref, stat_out_ref,
+                    w_in_ref, w_out_ref, gw_in_ref, gw_out_t_ref, xr, gate_r, g_s, stat_r,
                     fwd_send, fwd_recv, gate_send, gate_recv,
                     ret_send, ret_recv, g_send, g_recv, stat_send, stat_recv, loc_sem):
     me = lax.axis_index('ep')
@@ -472,6 +464,10 @@
     for c in own_in:
         c.start()
     own_gate.start()
+    weights = [pltpu.make_async_copy(w_in_hbm, w_in_ref, loc_sem.at[n_local + 1]),
+               pltpu.make_async_copy(w_out_hbm, w_out_ref, loc_sem.at[n_local + 2])]
+    for c in weights:
+        c.start()
     gw_in_ref[...] = jnp.zeros_like(gw_in_ref)
     gw_out_t_ref[...] = jnp.zeros_like(gw_out_t_ref)
     g_s[...] = jnp.zeros_like(g_s)
@@ -479,6 +475,8 @@
     for c in own_in:
         c.wait()
     own_gate.wait()
+    for c in weights:
+        c.wait()
 
     lanes = gate_r.shape[2]
 
@@ -563,6 +561,10 @@
         return carry
 
     lax.fori_loop(0, len(order), step, 0)
+    totals = [pltpu.make_async_copy(gw_in_ref, gw_in_hbm, loc_sem.at[n_local + 1]),
+              pltpu.make_async_copy(gw_out_t_ref, gw_out_t_hbm, loc_sem.at[n_local + 2])]
+    for c in totals:
+        c.start()
     grads_left(sets[2])
     send_grads(sets[3])
 
@@ -582,6 +584,8 @@
     for c in own_out:
         c.wait()
     own_g.wait()
+    for c in totals:
+        c.wait()
 
     def drain(k, carry):
         gate_copy(k).wait_send()
@@ -613,16 +617,20 @@
                    jax.ShapeDtypeStruct((n_dev, n_local, cap, d_model), jnp.bfloat16),
                    jax.ShapeDtypeStruct((n_dev, 8, lanes), jnp.float32),
                    jax.ShapeDtypeStruct(stats.shape, jnp.float32)),
-        in_specs=[any_spec, any_spec, vmem_spec, vmem_spec, vmem_spec],
-        out_specs=(vmem_spec, vmem_spec, any_spec, any_spec, vmem_spec),
+        in_specs=[any_spec, any_spec, vmem_spec, any_spec, any_spec],
+        out_specs=(any_spec, any_spec, any_spec, any_spec, vmem_spec),
         scratch_shapes=[
+            pltpu.VMEM(w_in.shape, jnp.bfloat16),
+            pltpu.VMEM(w_out.shape, jnp.bfloat16),
+            pltpu.VMEM(w_in.shape, jnp.float32),
+            pltpu.VMEM(w_in.shape, jnp.float32),
             pltpu.VMEM((n_dev, n_local, 2, cap, d_model), jnp.bfloat16),
             pltpu.VMEM((n_dev, 8, lanes), jnp.float32),
             pltpu.VMEM((n_dev, 8, lanes), jnp.float32),
             pltpu.VMEM((n_dev,) + stats.shape, jnp.float32),
             dma((2 * pairs,)), dma((2 * pairs,)), dma((n_dev,)), dma((n_dev,)),
             dma((pairs,)), dma((pairs,)), dma((n_dev,)), dma((n_dev,)),
-            dma((n_dev,)), dma((n_dev,)), dma((n_local + 1,)),
+            dma((n_dev,)), dma((n_dev,)), dma((n_local + 3,)),
         ],
         compiler_params=pltpu.CompilerParams(has_side_effects=True, vmem_limit_bytes=60 * 1024 * 1024),
         name='exchange',
@@ -641,6 +649,7 @@
         lanes = -(-capacity // 128) * 128
         idx_rows = expert_idx.reshape(-1, ROW_TOKENS)
         prob, slot_rows, gate_rows, norm_rows, stats = route(x_tokens, idx_rows, w_router, capacity)
+        slot_rows = slot_rows.reshape(tokens)
         xd, gates = dispatch(slot_rows, x_tokens, grad_y, gate_rows, n_dev, n_local, capacity, lanes)
         gw_in, gw_out_t, back, g_back, stats = exchange(xd, gates, stats, w_in, w_out, n_dev)
 

time: 412 us -> 375 us (0.910)
  Pallas kernels: 395 us -> 361 us
    pallas_call x1, Pallas kernels: 47.5 us -> 32.3 us  [combine(): pl.pallas_call(functools.partial(combine_kernel, fills, n_dev, capacity,...]
    pallas_call x1, Pallas kernels: 48.7 us -> 34.3 us  [dispatch(): pl.pallas_call(functools.partial(dispatch_kernel, steps, capacity), grid=...]
    pallas_call x1, Pallas kernels: 278 us -> 273 us  [exchange(): pl.pallas_call(functools.partial(exchange_kernel, n_dev, n_local), out_sh...]
where the time goes in v6:
time: 375 us; the launch traced here: 374 us
  Pallas kernels  361 us (96%)
  local copies, waits for them, and re-layouts  7.22 us (2%)
  between operations  4.25 us (1%)
    pallas_call x1, Pallas kernels, exchange(): pl.pallas_call(functools.partial(exchange_kernel, n_dev, n_local), out_sh...  273 us
    pallas_call x1, Pallas kernels, dispatch(): pl.pallas_call(functools.partial(dispatch_kernel, steps, capacity), grid=...  34.3 us
    pallas_call x1, Pallas kernels, combine(): pl.pallas_call(functools.partial(combine_kernel, fills, n_dev, capacity,...  32.3 us
    pallas_call x1, Pallas kernels, total(): pl.pallas_call(functools.partial(total_kernel, n_dev), out_shape=jax.Shap...  12.2 us
    pallas_call x1, Pallas kernels, route(): pl.pallas_call(functools.partial(route_kernel, capacity), grid=(steps,),...  8.94 us

profile of v6, /device:TPU:0, one launch (start us, length us, event | category | flops | bytes accessed | tf_op | source)
XLA Modules:
  0.0 374.4 jit_solution(5533432508722847074)
XLA Ops:
  0.6 1.4 reshape.51.idx_ref
  2.0 8.9 %route.1 = (f32[32,8192]{1,0:T(8,128)}, s32[8,1024]{1,0:T(8,128)}, f32[8,1024]{1,0:T(8,128)}, f32[8,1024]{1,0:T(8,128)}, f32[8,128]{1,0:T(8,128)}) custom-call(bf16[8192,384]{1,0:T(8,128)(2,1)} %x_ref.5, s32[8,1024]{1,0:T(8,128)} %reshape.51.idx_ref, f32[32,384]{1,0:T(8,128)} %bitcast.17), custom_call_target="tpu_custom_call" | custom-call | tf_op jit(solution)/shard_map/route/pallas_call | solution.py:93
  11.0 1.4 copy.18
  12.3 34.3 %dispatch.1 = (bf16[16,2,2,320,384]{4,3,2,1,0:T(8,128)(2,1)}, f32[16,8,384]{2,1,0:T(8,128)}) custom-call(s32[8192]{0:T(1024)} %bitcast.14, bf16[8192,384]{1,0:T(8,128)(2,1)} %x_ref.5, bf16[8192,384]{1,0:T(8,128)(2,1)} %dy_ref.1, f32[8,1024]{1,0:T(8,128)} %get-tuple-element.23.gate_ref), custom_call_target="tpu_custom_call" | custom-call | tf_op jit(solution)/shard_map/dispatch/pallas_call | solution.py:170
  46.7 272.9 %exchange.1 = (f32[2,384,1536]{2,1,0:T(8,128)}, f32[2,384,1536]{2,1,0:T(8,128)}, bf16[16,2,320,384]{3,2,1,0:T(8,128)(2,1)}, f32[16,8,384]{2,1,0:T(8,128)}, f32[8,128]{1,0:T(8,128)}) custom-call(bf16[16,2,2,320,384]{4,3,2,1,0:T(8,128)(2,1)} %get-tuple-element.24.xd_ref, f32[16,8,384]{2,1,0:T(8,128)} %get-tuple-element.25.gate_ref, ...), custom_call_target="tpu_custom_call" | custom-call | tf_op jit(solution)/shard_map/exchange/pallas_call | solution.py:613
  319.5 1.3 slice.30
  321.5 1.4 multiply_reduce_fusion
  323.5 0.7 broadcast_in_dim.2.aux_ref
  324.2 32.3 %combine.1 = (bf16[8192,384]{1,0:T(8,128)(2,1)}, f32[96,384]{1,0:T(8,128)}, f32[768,1536]{1,0:T(8,128)}, f32[2,1536,384]{2,1,0:T(8,128)}) custom-call(s32[8192]{0:T(1024)} %bitcast.15, bf16[16,2,320,384]{3,2,1,0:T(8,128)(2,1)} %get-tuple-element.27.back_ref, f32[16,8,384]{2,1,0:T(8,128)} %get-tuple-element.28.g_ref, bf16[8192,384]{1,0:T(8,128)(2,1)} %x_ref.5, ...), custom_call_target="tpu_custom_call" | custom-call | tf_op jit(solution)/shard_map/combine/pallas_call | solution.py:269
  356.5 0.9 add_bitcast_fusion
  357.4 0.1 copy.14
  357.5 0.1 reshape.55
  357.6 0.6 pad.4.part_ref
  358.2 12.2 %total.1 = f32[16,8,128]{2,1,0:T(8,128)} custom-call(f32[16,8,128]{2,1,0:T(8,128)} %pad.4.part_ref), custom_call_target="tpu_custom_call" | custom-call | tf_op jit(solution)/shard_map/total/pallas_call | solution.py:347
  370.4 0.9 reshape.56
  371.4 0.7 copy.15

commit v7 on v6

--- a/solution.py
+++ b/solution.py
@@ -33,7 +33,7 @@
     return hi, mid, low
 
 
-def route_kernel(capacity, x_ref, idx_ref, wr_ref, prob_ref, slot_ref, gate_ref, norm_ref, stat_ref, seen, load, prob_sum, z_sum):
+def route_kernel(capacity, x_ref, idx_ref, wr_ref, prob_ref, slot_ref, pos_ref, gate_ref, norm_ref, stat_ref, seen, prob_sum, z_sum):
     step = pl.program_id(0)
     num_experts, block = prob_ref.shape
 
@@ -63,13 +63,16 @@
                      <= lax.broadcasted_iota(jnp.int32, (TOKEN_BLOCK, TOKEN_BLOCK), 1), 1.0, 0.0).astype(jnp.bfloat16)
     before = seen[:, 0:1]
     slots = []
+    places = []
     for i in range(0, block, TOKEN_BLOCK):
         part = chosen[:, i:i + TOKEN_BLOCK]
         count = jnp.dot(part.astype(jnp.bfloat16), upto, preferred_element_type=jnp.float32) + before
         position = jnp.sum(part * count, axis=0, keepdims=True).astype(jnp.int32) - 1
+        places.append(position)
         slots.append(8 * jnp.where(position < capacity, idx[:, i:i + TOKEN_BLOCK] * capacity + position, num_experts * capacity))
         before = count[:, TOKEN_BLOCK - 1:TOKEN_BLOCK]
     slot_ref[pl.ds(step, 1), :] = jnp.concatenate(slots, axis=1)
+    pos_ref[pl.ds(step, 1), :] = jnp.concatenate(places, axis=1)
     seen[...] = jnp.broadcast_to(before, seen.shape)
 
     @pl.when(step == pl.num_programs(0) - 1)
@@ -93,14 +96,13 @@
     return pl.pallas_call(
         functools.partial(route_kernel, capacity),
         grid=(steps,),
-        out_shape=(jax.ShapeDtypeStruct((num_experts, tokens), jnp.float32), rows(jnp.int32), rows(jnp.float32), rows(jnp.float32),
+        out_shape=(jax.ShapeDtypeStruct((num_experts, tokens), jnp.float32), rows(jnp.int32), rows(jnp.int32), rows(jnp.float32), rows(jnp.float32),
                    jax.ShapeDtypeStruct((8, 128), jnp.float32)),
         in_specs=[pl.BlockSpec((block, d_model), lambda i: (i, 0)), whole,
                   pl.BlockSpec((num_experts, d_model), lambda i: (0, 0))],
-        out_specs=(pl.BlockSpec((num_experts, block), lambda i: (0, i)), whole, whole, whole,
+        out_specs=(pl.BlockSpec((num_experts, block), lambda i: (0, i)), whole, whole, whole, whole,
                    pl.BlockSpec((8, 128), lambda i: (0, 0))),
-        scratch_shapes=[pltpu.VMEM((num_experts, 128), jnp.float32), pltpu.VMEM((num_experts, 128), jnp.float32),
-                        pltpu.VMEM((num_experts, 128), jnp.float32), pltpu.VMEM((8, 128), jnp.float32)],
+        scratch_shapes=[pltpu.VMEM((num_experts, 128), jnp.float32), pltpu.VMEM((num_experts, 128), jnp.float32), pltpu.VMEM((8, 128), jnp.float32)],
         compiler_params=pltpu.CompilerParams(dimension_semantics=('arbitrary',)),
         name='route',
     )(x_tokens, idx_rows, w_router.T)
@@ -185,13 +187,12 @@
     )(slot_rows, x_tokens, grad_y, gate_rows)
 
 
-def combine_kernel(fills, sources, capacity, z_coef, slot_ref, back_ref, g_ref, x_ref, prob_ref, gate_ref, norm_ref, idx_ref, aux_ref,
-                   wr_t_ref, gwi_ref, gwo_t_ref, gx_ref, gwr_ref, gwi_out_ref, gwo_out_ref, table, stage):
+def combine_kernel(fills, sources, capacity, slot_ref, back_ref, dl_ref, wr_t_ref, gwi_ref, gwo_t_ref,
+                   gx_ref, gwi_out_ref, gwo_out_ref, table, stage):
     step = pl.program_id(0)
-    block, d_model = x_ref.shape
+    block, d_model = gx_ref.shape
     cols = d_model // 128
     group, n_local = back_ref.shape[:2]
-    num_experts = prob_ref.shape[0]
     n_slots = sources * n_local * capacity
     gwi_out_ref[...] = gwi_ref[...]
     gwo_out_ref[0] = gwo_t_ref[0].T
@@ -199,20 +200,15 @@
     @pl.when(step == 0)
     def _():
         table[pl.ds(n_slots * 8, 8), :] = jnp.zeros((8, 128), jnp.float32)
-        gwr_ref[...] = jnp.zeros_like(gwr_ref)
 
     @pl.when(step < fills)
     def _():
-        eye = eye_mask(capacity, g_ref.shape[2])
-
         def load(i, carry):
             d = i // n_local
             e = i % n_local
             first = ((step * group + d) * n_local + e) * (capacity * 8)
             for c in range(cols):
                 table[pl.ds(first + c, capacity, stride=8), :] = back_ref[d, e, :, c * 128:(c + 1) * 128].astype(jnp.float32)
-            g_col = jnp.sum(jnp.where(eye, g_ref[d, pl.ds(e, 1), :], 0.0), axis=1, keepdims=True)
-            table[pl.ds(first + cols, capacity, stride=8), :] = jnp.broadcast_to(g_col, (capacity, 128))
             return carry
         lax.fori_loop(0, group * n_local, load, 0)
 
@@ -227,19 +223,7 @@
                 stage[pl.ds(pl.multiple_of(t * 8, 8), 8), :] = table[pl.ds(pl.multiple_of(slot, 8), 8), :]
             return carry
         lax.fori_loop(0, block // UNROLL, pick, 0)
-        eye = eye_mask(128, 128)
-        g_tok = jnp.concatenate([
-            jnp.sum(jnp.where(eye, stage[pl.ds(i * 8 + cols, 128, stride=8), :], 0.0), axis=0, keepdims=True)
-            for i in range(0, block, 128)], axis=1)
-        here = pl.ds(part, 1)
-        prob = prob_ref[...]
-        chosen = jnp.where(lax.broadcasted_iota(jnp.int32, (num_experts, block), 0) == idx_ref[here, :], 1.0, 0.0)
-        aux_vec = aux_ref[:, 0:1]
-        spread = jnp.sum(prob * aux_vec, axis=0, keepdims=True)
-        d_logits = ((gate_ref[here, :] * g_tok) * (chosen - prob) + prob * (aux_vec - spread)
-                    + (z_coef * norm_ref[here, :]) * prob)
-        hi, mid, low = split3(d_logits)
-        gwr_ref[...] += jnp.dot(jnp.concatenate([hi, mid, low], axis=0), x_ref[...], preferred_element_type=jnp.float32)
+        hi, mid, low = split3(dl_ref[...])
         left = jnp.concatenate([hi, mid, hi, low, mid, hi], axis=0)
         w_hi, w_mid, w_low = split3(wr_t_ref[...])
         right = jnp.concatenate([w_hi, w_hi, w_mid, w_hi, w_mid, w_low], axis=0)
@@ -249,15 +233,14 @@
             gx_ref[:, span] = (stage[pl.ds(c, block, stride=8), :] + dx_router[:, span]).astype(jnp.bfloat16)
 
 
-def combine(slot_rows, back, g_back, x_tokens, prob, gate_rows, norm_rows, idx_rows, aux_vec, z_coef, w_router, gw_in, gw_out_t):
+def combine(slot_rows, back, d_logits, w_router, gw_in, gw_out_t):
     n_dev, n_local, capacity, d_model = back.shape
-    tokens = x_tokens.shape[0]
-    num_experts = prob.shape[0]
+    num_experts, tokens = d_logits.shape
     d_ff = gw_in.shape[2]
-    blocks, block = gate_rows.shape
+    block = ROW_TOKENS
+    blocks = tokens // block
     fills = n_dev // GROUP
     steps = fills + blocks
-    lanes = g_back.shape[2]
     n_slots = n_dev * n_local * capacity
     gw_in_rows = gw_in.reshape(n_local * d_model, d_ff)
     in_rows = n_local * d_model // steps
@@ -265,36 +248,27 @@
     src = lambda i: jnp.minimum(i, fills - 1)
     tok = lambda i: (jnp.maximum(i - fills, 0), 0)
     flip = lambda i: jnp.minimum(i, n_local * out_cols - 1)
-    rows = pl.BlockSpec((blocks, block), lambda i: (0, 0))
-    gx, gwr, gw_in_out, gw_out = pl.pallas_call(
-        functools.partial(combine_kernel, fills, n_dev, capacity, z_coef),
+    gx, gw_in_out, gw_out = pl.pallas_call(
+        functools.partial(combine_kernel, fills, n_dev, capacity),
         grid=(steps,),
         out_shape=(jax.ShapeDtypeStruct((tokens, d_model), jnp.bfloat16),
-                   jax.ShapeDtypeStruct((3 * num_experts, d_model), jnp.float32),
                    jax.ShapeDtypeStruct((n_local * d_model, d_ff), jnp.float32),
                    jax.ShapeDtypeStruct((n_local, d_ff, d_model), jnp.float32)),
         in_specs=[pl.BlockSpec(memory_space=pltpu.SMEM),
                   pl.BlockSpec((GROUP, n_local, capacity, d_model), lambda i: (src(i), 0, 0, 0)),
-                  pl.BlockSpec((GROUP, 8, lanes), lambda i: (src(i), 0, 0)),
-                  pl.BlockSpec((block, d_model), tok),
                   pl.BlockSpec((num_experts, block), lambda i: (0, jnp.maximum(i - fills, 0))),
-                  rows, rows, rows,
-                  pl.BlockSpec((num_experts, 128), lambda i: (0, 0)),
                   pl.BlockSpec((num_experts, d_model), lambda i: (0, 0)),
                   pl.BlockSpec((in_rows, d_ff), lambda i: (i, 0)),
                   pl.BlockSpec((1, d_model, 256), lambda i: (flip(i) // out_cols, 0, flip(i) % out_cols))],
         out_specs=(pl.BlockSpec((block, d_model), tok),
-                   pl.BlockSpec((3 * num_experts, d_model), lambda i: (0, 0)),
                    pl.BlockSpec((in_rows, d_ff), lambda i: (i, 0)),
                    pl.BlockSpec((1, 256, d_model), lambda i: (flip(i) // out_cols, flip(i) % out_cols, 0))),
         scratch_shapes=[pltpu.VMEM(((n_slots + 1) * 8, 128), jnp.float32),
                         pltpu.VMEM((block * 8, 128), jnp.float32)],
         compiler_params=pltpu.CompilerParams(dimension_semantics=('arbitrary',), vmem_limit_bytes=63 * 1024 * 1024),
         name='combine',
-    )(slot_rows, back, g_back, x_tokens, prob, gate_rows, norm_rows, idx_rows,
-      jnp.broadcast_to(aux_vec[:, None], (num_experts, 128)), w_router.T, gw_in_rows, gw_out_t)
-    part = gwr.reshape(3, num_experts, d_model)
-    return gx, (part[0] + part[1] + part[2]).T, gw_in_out.reshape(n_local, d_model, d_ff), gw_out
+    )(slot_rows, back, d_logits, w_router.T, gw_in_rows, gw_out_t)
+    return gx, gw_in_out.reshape(n_local, d_model, d_ff), gw_out
 
 
 def flip_bits(me, k, n):
@@ -308,55 +282,6 @@
     return out
 
 
-def total_kernel(n, part_ref, out_ref, inbox, mine, a_send, a_recv, b_send, b_recv):
-    me = lax.axis_index('ep')
-
-    def scatter(k):
-        peer = flip_bits(me, k, n)
-        return pltpu.make_async_remote_copy(src_ref=part_ref.at[peer], dst_ref=inbox.at[me], send_sem=a_send.at[k],
-                                            recv_sem=a_recv.at[k], device_id=(peer,), device_id_type=MESH)
-
-    def spread(k):
-        peer = flip_bits(me, k, n)
-        return pltpu.make_async_remote_copy(src_ref=mine, dst_ref=out_ref.at[me], send_sem=b_send.at[k],
-                                            recv_sem=b_recv.at[k], device_id=(peer,), device_id_type=MESH)
-
-    for k in range(1, n):
-        scatter(k).start()
-    inbox[me] = part_ref[me]
-    for k in range(1, n):
-        scatter(k).wait_recv()
-    total = inbox[0]
-    for i in range(1, n):
-        total = total + inbox[i]
-    mine[...] = total
-    out_ref[me] = total
-    for k in range(1, n):
-        spread(k).start()
-    for k in range(1, n):
-        scatter(k).wait_send()
-        spread(k).wait()
-
-
-def total(part, n_dev):
-    rows, cols = part.shape
-    piece = rows * cols // (n_dev * 128)
-    chunks = jnp.pad(part.reshape(n_dev, piece, 128), ((0, 0), (0, -piece % 8), (0, 0)))
-    dma = pltpu.SemaphoreType.DMA
-    vmem_spec = pl.BlockSpec(memory_space=pltpu.VMEM)
-    out = pl.pallas_call(
-        functools.partial(total_kernel, n_dev),
-        out_shape=jax.ShapeDtypeStruct(chunks.shape, jnp.float32),
-        in_specs=[vmem_spec],
-        out_specs=vmem_spec,
-        scratch_shapes=[pltpu.VMEM(chunks.shape, jnp.float32), pltpu.VMEM(chunks.shape[1:], jnp.float32),
-                        dma((n_dev,)), dma((n_dev,)), dma((n_dev,)), dma((n_dev,))],
-        compiler_params=pltpu.CompilerParams(has_side_effects=True),
-        name='total',
-    )(chunks)
-    return out[:, :piece].reshape(rows, cols)
-
-
 def tile_at(t):
     quarter = t // 4
     edge = (7 - quarter) // 7 + quarter // 7
@@ -376,11 +301,13 @@
     return pieces
 
 
-def exchange_kernel(n, n_local, xd_ref, gate_ref, stat_ref, w_in_hbm, w_out_hbm,
-                    gw_in_hbm, gw_out_t_hbm, back_ref, g_back_ref, stat_out_ref,
-                    w_in_ref, w_out_ref, gw_in_ref, gw_out_t_ref, xr, gate_r, g_s, stat_r,
+def exchange_kernel(n, n_local, total_tok, xd_ref, gate_ref, stat_ref, w_in_hbm, w_out_hbm,
+                    x_hbm, prob_ref, pos_ref, idx_ref, gate_rows_ref, norm_ref,
+                    gw_in_hbm, gw_out_t_hbm, back_ref, dl_ref, gwr_ref, stat_out_ref,
+                    w_in_ref, w_out_ref, gw_in_ref, gw_out_t_ref, x_ref, gwr_acc, gwr_s, gwr_r, gwr_mine,
+                    xr, gate_r, g_s, g_r, stat_r,
                     fwd_send, fwd_recv, gate_send, gate_recv,
-                    ret_send, ret_recv, g_send, g_recv, stat_send, stat_recv, loc_sem):
+                    ret_send, ret_recv, g_send, g_recv, stat_send, stat_recv, a_send, a_recv, b_send, b_recv, loc_sem):
     me = lax.axis_index('ep')
     cap, d_model = xr.shape[3], xr.shape[4]
     d_ff = w_in_ref.shape[2]
@@ -418,8 +345,19 @@
 
     def g_copy(k):
         return pltpu.make_async_remote_copy(
-            src_ref=g_s.at[k], dst_ref=g_back_ref.at[me],
+            src_ref=g_s.at[k], dst_ref=g_r.at[me],
             send_sem=g_send.at[k], recv_sem=g_recv.at[k],
+            device_id=(peer_of(k),), device_id_type=MESH)
+
+    def scatter_copy(k):
+        peer = peer_of(k)
+        return pltpu.make_async_remote_copy(
+            src_ref=gwr_s.at[peer], dst_ref=gwr_r.at[me], send_sem=a_send.at[k], recv_sem=a_recv.at[k],
+            device_id=(peer,), device_id_type=MESH)
+
+    def spread_copy(k):
+        return pltpu.make_async_remote_copy(
+            src_ref=gwr_mine, dst_ref=gwr_ref.at[me], send_sem=b_send.at[k], recv_sem=b_recv.at[k],
             device_id=(peer_of(k),), device_id_type=MESH)
 
     sets = link_sets(n, n_local)
@@ -442,11 +380,9 @@
                 if i < len(queue) - 1:
                     fwd_copy(k, e, 1).wait_send()
 
-    def send_grads(queues):
-        for k, e in interleave(queues):
+    def send_grads(queues, lo=0, hi=None):
+        for k, e in interleave(queues)[lo:hi]:
             ret_copy(k, e).start()
-            if e == n_local - 1:
-                g_copy(k).start()
 
     def grads_left(queues):
         for queue in queues:
@@ -457,7 +393,7 @@
     own_in = [pltpu.make_async_copy(xd_ref.at[me, e], xr.at[0, e], loc_sem.at[e]) for e in range(n_local)]
     own_gate = pltpu.make_async_copy(gate_ref.at[me], gate_r.at[0], loc_sem.at[n_local])
     own_out = [pltpu.make_async_copy(xr.at[0, e, 0], back_ref.at[me, e], loc_sem.at[e]) for e in range(n_local)]
-    own_g = pltpu.make_async_copy(g_s.at[0], g_back_ref.at[me], loc_sem.at[n_local])
+    load_x = pltpu.make_async_copy(x_hbm, x_ref, loc_sem.at[n_local + 3])
 
     send_rows(sets[0])
     send_rows(near)
@@ -468,6 +404,8 @@
                pltpu.make_async_copy(w_out_hbm, w_out_ref, loc_sem.at[n_local + 2])]
     for c in weights:
         c.start()
+    load_x.start()
+    gwr_s[...] = jnp.zeros_like(gwr_s)
     gw_in_ref[...] = jnp.zeros_like(gw_in_ref)
     gw_out_t_ref[...] = jnp.zeros_like(gw_out_t_ref)
     g_s[...] = jnp.zeros_like(g_s)
@@ -520,7 +458,6 @@
         send_grads(near)
         for c in own_out:
             c.start()
-        own_g.start()
 
     def after_rows(done, then):
         def run():
@@ -541,7 +478,7 @@
         first[2]: after_grads(0, lambda: send_rows(sets[2])),
         first[3] - 2: after_rows(2, lambda: send_grads(sets[1])),
         first[3]: after_grads(1, lambda: send_rows(sets[3])),
-        len(order) - 1: after_rows(3, lambda: send_grads(sets[2])),
+        len(order) - 1: after_rows(3, lambda: send_grads(sets[2], 0, 4)),
     }
 
     def step(t, carry):
@@ -558,15 +495,88 @@
                 fwd_copy(k, e, part).wait_recv()
 
         tile(k, e)
+
+        @pl.when(t >= n_local)
+        def _():
+            @pl.when(e == n_local - 1)
+            def _():
+                g_copy(k).start()
         return carry
 
     lax.fori_loop(0, len(order), step, 0)
+    send_grads(sets[2], 4)
     totals = [pltpu.make_async_copy(gw_in_ref, gw_in_hbm, loc_sem.at[n_local + 1]),
               pltpu.make_async_copy(gw_out_t_ref, gw_out_t_hbm, loc_sem.at[n_local + 2])]
     for c in totals:
         c.start()
+    load_x.wait()
+    g_r[me] = g_s[0]
     grads_left(sets[2])
-    send_grads(sets[3])
+    send_grads(sets[3], 0, 2)
+
+    def arrive(k, carry):
+        stat_copy(k).wait()
+        g_copy(k).wait()
+        return carry
+
+    lax.fori_loop(1, n, arrive, 0)
+    stat = stat_r[0]
+    for i in range(1, n):
+        stat = stat + stat_r[i]
+    stat_out_ref[...] = stat
+    num_experts = n * n_local
+    load = jnp.sum(jnp.where(eye_mask(num_experts, 128), stat[0:1, :], 0.0), axis=1, keepdims=True)
+    aux_vec = (AUX_WEIGHT * num_experts / total_tok) * (load / total_tok)
+    g_all = jnp.concatenate([g_r[d, 0:n_local, :] for d in range(n)], axis=0)
+    g_parts = jnp.concatenate(split3(g_all), axis=0)
+    span = pos_ref.shape[1]
+    gwr_acc[...] = jnp.zeros_like(gwr_acc)
+
+    def router(c, carry):
+        here = pl.ds(c, 1)
+        cols = pl.ds(pl.multiple_of(c * span, span), span)
+        place = jnp.where(lax.broadcasted_iota(jnp.int32, (lanes, span), 0) == pos_ref[here, :], 1.0, 0.0)
+        found = jnp.dot(g_parts, place.astype(jnp.bfloat16), preferred_element_type=jnp.float32)
+        found = found[:num_experts] + found[num_experts:2 * num_experts] + found[2 * num_experts:]
+        chosen = jnp.where(lax.broadcasted_iota(jnp.int32, (num_experts, span), 0) == idx_ref[here, :], 1.0, 0.0)
+        g_tok = jnp.sum(found * chosen, axis=0, keepdims=True)
+        prob = prob_ref[:, cols]
+        spread = jnp.sum(prob * aux_vec, axis=0, keepdims=True)
+        d_logits = ((gate_rows_ref[here, :] * g_tok) * (chosen - prob) + prob * (aux_vec - spread)
+                    + ((2.0 * Z_WEIGHT / total_tok) * norm_ref[here, :]) * prob)
+        dl_ref[:, cols] = d_logits
+        gwr_acc[...] += jnp.dot(jnp.concatenate(split3(d_logits), axis=0), x_ref[cols, :], preferred_element_type=jnp.float32)
+        return carry
+
+    lax.fori_loop(0, pos_ref.shape[0], router, 0)
+    part = gwr_acc[0:num_experts, :] + gwr_acc[num_experts:2 * num_experts, :] + gwr_acc[2 * num_experts:, :]
+    for d in range(n):
+        gwr_s[d, 0:n_local, :] = part[d * n_local:(d + 1) * n_local]
+    gwr_r[me] = gwr_s[me]
+
+    def scatter(k, carry):
+        scatter_copy(k).start()
+        return carry
+
+    lax.fori_loop(1, n, scatter, 0)
+    send_grads(sets[3], 2)
+
+    def gathered(k, carry):
+        scatter_copy(k).wait()
+        return carry
+
+    lax.fori_loop(1, n, gathered, 0)
+    mine = gwr_r[0]
+    for i in range(1, n):
+        mine = mine + gwr_r[i]
+    gwr_mine[...] = mine
+    gwr_ref[me] = mine
+
+    def spread_all(k, carry):
+        spread_copy(k).start()
+        return carry
+
+    lax.fori_loop(1, n, spread_all, 0)
 
     for queues in sets:
         for queue in queues:
@@ -583,26 +593,20 @@
         ret_copy(k, e).wait_send()
     for c in own_out:
         c.wait()
-    own_g.wait()
     for c in totals:
         c.wait()
 
     def drain(k, carry):
         gate_copy(k).wait_send()
-        stat_copy(k).wait()
-        g_copy(k).wait()
+        spread_copy(k).wait()
         for e in range(n_local):
             ret_copy(k, e).wait_recv()
         return carry
 
     lax.fori_loop(1, n, drain, 0)
-    stat = stat_r[0]
-    for i in range(1, n):
-        stat = stat + stat_r[i]
-    stat_out_ref[...] = stat
-
-
-def exchange(xd, gates, stats, w_in, w_out, n_dev):
+
+
+def exchange(xd, gates, stats, w_in, w_out, x_tokens, prob, pos_rows, idx_rows, gate_rows, norm_rows, n_dev):
     n_local, d_model, d_ff = w_in.shape
     cap = xd.shape[3]
     lanes = gates.shape[2]
@@ -611,30 +615,38 @@
     pairs = n_dev * n_local
     dma = pltpu.SemaphoreType.DMA
     return pl.pallas_call(
-        functools.partial(exchange_kernel, n_dev, n_local),
+        functools.partial(exchange_kernel, n_dev, n_local, x_tokens.shape[0] * n_dev),
         out_shape=(jax.ShapeDtypeStruct((n_local, d_model, d_ff), jnp.float32),
                    jax.ShapeDtypeStruct((n_local, d_model, d_ff), jnp.float32),
                    jax.ShapeDtypeStruct((n_dev, n_local, cap, d_model), jnp.bfloat16),
-                   jax.ShapeDtypeStruct((n_dev, 8, lanes), jnp.float32),
+                   jax.ShapeDtypeStruct(prob.shape, jnp.float32),
+                   jax.ShapeDtypeStruct((n_dev, 8, d_model), jnp.float32),
                    jax.ShapeDtypeStruct(stats.shape, jnp.float32)),
-        in_specs=[any_spec, any_spec, vmem_spec, any_spec, any_spec],
-        out_specs=(any_spec, any_spec, any_spec, any_spec, vmem_spec),
+        in_specs=[any_spec, any_spec, vmem_spec, any_spec, any_spec, any_spec] + [vmem_spec] * 5,
+        out_specs=(any_spec, any_spec, any_spec, vmem_spec, vmem_spec, vmem_spec),
         scratch_shapes=[
             pltpu.VMEM(w_in.shape, jnp.bfloat16),
             pltpu.VMEM(w_out.shape, jnp.bfloat16),
             pltpu.VMEM(w_in.shape, jnp.float32),
             pltpu.VMEM(w_in.shape, jnp.float32),
+            pltpu.VMEM(x_tokens.shape, jnp.bfloat16),
+            pltpu.VMEM((3 * pairs, d_model), jnp.float32),
+            pltpu.VMEM((n_dev, 8, d_model), jnp.float32),
+            pltpu.VMEM((n_dev, 8, d_model), jnp.float32),
+            pltpu.VMEM((8, d_model), jnp.float32),
             pltpu.VMEM((n_dev, n_local, 2, cap, d_model), jnp.bfloat16),
+            pltpu.VMEM((n_dev, 8, lanes), jnp.float32),
             pltpu.VMEM((n_dev, 8, lanes), jnp.float32),
             pltpu.VMEM((n_dev, 8, lanes), jnp.float32),
             pltpu.VMEM((n_dev,) + stats.shape, jnp.float32),
             dma((2 * pairs,)), dma((2 * pairs,)), dma((n_dev,)), dma((n_dev,)),
             dma((pairs,)), dma((pairs,)), dma((n_dev,)), dma((n_dev,)),
-            dma((n_dev,)), dma((n_dev,)), dma((n_local + 3,)),
+            dma((n_dev,)), dma((n_dev,)), dma((n_dev,)), dma((n_dev,)), dma((n_dev,)), dma((n_dev,)),
+            dma((n_local + 4,)),
         ],
         compiler_params=pltpu.CompilerParams(has_side_effects=True, vmem_limit_bytes=60 * 1024 * 1024),
         name='exchange',
-    )(xd, gates, stats, w_in, w_out)
+    )(xd, gates, stats, w_in, w_out, x_tokens, prob, pos_rows, idx_rows, gate_rows, norm_rows)
 
 
 def solution(mesh):
@@ -648,19 +660,18 @@
         total_tok = tokens * n_dev
         lanes = -(-capacity // 128) * 128
         idx_rows = expert_idx.reshape(-1, ROW_TOKENS)
-        prob, slot_rows, gate_rows, norm_rows, stats = route(x_tokens, idx_rows, w_router, capacity)
+        prob, slot_rows, pos_rows, gate_rows, norm_rows, stats = route(x_tokens, idx_rows, w_router, capacity)
         slot_rows = slot_rows.reshape(tokens)
         xd, gates = dispatch(slot_rows, x_tokens, grad_y, gate_rows, n_dev, n_local, capacity, lanes)
-        gw_in, gw_out_t, back, g_back, stats = exchange(xd, gates, stats, w_in, w_out, n_dev)
+        gw_in, gw_out_t, back, d_logits, gwr, stats = exchange(xd, gates, stats, w_in, w_out, x_tokens, prob, pos_rows, idx_rows,
+                                                               gate_rows, norm_rows, n_dev)
+        grad_x, grad_w_in, grad_w_out = combine(slot_rows, back, d_logits, w_router, gw_in, gw_out_t)
+        grad_w_router = gwr[:, :n_local].reshape(num_experts, d_model).T
 
         load_frac = stats[0, :num_experts] / total_tok
         mean_prob = stats[0, num_experts:2 * num_experts] / total_tok
         aux_loss = AUX_WEIGHT * num_experts * jnp.sum(load_frac * mean_prob)
         z_loss = Z_WEIGHT * stats[0, 2 * num_experts] / total_tok
-        aux_vec = AUX_WEIGHT * num_experts * load_frac / total_tok
-        grad_x, part, grad_w_in, grad_w_out = combine(slot_rows, back, g_back, x_tokens, prob, gate_rows, norm_rows, idx_rows, aux_vec,
-                                                      2.0 * Z_WEIGHT / total_tok, w_router, gw_in, gw_out_t)
-        grad_w_router = total(part, n_dev)
         return grad_x, grad_w_in, grad_w_out, grad_w_router, aux_loss, z_loss
 
     return jax.shard_map(expert_layer, mesh=mesh,

time: 375 us -> 365 us (0.973)
  Pallas kernels: 361 us -> 352 us
    pallas_call x3 -> x2, Pallas kernels: 317 us -> 309 us  [the longest x1 281 us: exchange(): pl.pallas_call(functools.partial(exchange_kernel, n_dev, n_local, x_token...]
where the time goes in v7:
time: 365 us; the launch traced here: 364 us
  Pallas kernels  352 us (96%)
  local copies, waits for them, and re-layouts  5.61 us (2%)
  between operations  4.21 us (1%)
    pallas_call x1, Pallas kernels, exchange(): pl.pallas_call(functools.partial(exchange_kernel, n_dev, n_local, x_token...  281 us
    pallas_call x1, Pallas kernels, dispatch(): pl.pallas_call(functools.partial(dispatch_kernel, steps, capacity), grid=...  34.3 us
    pallas_call x1, Pallas kernels, combine(): pl.pallas_call(functools.partial(combine_kernel, fills, n_dev, capacity),...  27.8 us
    pallas_call x1, Pallas kernels, route(): pl.pallas_call(functools.partial(route_kernel, capacity), grid=(steps,),...  8.95 us

profile of v7, /device:TPU:0, one launch (start us, length us, event | category | flops | bytes accessed | tf_op | source)
XLA Modules:
  0.0 363.8 jit_solution(13671988354616759928)
XLA Ops:
  0.6 1.4 reshape.34.idx_ref
  2.0 8.9 %route.1 = (f32[32,8192]{1,0:T(8,128)}, s32[8,1024]{1,0:T(8,128)}, s32[8,1024]{1,0:T(8,128)}, f32[8,1024]{1,0:T(8,128)}, f32[8,1024]{1,0:T(8,128)}, /*index=5*/f32[8,128]{1,0:T(8,128)}) custom-call(bf16[8192,384]{1,0:T(8,128)(2,1)} %x_hbm.1, s32[8,1024]{1,0:T(8,128)} %reshape.34.idx_ref, f32[32,384]{1,0:T(8,128)} %bitcast.12), custom_call_target="tpu_custom_call" | custom-call | tf_op jit(solution)/shard_map/route/pallas_call | solution.py:96
  11.0 1.4 copy.14
  12.3 34.3 %dispatch.1 = (bf16[16,2,2,320,384]{4,3,2,1,0:T(8,128)(2,1)}, f32[16,8,384]{2,1,0:T(8,128)}) custom-call(s32[8192]{0:T(1024)} %bitcast.10, bf16[8192,384]{1,0:T(8,128)(2,1)} %x_hbm.1, bf16[8192,384]{1,0:T(8,128)(2,1)} %dy_ref.1, f32[8,1024]{1,0:T(8,128)} %get-tuple-element.24.gate_ref.gate_rows_ref), custom_call_target="tpu_custom_call" | custom-call | tf_op jit(solution)/shard_map/dispatch/pallas_call | solution.py:172
  46.7 281.4 %exchange.1 = (f32[2,384,1536]{2,1,0:T(8,128)}, f32[2,384,1536]{2,1,0:T(8,128)}, bf16[16,2,320,384]{3,2,1,0:T(8,128)(2,1)}, f32[32,8192]{1,0:T(8,128)}, f32[16,8,384]{2,1,0:T(8,128)}, /*index=5*/f32[8,128]{1,0:T(8,128)}) custom-call(bf16[16,2,2,320,384]{4,3,2,1,0:T(8,128)(2,1)} %get-tuple-element.25.xd_ref, f32[16,8,384]{2,1,0:T(8,128)} %get-tuple-element.26.gate_ref, ...), custom_call_target="tpu_custom_call" | custom-call | tf_op jit(solution)/shard_map/exchange/pallas_call | solution.py:617
  328.1 1.4 multiply_reduce_fusion
  330.2 1.3 slice.15
  332.1 27.8 %combine.1 = (bf16[8192,384]{1,0:T(8,128)(2,1)}, f32[768,1536]{1,0:T(8,128)}, f32[2,1536,384]{2,1,0:T(8,128)}) custom-call(s32[8192]{0:T(1024)} %bitcast.11, bf16[16,2,320,384]{3,2,1,0:T(8,128)(2,1)} %get-tuple-element.31.back_ref, f32[32,8192]{1,0:T(8,128)} %get-tuple-element.32.dl_ref, f32[32,384]{1,0:T(8,128)} %bitcast.13, f32[768,1536]{1,0:T(8,128)} %bitcast.9, ...), custom_call_target="tpu_custom_call" | custom-call | tf_op jit(solution)/shard_map/combine/pallas_call | solution.py:251
  359.9 0.9 slice.12
  360.8 0.7 reshape.38

commit v8 on v7

--- a/solution.py
+++ b/solution.py
@@ -13,6 +13,7 @@
 F_CHUNK = 512
 TOKEN_BLOCK = 256
 UNROLL = 32
+ROW_GROUP = 32
 ROW_TOKENS = 1024
 GROUP = 2
 
@@ -124,9 +125,11 @@
 
     @pl.when(step < steps)
     def _():
-        for c in range(cols):
-            stage[pl.ds(c, block, stride=8), :] = x_ref[:, c * 128:(c + 1) * 128].astype(jnp.float32)
-            stage[pl.ds(cols + c, block, stride=8), :] = dy_ref[:, c * 128:(c + 1) * 128].astype(jnp.float32)
+        for r in range(0, block, ROW_GROUP):
+            for c in range(2 * cols):
+                rows_ref = x_ref if c < cols else dy_ref
+                span = slice(c % cols * 128, (c % cols + 1) * 128)
+                stage[pl.ds(r * 8 + c, ROW_GROUP, stride=8), :] = rows_ref[r:r + ROW_GROUP, span].astype(jnp.float32)
         eye = eye_mask(128, 128)
         gate_row = gate_ref[pl.ds(step, 1), :]
         for i in range(0, block, 128):
@@ -151,9 +154,11 @@
             d = i // n_local
             e = i % n_local
             first = (((step - steps) * group + d) * n_local + e) * (capacity * 8)
-            for c in range(cols):
-                xd_ref[d, e, 0, :, c * 128:(c + 1) * 128] = table[pl.ds(first + c, capacity, stride=8), :].astype(jnp.bfloat16)
-                xd_ref[d, e, 1, :, c * 128:(c + 1) * 128] = table[pl.ds(first + cols + c, capacity, stride=8), :].astype(jnp.bfloat16)
+            for r in range(0, capacity, ROW_GROUP):
+                for c in range(2 * cols):
+                    span = slice(c % cols * 128, (c % cols + 1) * 128)
+                    xd_ref[d, e, c // cols, r:r + ROW_GROUP, span] = table[
+                        pl.ds(first + r * 8 + c, ROW_GROUP, stride=8), :].astype(jnp.bfloat16)
             gate = table[pl.ds(first + 2 * cols, capacity, stride=8), :]
             gates_ref[d, pl.ds(e, 1), :] = jnp.concatenate([
                 jnp.sum(jnp.where(row == lane + c * 128, gate, 0.0), axis=0, keepdims=True)
@@ -207,8 +212,10 @@
             d = i // n_local
             e = i % n_local
             first = ((step * group + d) * n_local + e) * (capacity * 8)
-            for c in range(cols):
-                table[pl.ds(first + c, capacity, stride=8), :] = back_ref[d, e, :, c * 128:(c + 1) * 128].astype(jnp.float32)
+            for r in range(0, capacity, ROW_GROUP):
+                for c in range(cols):
+                    table[pl.ds(first + r * 8 + c, ROW_GROUP, stride=8), :] = back_ref[
+                        d, e, r:r + ROW_GROUP, c * 128:(c + 1) * 128].astype(jnp.float32)
             return carry
         lax.fori_loop(0, group * n_local, load, 0)
 
@@ -228,9 +235,11 @@
         w_hi, w_mid, w_low = split3(wr_t_ref[...])
         right = jnp.concatenate([w_hi, w_hi, w_mid, w_hi, w_mid, w_low], axis=0)
         dx_router = lax.dot_general(left, right, (((0,), (0,)), ((), ())), preferred_element_type=jnp.float32)
-        for c in range(cols):
-            span = slice(c * 128, (c + 1) * 128)
-            gx_ref[:, span] = (stage[pl.ds(c, block, stride=8), :] + dx_router[:, span]).astype(jnp.bfloat16)
+        for r in range(0, block, ROW_GROUP):
+            for c in range(cols):
+                span = slice(c * 128, (c + 1) * 128)
+                gx_ref[r:r + ROW_GROUP, span] = (stage[pl.ds(r * 8 + c, ROW_GROUP, stride=8), :]
+                                                 + dx_router[r:r + ROW_GROUP, span]).astype(jnp.bfloat16)
 
 
 def combine(slot_rows, back, d_logits, w_router, gw_in, gw_out_t):
@@ -559,7 +568,7 @@
         return carry
 
     lax.fori_loop(1, n, scatter, 0)
-    send_grads(sets[3], 2)
+    send_grads(sets[3], 2, 3)
 
     def gathered(k, carry):
         scatter_copy(k).wait()
@@ -577,6 +586,7 @@
         return carry
 
     lax.fori_loop(1, n, spread_all, 0)
+    send_grads(sets[3], 3)
 
     for queues in sets:
         for queue in queues:

time: 365 us -> 360 us (0.986)
  Pallas kernels: 352 us -> 348 us
    pallas_call x1, Pallas kernels: 34.3 us -> 30.6 us  [dispatch(): pl.pallas_call(functools.partial(dispatch_kernel, steps, capacity), grid=...]
where the time goes in v8:
time: 360 us; the launch traced here: 359 us
  Pallas kernels  348 us (97%)
  local copies, waits for them, and re-layouts  5.61 us (2%)
  between operations  4.21 us (1%)
    pallas_call x1, Pallas kernels, exchange(): pl.pallas_call(functools.partial(exchange_kernel, n_dev, n_local, x_token...  281 us
    pallas_call x1, Pallas kernels, dispatch(): pl.pallas_call(functools.partial(dispatch_kernel, steps, capacity), grid=...  30.6 us
    pallas_call x1, Pallas kernels, combine(): pl.pallas_call(functools.partial(combine_kernel, fills, n_dev, capacity),...  27.8 us
    pallas_call x1, Pallas kernels, route(): pl.pallas_call(functools.partial(route_kernel, capacity), grid=(steps,),...  8.95 us

profile of v8, /device:TPU:0, one launch (start us, length us, event | category | flops | bytes accessed | tf_op | source)
XLA Modules:
  0.0 359.5 jit_solution(11521593577527959133)
XLA Ops:
  0.6 1.4 reshape.34.idx_ref
  2.0 8.9 %route.1 = (f32[32,8192]{1,0:T(8,128)}, s32[8,1024]{1,0:T(8,128)}, s32[8,1024]{1,0:T(8,128)}, f32[8,1024]{1,0:T(8,128)}, f32[8,1024]{1,0:T(8,128)}, /*index=5*/f32[8,128]{1,0:T(8,128)}) custom-call(bf16[8192,384]{1,0:T(8,128)(2,1)} %x_hbm.1, s32[8,1024]{1,0:T(8,128)} %reshape.34.idx_ref, f32[32,384]{1,0:T(8,128)} %bitcast.12), custom_call_target="tpu_custom_call" | custom-call | tf_op jit(solution)/shard_map/route/pallas_call | solution.py:97
  11.0 1.4 copy.14
  12.3 30.6 %dispatch.1 = (bf16[16,2,2,320,384]{4,3,2,1,0:T(8,128)(2,1)}, f32[16,8,384]{2,1,0:T(8,128)}) custom-call(s32[8192]{0:T(1024)} %bitcast.10, bf16[8192,384]{1,0:T(8,128)(2,1)} %x_hbm.1, bf16[8192,384]{1,0:T(8,128)(2,1)} %dy_ref.1, f32[8,1024]{1,0:T(8,128)} %get-tuple-element.24.gate_ref.gate_rows_ref), custom_call_target="tpu_custom_call" | custom-call | tf_op jit(solution)/shard_map/dispatch/pallas_call | solution.py:177
  42.9 280.9 %exchange.1 = (f32[2,384,1536]{2,1,0:T(8,128)}, f32[2,384,1536]{2,1,0:T(8,128)}, bf16[16,2,320,384]{3,2,1,0:T(8,128)(2,1)}, f32[32,8192]{1,0:T(8,128)}, f32[16,8,384]{2,1,0:T(8,128)}, /*index=5*/f32[8,128]{1,0:T(8,128)}) custom-call(bf16[16,2,2,320,384]{4,3,2,1,0:T(8,128)(2,1)} %get-tuple-element.25.xd_ref, f32[16,8,384]{2,1,0:T(8,128)} %get-tuple-element.26.gate_ref, ...), custom_call_target="tpu_custom_call" | custom-call | tf_op jit(solution)/shard_map/exchange/pallas_call | solution.py:627
  323.8 1.4 multiply_reduce_fusion
  325.9 1.3 slice.15
  327.8 27.8 %combine.1 = (bf16[8192,384]{1,0:T(8,128)(2,1)}, f32[768,1536]{1,0:T(8,128)}, f32[2,1536,384]{2,1,0:T(8,128)}) custom-call(s32[8192]{0:T(1024)} %bitcast.11, bf16[16,2,320,384]{3,2,1,0:T(8,128)(2,1)} %get-tuple-element.31.back_ref, f32[32,8192]{1,0:T(8,128)} %get-tuple-element.32.dl_ref, f32[32,384]{1,0:T(8,128)} %bitcast.13, f32[768,1536]{1,0:T(8,128)} %bitcast.9, ...), custom_call_target="tpu_custom_call" | custom-call | tf_op jit(solution)/shard_map/combine/pallas_call | solution.py:260
  355.6 0.9 slice.12
  356.6 0.7 reshape.38

commit v9 on v8

--- a/solution.py
+++ b/solution.py
@@ -109,11 +109,10 @@
     )(x_tokens, idx_rows, w_router.T)
 
 
-def dispatch_kernel(steps, capacity, slot_ref, x_ref, dy_ref, gate_ref, xd_ref, gates_ref, table, stage):
+def dispatch_kernel(steps, capacity, lane_cols, slot_ref, x_ref, dy_ref, gate_ref, xd_ref, gates_ref, table, stage):
     step = pl.program_id(0)
     block, d_model = x_ref.shape
     cols = d_model // 128
-    lanes = gates_ref.shape[2]
     group, n_local = xd_ref.shape[:2]
 
     @pl.when(step == 0)
@@ -160,9 +159,9 @@
                     xd_ref[d, e, c // cols, r:r + ROW_GROUP, span] = table[
                         pl.ds(first + r * 8 + c, ROW_GROUP, stride=8), :].astype(jnp.bfloat16)
             gate = table[pl.ds(first + 2 * cols, capacity, stride=8), :]
-            gates_ref[d, pl.ds(e, 1), :] = jnp.concatenate([
-                jnp.sum(jnp.where(row == lane + c * 128, gate, 0.0), axis=0, keepdims=True)
-                for c in range(lanes // 128)], axis=1)
+            for c in range(lane_cols):
+                gates_ref[d, pl.ds(e * lane_cols + c, 1), :] = jnp.sum(
+                    jnp.where(row == lane + c * 128, gate, 0.0), axis=0, keepdims=True)
             return carry
         lax.fori_loop(0, group * n_local, unload, 0)
 
@@ -175,16 +174,16 @@
     tok = lambda i: (jnp.minimum(i, steps - 1), 0)
     dst = lambda i: jnp.maximum(i - steps, 0)
     return pl.pallas_call(
-        functools.partial(dispatch_kernel, steps, capacity),
+        functools.partial(dispatch_kernel, steps, capacity, lanes // 128),
         grid=(steps + n_dev // GROUP,),
         out_shape=(jax.ShapeDtypeStruct((n_dev, n_local, 2, capacity, d_model), jnp.bfloat16),
-                   jax.ShapeDtypeStruct((n_dev, 8, lanes), jnp.float32)),
+                   jax.ShapeDtypeStruct((n_dev, 8, 128), jnp.float32)),
         in_specs=[pl.BlockSpec(memory_space=pltpu.SMEM),
                   pl.BlockSpec((block, d_model), tok),
                   pl.BlockSpec((block, d_model), tok),
                   pl.BlockSpec((steps, block), lambda i: (0, 0))],
         out_specs=(pl.BlockSpec((GROUP, n_local, 2, capacity, d_model), lambda i: (dst(i), 0, 0, 0, 0)),
-                   pl.BlockSpec((GROUP, 8, lanes), lambda i: (dst(i), 0, 0))),
+                   pl.BlockSpec((GROUP, 8, 128), lambda i: (dst(i), 0, 0))),
         scratch_shapes=[pltpu.VMEM((table_rows, 128), jnp.float32),
                         pltpu.VMEM((block * 8, 128), jnp.float32)],
         compiler_params=pltpu.CompilerParams(dimension_semantics=('arbitrary',), vmem_limit_bytes=62 * 1024 * 1024),
@@ -425,14 +424,15 @@
     for c in weights:
         c.wait()
 
-    lanes = gate_r.shape[2]
+    lane_cols = -(-cap // 128)
+    lanes = lane_cols * 128
 
     def tile(k, e):
         eye = (lax.broadcasted_iota(jnp.int32, (cap, lanes), 0)
                == lax.broadcasted_iota(jnp.int32, (cap, lanes), 1))
         rows = xr[k, e, 0]
         dy = xr[k, e, 1].astype(jnp.float32)
-        gate_row = gate_r[k, pl.ds(e, 1), :]
+        gate_row = jnp.concatenate([gate_r[k, pl.ds(e * lane_cols + c, 1), :] for c in range(lane_cols)], axis=1)
         gate_col = jnp.sum(jnp.where(eye, gate_row, 0.0), axis=1, keepdims=True)
         grad = (gate_col * dy).astype(jnp.bfloat16)
         rows_t = rows.T
@@ -453,7 +453,9 @@
             d_rows = d_rows + nt_dot(d_pre, w_a)
         out = out.astype(jnp.bfloat16).astype(jnp.float32)
         g_col = jnp.sum(out * dy, axis=1, keepdims=True)
-        g_s[k, pl.ds(e, 1), :] = jnp.sum(jnp.where(eye, g_col, 0.0), axis=0, keepdims=True)
+        g_row = jnp.sum(jnp.where(eye, g_col, 0.0), axis=0, keepdims=True)
+        for c in range(lane_cols):
+            g_s[k, pl.ds(e * lane_cols + c, 1), :] = g_row[:, c * 128:(c + 1) * 128]
         xr[k, e, 0] = d_rows.astype(jnp.bfloat16)
 
     order = [(0, e) for e in range(n_local)] + near[0]
@@ -536,7 +538,8 @@
     num_experts = n * n_local
     load = jnp.sum(jnp.where(eye_mask(num_experts, 128), stat[0:1, :], 0.0), axis=1, keepdims=True)
     aux_vec = (AUX_WEIGHT * num_experts / total_tok) * (load / total_tok)
-    g_all = jnp.concatenate([g_r[d, 0:n_local, :] for d in range(n)], axis=0)
+    g_all = jnp.concatenate([
+        jnp.concatenate([g_r[:, e * lane_cols + c, :] for c in range(lane_cols)], axis=1) for e in range(n_local)], axis=0)
     g_parts = jnp.concatenate(split3(g_all), axis=0)
     span = pos_ref.shape[1]
     gwr_acc[...] = jnp.zeros_like(gwr_acc)
@@ -548,7 +551,9 @@
         found = jnp.dot(g_parts, place.astype(jnp.bfloat16), preferred_element_type=jnp.float32)
         found = found[:num_experts] + found[num_experts:2 * num_experts] + found[2 * num_experts:]
         chosen = jnp.where(lax.broadcasted_iota(jnp.int32, (num_experts, span), 0) == idx_ref[here, :], 1.0, 0.0)
-        g_tok = jnp.sum(found * chosen, axis=0, keepdims=True)
+        row = lax.broadcasted_iota(jnp.int32, (num_experts, span), 0)
+        owner = jnp.where(row < n, row * n_local, (row - n) * n_local + 1)
+        g_tok = jnp.sum(jnp.where(owner == idx_ref[here, :], found, 0.0), axis=0, keepdims=True)
         prob = prob_ref[:, cols]
         spread = jnp.sum(prob * aux_vec, axis=0, keepdims=True)
         d_logits = ((gate_rows_ref[here, :] * g_tok) * (chosen - prob) + prob * (aux_vec - spread)
@@ -559,8 +564,11 @@
 
     lax.fori_loop(0, pos_ref.shape[0], router, 0)
     part = gwr_acc[0:num_experts, :] + gwr_acc[num_experts:2 * num_experts, :] + gwr_acc[2 * num_experts:, :]
+    d_cols = d_model // 128
     for d in range(n):
-        gwr_s[d, 0:n_local, :] = part[d * n_local:(d + 1) * n_local]
+        for c in range(n_local * d_cols):
+            r = d * n_local + c // d_cols
+            gwr_s[d, c:c + 1, :] = part[r:r + 1, c % d_cols * 128:(c % d_cols + 1) * 128]
     gwr_r[me] = gwr_s[me]
 
     def scatter(k, carry):
@@ -619,7 +627,6 @@
 def exchange(xd, gates, stats, w_in, w_out, x_tokens, prob, pos_rows, idx_rows, gate_rows, norm_rows, n_dev):
     n_local, d_model, d_ff = w_in.shape
     cap = xd.shape[3]
-    lanes = gates.shape[2]
     any_spec = pl.BlockSpec(memory_space=pl.ANY)
     vmem_spec = pl.BlockSpec(memory_space=pltpu.VMEM)
     pairs = n_dev * n_local
@@ -630,7 +637,7 @@
                    jax.ShapeDtypeStruct((n_local, d_model, d_ff), jnp.float32),
                    jax.ShapeDtypeStruct((n_dev, n_local, cap, d_model), jnp.bfloat16),
                    jax.ShapeDtypeStruct(prob.shape, jnp.float32),
-                   jax.ShapeDtypeStruct((n_dev, 8, d_model), jnp.float32),
+                   jax.ShapeDtypeStruct((n_dev, 8, 128), jnp.float32),
                    jax.ShapeDtypeStruct(stats.shape, jnp.float32)),
         in_specs=[any_spec, any_spec, vmem_spec, any_spec, any_spec, any_spec] + [vmem_spec] * 5,
         out_specs=(any_spec, any_spec, any_spec, vmem_spec, vmem_spec, vmem_spec),
@@ -641,13 +648,13 @@
             pltpu.VMEM(w_in.shape, jnp.float32),
             pltpu.VMEM(x_tokens.shape, jnp.bfloat16),
             pltpu.VMEM((3 * pairs, d_model), jnp.float32),
-            pltpu.VMEM((n_dev, 8, d_model), jnp.float32),
-            pltpu.VMEM((n_dev, 8, d_model), jnp.float32),
-            pltpu.VMEM((8, d_model), jnp.float32),
+            pltpu.VMEM((n_dev, 8, 128), jnp.float32),
+            pltpu.VMEM((n_dev, 8, 128), jnp.float32),
+            pltpu.VMEM((8, 128), jnp.float32),
             pltpu.VMEM((n_dev, n_local, 2, cap, d_model), jnp.bfloat16),
-            pltpu.VMEM((n_dev, 8, lanes), jnp.float32),
-            pltpu.VMEM((n_dev, 8, lanes), jnp.float32),
-            pltpu.VMEM((n_dev, 8, lanes), jnp.float32),
+            pltpu.VMEM((n_dev, 8, 128), jnp.float32),
+            pltpu.VMEM((n_dev, 8, 128), jnp.float32),
+            pltpu.VMEM((n_dev, 8, 128), jnp.float32),
             pltpu.VMEM((n_dev,) + stats.shape, jnp.float32),
             dma((2 * pairs,)), dma((2 * pairs,)), dma((n_dev,)), dma((n_dev,)),
             dma((pairs,)), dma((pairs,)), dma((n_dev,)), dma((n_dev,)),
@@ -676,7 +683,7 @@
         gw_in, gw_out_t, back, d_logits, gwr, stats = exchange(xd, gates, stats, w_in, w_out, x_tokens, prob, pos_rows, idx_rows,
                                                                gate_rows, norm_rows, n_dev)
         grad_x, grad_w_in, grad_w_out = combine(slot_rows, back, d_logits, w_router, gw_in, gw_out_t)
-        grad_w_router = gwr[:, :n_local].reshape(num_experts, d_model).T
+        grad_w_router = gwr[:, :n_local * d_model // 128].reshape(num_experts, d_model).T
 
         load_frac = stats[0, :num_experts] / total_tok
         mean_prob = stats[0, num_experts:2 * num_experts] / total_tok

time: 360 us -> 354 us (0.983)
  Pallas kernels: 348 us -> 343 us
    pallas_call x1, Pallas kernels: 281 us -> 275 us  [exchange(): pl.pallas_call(functools.partial(exchange_kernel, n_dev, n_local, x_token...]
where the time goes in v9:
time: 354 us; the launch traced here: 353 us
  Pallas kernels  343 us (97%)
  local copies, waits for them, and re-layouts  4.66 us (1%)
  between operations  4.22 us (1%)
    pallas_call x1, Pallas kernels, exchange(): pl.pallas_call(functools.partial(exchange_kernel, n_dev, n_local, x_token...  275 us
    pallas_call x1, Pallas kernels, dispatch(): pl.pallas_call(functools.partial(dispatch_kernel, steps, capacity, lanes...  30.4 us
    pallas_call x1, Pallas kernels, combine(): pl.pallas_call(functools.partial(combine_kernel, fills, n_dev, capacity),...  27.8 us
    pallas_call x1, Pallas kernels, route(): pl.pallas_call(functools.partial(route_kernel, capacity), grid=(steps,),...  8.95 us

profile of v9, /device:TPU:0, one launch (start us, length us, event | category | flops | bytes accessed | tf_op | source)
XLA Modules:
  0.0 352.9 jit_solution(7966292852730775078)
XLA Ops:
  0.6 1.4 reshape.34.idx_ref
  2.0 9.0 %route.1 = (f32[32,8192]{1,0:T(8,128)}, s32[8,1024]{1,0:T(8,128)}, s32[8,1024]{1,0:T(8,128)}, f32[8,1024]{1,0:T(8,128)}, f32[8,1024]{1,0:T(8,128)}, /*index=5*/f32[8,128]{1,0:T(8,128)}) custom-call(bf16[8192,384]{1,0:T(8,128)(2,1)} %x_hbm.1, s32[8,1024]{1,0:T(8,128)} %reshape.34.idx_ref, f32[32,384]{1,0:T(8,128)} %bitcast.13), custom_call_target="tpu_custom_call" | custom-call | tf_op jit(solution)/shard_map/route/pallas_call | solution.py:97
  11.0 1.4 copy.14
  12.3 30.4 %dispatch.1 = (bf16[16,2,2,320,384]{4,3,2,1,0:T(8,128)(2,1)}, f32[16,8,128]{2,1,0:T(8,128)}) custom-call(s32[8192]{0:T(1024)} %bitcast.11, bf16[8192,384]{1,0:T(8,128)(2,1)} %x_hbm.1, bf16[8192,384]{1,0:T(8,128)(2,1)} %dy_ref.1, f32[8,1024]{1,0:T(8,128)} %get-tuple-element.24.gate_ref.gate_rows_ref), custom_call_target="tpu_custom_call" | custom-call | tf_op jit(solution)/shard_map/dispatch/pallas_call | solution.py:176
  42.8 275.4 %exchange.1 = (f32[2,384,1536]{2,1,0:T(8,128)}, f32[2,384,1536]{2,1,0:T(8,128)}, bf16[16,2,320,384]{3,2,1,0:T(8,128)(2,1)}, f32[32,8192]{1,0:T(8,128)}, f32[16,8,128]{2,1,0:T(8,128)}, /*index=5*/f32[8,128]{1,0:T(8,128)}) custom-call(bf16[16,2,2,320,384]{4,3,2,1,0:T(8,128)(2,1)} %get-tuple-element.25.xd_ref, f32[16,8,128]{2,1,0:T(8,128)} %get-tuple-element.26.gate_ref, ...), custom_call_target="tpu_custom_call" | custom-call | tf_op jit(solution)/shard_map/exchange/pallas_call | solution.py:634
  318.2 1.4 multiply_reduce_fusion
  320.3 1.3 slice.15
  322.2 0.0 copy-start
  322.2 27.8 %combine.1 = (bf16[8192,384]{1,0:T(8,128)(2,1)}, f32[768,1536]{1,0:T(8,128)}, f32[2,1536,384]{2,1,0:T(8,128)}) custom-call(s32[8192]{0:T(1024)} %bitcast.12, bf16[16,2,320,384]{3,2,1,0:T(8,128)(2,1)} %get-tuple-element.31.back_ref, f32[32,8192]{1,0:T(8,128)} %get-tuple-element.32.dl_ref, f32[32,384]{1,0:T(8,128)} %bitcast.14, f32[768,1536]{1,0:T(8,128)} %bitcast.10, ...), custom_call_target="tpu_custom_call" | custom-call | tf_op jit(solution)/shard_map/combine/pallas_call | solution.py:259
  350.0 0.0 copy-done
  350.0 0.6 reshape.38
Async XLA Ops:
  322.2 27.8 %copy-start = (f32[16,8,128]{2,1,0:T(8,128)S(1)}, f32[16,8,128]{2,1,0:T(8,128)}, u32[]{:S(2)}) copy-start(f32[16,8,128]{2,1,0:T(8,128)} %get-tuple-element.38) | copy-start | bytes 196612

commit v10 on v9

--- a/solution.py
+++ b/solution.py
@@ -13,13 +13,15 @@
 F_CHUNK = 512
 TOKEN_BLOCK = 256
 UNROLL = 32
+LANE = 128
+F32 = jnp.float32
 ROW_GROUP = 32
 ROW_TOKENS = 1024
 GROUP = 2
 
 
 def nt_dot(a, b):
-    return lax.dot_general(a, b, (((1,), (1,)), ((), ())), preferred_element_type=jnp.float32)
+    return lax.dot_general(a, b, (((1,), (1,)), ((), ())), preferred_element_type=F32)
 
 
 def eye_mask(rows, cols):
@@ -57,9 +59,9 @@
     gate_ref[pl.ds(step, 1), :] = jnp.sum(prob * chosen, axis=0, keepdims=True)
     norm_ref[pl.ds(step, 1), :] = log_norm
     squares = log_norm * log_norm
-    for i in range(0, block, 128):
-        prob_sum[...] += prob[:, i:i + 128]
-        z_sum[0:1, :] += squares[:, i:i + 128]
+    for i in range(0, block, LANE):
+        prob_sum[...] += prob[:, i:i + LANE]
+        z_sum[0:1, :] += squares[:, i:i + LANE]
     upto = jnp.where(lax.broadcasted_iota(jnp.int32, (TOKEN_BLOCK, TOKEN_BLOCK), 0)
                      <= lax.broadcasted_iota(jnp.int32, (TOKEN_BLOCK, TOKEN_BLOCK), 1), 1.0, 0.0).astype(jnp.bfloat16)
     before = seen[:, 0:1]
@@ -67,7 +69,7 @@
     places = []
     for i in range(0, block, TOKEN_BLOCK):
         part = chosen[:, i:i + TOKEN_BLOCK]
-        count = jnp.dot(part.astype(jnp.bfloat16), upto, preferred_element_type=jnp.float32) + before
+        count = jnp.dot(part.astype(jnp.bfloat16), upto, preferred_element_type=F32) + before
         position = jnp.sum(part * count, axis=0, keepdims=True).astype(jnp.int32) - 1
         places.append(position)
         slots.append(8 * jnp.where(position < capacity, idx[:, i:i + TOKEN_BLOCK] * capacity + position, num_experts * capacity))
@@ -78,8 +80,8 @@
 
     @pl.when(step == pl.num_programs(0) - 1)
     def _():
-        row = lax.broadcasted_iota(jnp.int32, (num_experts, 128), 0)
-        lane = lax.broadcasted_iota(jnp.int32, (num_experts, 128), 1)
+        row = lax.broadcasted_iota(jnp.int32, (num_experts, LANE), 0)
+        lane = lax.broadcasted_iota(jnp.int32, (num_experts, LANE), 1)
         probs = jnp.sum(prob_sum[...], axis=1, keepdims=True)
         stat_ref[...] = jnp.zeros_like(stat_ref)
         total = jnp.sum(jnp.where(row == lane, seen[...], 0.0) + jnp.where(row + num_experts == lane, probs, 0.0),
@@ -98,12 +100,12 @@
         functools.partial(route_kernel, capacity),
         grid=(steps,),
         out_shape=(jax.ShapeDtypeStruct((num_experts, tokens), jnp.float32), rows(jnp.int32), rows(jnp.int32), rows(jnp.float32), rows(jnp.float32),
-                   jax.ShapeDtypeStruct((8, 128), jnp.float32)),
+                   jax.ShapeDtypeStruct((8, LANE), jnp.float32)),
         in_specs=[pl.BlockSpec((block, d_model), lambda i: (i, 0)), whole,
                   pl.BlockSpec((num_experts, d_model), lambda i: (0, 0))],
         out_specs=(pl.BlockSpec((num_experts, block), lambda i: (0, i)), whole, whole, whole, whole,
-                   pl.BlockSpec((8, 128), lambda i: (0, 0))),
-        scratch_shapes=[pltpu.VMEM((num_experts, 128), jnp.float32), pltpu.VMEM((num_experts, 128), jnp.float32), pltpu.VMEM((8, 128), jnp.float32)],
+                   pl.BlockSpec((8, LANE), lambda i: (0, 0))),
+        scratch_shapes=[pltpu.VMEM((num_experts, LANE), jnp.float32), pltpu.VMEM((num_experts, LANE), jnp.float32), pltpu.VMEM((8, LANE), jnp.float32)],
         compiler_params=pltpu.CompilerParams(dimension_semantics=('arbitrary',)),
         name='route',
     )(x_tokens, idx_rows, w_router.T)
@@ -112,13 +114,13 @@
 def dispatch_kernel(steps, capacity, lane_cols, slot_ref, x_ref, dy_ref, gate_ref, xd_ref, gates_ref, table, stage):
     step = pl.program_id(0)
     block, d_model = x_ref.shape
-    cols = d_model // 128
+    cols = d_model // LANE
     group, n_local = xd_ref.shape[:2]
 
     @pl.when(step == 0)
     def _():
         def clear(i, carry):
-            table[pl.ds(pl.multiple_of(i * 512, 512), 512), :] = jnp.zeros((512, 128), jnp.float32)
+            table[pl.ds(pl.multiple_of(i * 512, 512), 512), :] = jnp.zeros((512, LANE), jnp.float32)
             return carry
         lax.fori_loop(0, table.shape[0] // 512, clear, 0)
 
@@ -127,13 +129,13 @@
         for r in range(0, block, ROW_GROUP):
             for c in range(2 * cols):
                 rows_ref = x_ref if c < cols else dy_ref
-                span = slice(c % cols * 128, (c % cols + 1) * 128)
+                span = slice(c % cols * LANE, (c % cols + 1) * LANE)
                 stage[pl.ds(r * 8 + c, ROW_GROUP, stride=8), :] = rows_ref[r:r + ROW_GROUP, span].astype(jnp.float32)
-        eye = eye_mask(128, 128)
+        eye = eye_mask(LANE, LANE)
         gate_row = gate_ref[pl.ds(step, 1), :]
-        for i in range(0, block, 128):
-            gate = jnp.sum(jnp.where(eye, gate_row[:, i:i + 128], 0.0), axis=1, keepdims=True)
-            stage[pl.ds(i * 8 + 2 * cols, 128, stride=8), :] = jnp.broadcast_to(gate, (128, 128))
+        for i in range(0, block, LANE):
+            gate = jnp.sum(jnp.where(eye, gate_row[:, i:i + LANE], 0.0), axis=1, keepdims=True)
+            stage[pl.ds(i * 8 + 2 * cols, LANE, stride=8), :] = jnp.broadcast_to(gate, (LANE, LANE))
 
         def place(i, carry):
             for u in range(UNROLL):
@@ -146,8 +148,8 @@
     @pl.when(step >= steps)
     def _():
         gates_ref[...] = jnp.zeros_like(gates_ref)
-        row = lax.broadcasted_iota(jnp.int32, (capacity, 128), 0)
-        lane = lax.broadcasted_iota(jnp.int32, (capacity, 128), 1)
+        row = lax.broadcasted_iota(jnp.int32, (capacity, LANE), 0)
+        lane = lax.broadcasted_iota(jnp.int32, (capacity, LANE), 1)
 
         def unload(i, carry):
             d = i // n_local
@@ -155,13 +157,13 @@
             first = (((step - steps) * group + d) * n_local + e) * (capacity * 8)
             for r in range(0, capacity, ROW_GROUP):
                 for c in range(2 * cols):
-                    span = slice(c % cols * 128, (c % cols + 1) * 128)
+                    span = slice(c % cols * LANE, (c % cols + 1) * LANE)
                     xd_ref[d, e, c // cols, r:r + ROW_GROUP, span] = table[
                         pl.ds(first + r * 8 + c, ROW_GROUP, stride=8), :].astype(jnp.bfloat16)
             gate = table[pl.ds(first + 2 * cols, capacity, stride=8), :]
             for c in range(lane_cols):
                 gates_ref[d, pl.ds(e * lane_cols + c, 1), :] = jnp.sum(
-                    jnp.where(row == lane + c * 128, gate, 0.0), axis=0, keepdims=True)
+                    jnp.where(row == lane + c * LANE, gate, 0.0), axis=0, keepdims=True)
             return carry
         lax.fori_loop(0, group * n_local, unload, 0)
 
@@ -174,18 +176,18 @@
     tok = lambda i: (jnp.minimum(i, steps - 1), 0)
     dst = lambda i: jnp.maximum(i - steps, 0)
     return pl.pallas_call(
-        functools.partial(dispatch_kernel, steps, capacity, lanes // 128),
+        functools.partial(dispatch_kernel, steps, capacity, lanes // LANE),
         grid=(steps + n_dev // GROUP,),
         out_shape=(jax.ShapeDtypeStruct((n_dev, n_local, 2, capacity, d_model), jnp.bfloat16),
-                   jax.ShapeDtypeStruct((n_dev, 8, 128), jnp.float32)),
+                   jax.ShapeDtypeStruct((n_dev, 8, LANE), jnp.float32)),
         in_specs=[pl.BlockSpec(memory_space=pltpu.SMEM),
                   pl.BlockSpec((block, d_model), tok),
                   pl.BlockSpec((block, d_model), tok),
                   pl.BlockSpec((steps, block), lambda i: (0, 0))],
         out_specs=(pl.BlockSpec((GROUP, n_local, 2, capacity, d_model), lambda i: (dst(i), 0, 0, 0, 0)),
-                   pl.BlockSpec((GROUP, 8, 128), lambda i: (dst(i), 0, 0))),
-        scratch_shapes=[pltpu.VMEM((table_rows, 128), jnp.float32),
-                        pltpu.VMEM((block * 8, 128), jnp.float32)],
+                   pl.BlockSpec((GROUP, 8, LANE), lambda i: (dst(i), 0, 0))),
+        scratch_shapes=[pltpu.VMEM((table_rows, LANE), jnp.float32),
+                        pltpu.VMEM((block * 8, LANE), jnp.float32)],
         compiler_params=pltpu.CompilerParams(dimension_semantics=('arbitrary',), vmem_limit_bytes=62 * 1024 * 1024),
         name='dispatch',
     )(slot_rows, x_tokens, grad_y, gate_rows)
@@ -195,7 +197,7 @@
                    gx_ref, gwi_out_ref, gwo_out_ref, table, stage):
     step = pl.program_id(0)
     block, d_model = gx_ref.shape
-    cols = d_model // 128
+    cols = d_model // LANE
     group, n_local = back_ref.shape[:2]
     n_slots = sources * n_local * capacity
     gwi_out_ref[...] = gwi_ref[...]
@@ -203,7 +205,7 @@
 
     @pl.when(step == 0)
     def _():
-        table[pl.ds(n_slots * 8, 8), :] = jnp.zeros((8, 128), jnp.float32)
+        table[pl.ds(n_slots * 8, 8), :] = jnp.zeros((8, LANE), jnp.float32)
 
     @pl.when(step < fills)
     def _():
@@ -214,7 +216,7 @@
             for r in range(0, capacity, ROW_GROUP):
                 for c in range(cols):
                     table[pl.ds(first + r * 8 + c, ROW_GROUP, stride=8), :] = back_ref[
-                        d, e, r:r + ROW_GROUP, c * 128:(c + 1) * 128].astype(jnp.float32)
+                        d, e, r:r + ROW_GROUP, c * LANE:(c + 1) * LANE].astype(jnp.float32)
             return carry
         lax.fori_loop(0, group * n_local, load, 0)
 
@@ -233,10 +235,10 @@
         left = jnp.concatenate([hi, mid, hi, low, mid, hi], axis=0)
         w_hi, w_mid, w_low = split3(wr_t_ref[...])
         right = jnp.concatenate([w_hi, w_hi, w_mid, w_hi, w_mid, w_low], axis=0)
-        dx_router = lax.dot_general(left, right, (((0,), (0,)), ((), ())), preferred_element_type=jnp.float32)
+        dx_router = lax.dot_general(left, right, (((0,), (0,)), ((), ())), preferred_element_type=F32)
         for r in range(0, block, ROW_GROUP):
             for c in range(cols):
-                span = slice(c * 128, (c + 1) * 128)
+                span = slice(c * LANE, (c + 1) * LANE)
                 gx_ref[r:r + ROW_GROUP, span] = (stage[pl.ds(r * 8 + c, ROW_GROUP, stride=8), :]
                                                  + dx_router[r:r + ROW_GROUP, span]).astype(jnp.bfloat16)
 
@@ -271,8 +273,8 @@
         out_specs=(pl.BlockSpec((block, d_model), tok),
                    pl.BlockSpec((in_rows, d_ff), lambda i: (i, 0)),
                    pl.BlockSpec((1, 256, d_model), lambda i: (flip(i) // out_cols, flip(i) % out_cols, 0))),
-        scratch_shapes=[pltpu.VMEM(((n_slots + 1) * 8, 128), jnp.float32),
-                        pltpu.VMEM((block * 8, 128), jnp.float32)],
+        scratch_shapes=[pltpu.VMEM(((n_slots + 1) * 8, LANE), jnp.float32),
+                        pltpu.VMEM((block * 8, LANE), jnp.float32)],
         compiler_params=pltpu.CompilerParams(dimension_semantics=('arbitrary',), vmem_limit_bytes=63 * 1024 * 1024),
         name='combine',
     )(slot_rows, back, d_logits, w_router.T, gw_in_rows, gw_out_t)
@@ -424,8 +426,8 @@
     for c in weights:
         c.wait()
 
-    lane_cols = -(-cap // 128)
-    lanes = lane_cols * 128
+    lane_cols = -(-cap // LANE)
+    lanes = lane_cols * LANE
 
     def tile(k, e):
         eye = (lax.broadcasted_iota(jnp.int32, (cap, lanes), 0)
@@ -443,19 +445,19 @@
             fs = pl.ds(f, F_CHUNK)
             w_a = w_in_ref[e, :, fs]
             w_b = w_out_ref[e, fs, :]
-            pre = jnp.dot(rows, w_a, preferred_element_type=jnp.float32)
+            pre = jnp.dot(rows, w_a, preferred_element_type=F32)
             hid = jnp.maximum(pre, 0.0).astype(jnp.bfloat16)
-            out = out + jnp.dot(hid, w_b, preferred_element_type=jnp.float32)
+            out = out + jnp.dot(hid, w_b, preferred_element_type=F32)
             d_hid = nt_dot(grad, w_b)
             d_pre = jnp.where(hid.astype(jnp.float32) > 0, d_hid, 0.0).astype(jnp.bfloat16)
-            gw_out_t_ref[e, :, fs] += jnp.dot(grad_t, hid, preferred_element_type=jnp.float32)
-            gw_in_ref[e, :, fs] += jnp.dot(rows_t, d_pre, preferred_element_type=jnp.float32)
+            gw_out_t_ref[e, :, fs] += jnp.dot(grad_t, hid, preferred_element_type=F32)
+            gw_in_ref[e, :, fs] += jnp.dot(rows_t, d_pre, preferred_element_type=F32)
             d_rows = d_rows + nt_dot(d_pre, w_a)
         out = out.astype(jnp.bfloat16).astype(jnp.float32)
         g_col = jnp.sum(out * dy, axis=1, keepdims=True)
         g_row = jnp.sum(jnp.where(eye, g_col, 0.0), axis=0, keepdims=True)
         for c in range(lane_cols):
-            g_s[k, pl.ds(e * lane_cols + c, 1), :] = g_row[:, c * 128:(c + 1) * 128]
+            g_s[k, pl.ds(e * lane_cols + c, 1), :] = g_row[:, c * LANE:(c + 1) * LANE]
         xr[k, e, 0] = d_rows.astype(jnp.bfloat16)
 
     order = [(0, e) for e in range(n_local)] + near[0]
@@ -536,7 +538,7 @@
         stat = stat + stat_r[i]
     stat_out_ref[...] = stat
     num_experts = n * n_local
-    load = jnp.sum(jnp.where(eye_mask(num_experts, 128), stat[0:1, :], 0.0), axis=1, keepdims=True)
+    load = jnp.sum(jnp.where(eye_mask(num_experts, LANE), stat[0:1, :], 0.0), axis=1, keepdims=True)
     aux_vec = (AUX_WEIGHT * num_experts / total_tok) * (load / total_tok)
     g_all = jnp.concatenate([
         jnp.concatenate([g_r[:, e * lane_cols + c, :] for c in range(lane_cols)], axis=1) for e in range(n_local)], axis=0)
@@ -548,7 +550,7 @@
         here = pl.ds(c, 1)
         cols = pl.ds(pl.multiple_of(c * span, span), span)
         place = jnp.where(lax.broadcasted_iota(jnp.int32, (lanes, span), 0) == pos_ref[here, :], 1.0, 0.0)
-        found = jnp.dot(g_parts, place.astype(jnp.bfloat16), preferred_element_type=jnp.float32)
+        found = jnp.dot(g_parts, place.astype(jnp.bfloat16), preferred_element_type=F32)
         found = found[:num_experts] + found[num_experts:2 * num_experts] + found[2 * num_experts:]
         chosen = jnp.where(lax.broadcasted_iota(jnp.int32, (num_experts, span), 0) == idx_ref[here, :], 1.0, 0.0)
         row = lax.broadcasted_iota(jnp.int32, (num_experts, span), 0)
@@ -559,16 +561,16 @@
         d_logits = ((gate_rows_ref[here, :] * g_tok) * (chosen - prob) + prob * (aux_vec - spread)
                     + ((2.0 * Z_WEIGHT / total_tok) * norm_ref[here, :]) * prob)
         dl_ref[:, cols] = d_logits
-        gwr_acc[...] += jnp.dot(jnp.concatenate(split3(d_logits), axis=0), x_ref[cols, :], preferred_element_type=jnp.float32)
+        gwr_acc[...] += jnp.dot(jnp.concatenate(split3(d_logits), axis=0), x_ref[cols, :], preferred_element_type=F32)
         return carry
 
     lax.fori_loop(0, pos_ref.shape[0], router, 0)
     part = gwr_acc[0:num_experts, :] + gwr_acc[num_experts:2 * num_experts, :] + gwr_acc[2 * num_experts:, :]
-    d_cols = d_model // 128
+    d_cols = d_model // LANE
     for d in range(n):
         for c in range(n_local * d_cols):
             r = d * n_local + c // d_cols
-            gwr_s[d, c:c + 1, :] = part[r:r + 1, c % d_cols * 128:(c % d_cols + 1) * 128]
+            gwr_s[d, c:c + 1, :] = part[r:r + 1, c % d_cols * LANE:(c % d_cols + 1) * LANE]
     gwr_r[me] = gwr_s[me]
 
     def scatter(k, carry):
@@ -637,7 +639,7 @@
                    jax.ShapeDtypeStruct((n_local, d_model, d_ff), jnp.float32),
                    jax.ShapeDtypeStruct((n_dev, n_local, cap, d_model), jnp.bfloat16),
                    jax.ShapeDtypeStruct(prob.shape, jnp.float32),
-                   jax.ShapeDtypeStruct((n_dev, 8, 128), jnp.float32),
+                   jax.ShapeDtypeStruct((n_dev, 8, LANE), jnp.float32),
                    jax.ShapeDtypeStruct(stats.shape, jnp.float32)),
         in_specs=[any_spec, any_spec, vmem_spec, any_spec, any_spec, any_spec] + [vmem_spec] * 5,
         out_specs=(any_spec, any_spec, any_spec, vmem_spec, vmem_spec, vmem_spec),
@@ -648,13 +650,13 @@
             pltpu.VMEM(w_in.shape, jnp.float32),
             pltpu.VMEM(x_tokens.shape, jnp.bfloat16),
             pltpu.VMEM((3 * pairs, d_model), jnp.float32),
-            pltpu.VMEM((n_dev, 8, 128), jnp.float32),
-            pltpu.VMEM((n_dev, 8, 128), jnp.float32),
-            pltpu.VMEM((8, 128), jnp.float32),
+            pltpu.VMEM((n_dev, 8, LANE), jnp.float32),
+            pltpu.VMEM((n_dev, 8, LANE), jnp.float32),
+            pltpu.VMEM((8, LANE), jnp.float32),
             pltpu.VMEM((n_dev, n_local, 2, cap, d_model), jnp.bfloat16),
-            pltpu.VMEM((n_dev, 8, 128), jnp.float32),
-            pltpu.VMEM((n_dev, 8, 128), jnp.float32),
-            pltpu.VMEM((n_dev, 8, 128), jnp.float32),
+            pltpu.VMEM((n_dev, 8, LANE), jnp.float32),
+            pltpu.VMEM((n_dev, 8, LANE), jnp.float32),
+            pltpu.VMEM((n_dev, 8, LANE), jnp.float32),
             pltpu.VMEM((n_dev,) + stats.shape, jnp.float32),
             dma((2 * pairs,)), dma((2 * pairs,)), dma((n_dev,)), dma((n_dev,)),
             dma((pairs,)), dma((pairs,)), dma((n_dev,)), dma((n_dev,)),
@@ -675,7 +677,7 @@
         num_experts = n_local * n_dev
         capacity = (5 * tokens + 4 * num_experts - 1) // (4 * num_experts)
         total_tok = tokens * n_dev
-        lanes = -(-capacity // 128) * 128
+        lanes = -(-capacity // LANE) * LANE
         idx_rows = expert_idx.reshape(-1, ROW_TOKENS)
         prob, slot_rows, pos_rows, gate_rows, norm_rows, stats = route(x_tokens, idx_rows, w_router, capacity)
         slot_rows = slot_rows.reshape(tokens)
@@ -683,7 +685,7 @@
         gw_in, gw_out_t, back, d_logits, gwr, stats = exchange(xd, gates, stats, w_in, w_out, x_tokens, prob, pos_rows, idx_rows,
                                                                gate_rows, norm_rows, n_dev)
         grad_x, grad_w_in, grad_w_out = combine(slot_rows, back, d_logits, w_router, gw_in, gw_out_t)
-        grad_w_router = gwr[:, :n_local * d_model // 128].reshape(num_experts, d_model).T
+        grad_w_router = gwr[:, :n_local * d_model // LANE].reshape(num_experts, d_model).T
 
         load_frac = stats[0, :num_experts] / total_tok
         mean_prob = stats[0, num_experts:2 * num_experts] / total_tok

time: 354 us -> 354 us (level)
  no operation moved by 1% of the time
where the time goes in v10:
time: 354 us; the launch traced here: 353 us
  Pallas kernels  343 us (97%)
  local copies, waits for them, and re-layouts  4.66 us (1%)
  between operations  4.22 us (1%)
    pallas_call x1, Pallas kernels, exchange(): pl.pallas_call(functools.partial(exchange_kernel, n_dev, n_local, x_token...  275 us
    pallas_call x1, Pallas kernels, dispatch(): pl.pallas_call(functools.partial(dispatch_kernel, steps, capacity, lanes...  30.4 us
    pallas_call x1, Pallas kernels, combine(): pl.pallas_call(functools.partial(combine_kernel, fills, n_dev, capacity),...  27.8 us
    pallas_call x1, Pallas kernels, route(): pl.pallas_call(functools.partial(route_kernel, capacity), grid=(steps,),...  8.95 us

profile of v10, /device:TPU:0, one launch (start us, length us, event | category | flops | bytes accessed | tf_op | source)
XLA Modules:
  0.0 352.9 jit_solution(7966292852730775078)
XLA Ops:
  0.6 1.4 reshape.34.idx_ref
  2.0 9.0 %route.1 = (f32[32,8192]{1,0:T(8,128)}, s32[8,1024]{1,0:T(8,128)}, s32[8,1024]{1,0:T(8,128)}, f32[8,1024]{1,0:T(8,128)}, f32[8,1024]{1,0:T(8,128)}, /*index=5*/f32[8,128]{1,0:T(8,128)}) custom-call(bf16[8192,384]{1,0:T(8,128)(2,1)} %x_hbm.1, s32[8,1024]{1,0:T(8,128)} %reshape.34.idx_ref, f32[32,384]{1,0:T(8,128)} %bitcast.13), custom_call_target="tpu_custom_call" | custom-call | tf_op jit(solution)/shard_map/route/pallas_call | solution.py:99
  11.0 1.4 copy.14
  12.3 30.4 %dispatch.1 = (bf16[16,2,2,320,384]{4,3,2,1,0:T(8,128)(2,1)}, f32[16,8,128]{2,1,0:T(8,128)}) custom-call(s32[8192]{0:T(1024)} %bitcast.11, bf16[8192,384]{1,0:T(8,128)(2,1)} %x_hbm.1, bf16[8192,384]{1,0:T(8,128)(2,1)} %dy_ref.1, f32[8,1024]{1,0:T(8,128)} %get-tuple-element.24.gate_ref.gate_rows_ref), custom_call_target="tpu_custom_call" | custom-call | tf_op jit(solution)/shard_map/dispatch/pallas_call | solution.py:178
  42.8 275.4 %exchange.1 = (f32[2,384,1536]{2,1,0:T(8,128)}, f32[2,384,1536]{2,1,0:T(8,128)}, bf16[16,2,320,384]{3,2,1,0:T(8,128)(2,1)}, f32[32,8192]{1,0:T(8,128)}, f32[16,8,128]{2,1,0:T(8,128)}, /*index=5*/f32[8,128]{1,0:T(8,128)}) custom-call(bf16[16,2,2,320,384]{4,3,2,1,0:T(8,128)(2,1)} %get-tuple-element.25.xd_ref, f32[16,8,128]{2,1,0:T(8,128)} %get-tuple-element.26.gate_ref, ...), custom_call_target="tpu_custom_call" | custom-call | tf_op jit(solution)/shard_map/exchange/pallas_call | solution.py:636
  318.2 1.4 multiply_reduce_fusion
  320.3 1.3 slice.15
  322.2 0.0 copy-start
  322.2 27.8 %combine.1 = (bf16[8192,384]{1,0:T(8,128)(2,1)}, f32[768,1536]{1,0:T(8,128)}, f32[2,1536,384]{2,1,0:T(8,128)}) custom-call(s32[8192]{0:T(1024)} %bitcast.12, bf16[16,2,320,384]{3,2,1,0:T(8,128)(2,1)} %get-tuple-element.31.back_ref, f32[32,8192]{1,0:T(8,128)} %get-tuple-element.32.dl_ref, f32[32,384]{1,0:T(8,128)} %bitcast.14, f32[768,1536]{1,0:T(8,128)} %bitcast.10, ...), custom_call_target="tpu_custom_call" | custom-call | tf_op jit(solution)/shard_map/combine/pallas_call | solution.py:261
  350.0 0.0 copy-done
  350.0 0.6 reshape.38
Async XLA Ops:
  322.2 27.8 %copy-start = (f32[16,8,128]{2,1,0:T(8,128)S(1)}, f32[16,8,128]{2,1,0:T(8,128)}, u32[]{:S(2)}) copy-start(f32[16,8,128]{2,1,0:T(8,128)} %get-tuple-element.38) | copy-start | bytes 196612

commit v11 on v10

--- a/solution.py
+++ b/solution.py
@@ -385,10 +385,9 @@
 
     def rows_left(queues):
         for queue in queues:
-            for i, (k, e) in enumerate(queue):
-                fwd_copy(k, e, 0).wait_send()
-                if i < len(queue) - 1:
-                    fwd_copy(k, e, 1).wait_send()
+            for k, e in queue[:-1]:
+                for part in range(2):
+                    fwd_copy(k, e, part).wait_send()
 
     def send_grads(queues, lo=0, hi=None):
         for k, e in interleave(queues)[lo:hi]:
@@ -601,7 +600,8 @@
     for queues in sets:
         for queue in queues:
             k, e = queue[-1]
-            fwd_copy(k, e, 1).wait_send()
+            for part in range(2):
+                fwd_copy(k, e, part).wait_send()
             if queues is not sets[3]:
                 ret_copy(k, e).wait_send()
     grads_left(sets[3])

time: 354 us -> 354 us (level)
  no operation moved by 1% of the time
where the time goes in v11:
time: 354 us; the launch traced here: 353 us
  Pallas kernels  343 us (97%)
  local copies, waits for them, and re-layouts  4.66 us (1%)
  between operations  4.22 us (1%)
    pallas_call x1, Pallas kernels, exchange(): pl.pallas_call(functools.partial(exchange_kernel, n_dev, n_local, x_token...  275 us
    pallas_call x1, Pallas kernels, dispatch(): pl.pallas_call(functools.partial(dispatch_kernel, steps, capacity, lanes...  30.4 us
    pallas_call x1, Pallas kernels, combine(): pl.pallas_call(functools.partial(combine_kernel, fills, n_dev, capacity),...  27.8 us
    pallas_call x1, Pallas kernels, route(): pl.pallas_call(functools.partial(route_kernel, capacity), grid=(steps,),...  8.95 us

profile of v11, /device:TPU:0, one launch (start us, length us, event | category | flops | bytes accessed | tf_op | source)
XLA Modules:
  0.0 352.9 jit_solution(17743112913104690361)
XLA Ops:
  0.6 1.4 reshape.34.idx_ref
  2.0 9.0 %route.1 = (f32[32,8192]{1,0:T(8,128)}, s32[8,1024]{1,0:T(8,128)}, s32[8,1024]{1,0:T(8,128)}, f32[8,1024]{1,0:T(8,128)}, f32[8,1024]{1,0:T(8,128)}, /*index=5*/f32[8,128]{1,0:T(8,128)}) custom-call(bf16[8192,384]{1,0:T(8,128)(2,1)} %x_hbm.1, s32[8,1024]{1,0:T(8,128)} %reshape.34.idx_ref, f32[32,384]{1,0:T(8,128)} %bitcast.13), custom_call_target="tpu_custom_call" | custom-call | tf_op jit(solution)/shard_map/route/pallas_call | solution.py:99
  11.0 1.4 copy.14
  12.3 30.4 %dispatch.1 = (bf16[16,2,2,320,384]{4,3,2,1,0:T(8,128)(2,1)}, f32[16,8,128]{2,1,0:T(8,128)}) custom-call(s32[8192]{0:T(1024)} %bitcast.11, bf16[8192,384]{1,0:T(8,128)(2,1)} %x_hbm.1, bf16[8192,384]{1,0:T(8,128)(2,1)} %dy_ref.1, f32[8,1024]{1,0:T(8,128)} %get-tuple-element.24.gate_ref.gate_rows_ref), custom_call_target="tpu_custom_call" | custom-call | tf_op jit(solution)/shard_map/dispatch/pallas_call | solution.py:178
  42.8 275.4 %exchange.1 = (f32[2,384,1536]{2,1,0:T(8,128)}, f32[2,384,1536]{2,1,0:T(8,128)}, bf16[16,2,320,384]{3,2,1,0:T(8,128)(2,1)}, f32[32,8192]{1,0:T(8,128)}, f32[16,8,128]{2,1,0:T(8,128)}, /*index=5*/f32[8,128]{1,0:T(8,128)}) custom-call(bf16[16,2,2,320,384]{4,3,2,1,0:T(8,128)(2,1)} %get-tuple-element.25.xd_ref, f32[16,8,128]{2,1,0:T(8,128)} %get-tuple-element.26.gate_ref, ...), custom_call_target="tpu_custom_call" | custom-call | tf_op jit(solution)/shard_map/exchange/pallas_call | solution.py:636
  318.2 1.4 multiply_reduce_fusion
  320.3 1.3 slice.15
  322.2 0.0 copy-start
  322.2 27.8 %combine.1 = (bf16[8192,384]{1,0:T(8,128)(2,1)}, f32[768,1536]{1,0:T(8,128)}, f32[2,1536,384]{2,1,0:T(8,128)}) custom-call(s32[8192]{0:T(1024)} %bitcast.12, bf16[16,2,320,384]{3,2,1,0:T(8,128)(2,1)} %get-tuple-element.31.back_ref, f32[32,8192]{1,0:T(8,128)} %get-tuple-element.32.dl_ref, f32[32,384]{1,0:T(8,128)} %bitcast.14, f32[768,1536]{1,0:T(8,128)} %bitcast.10, ...), custom_call_target="tpu_custom_call" | custom-call | tf_op jit(solution)/shard_map/combine/pallas_call | solution.py:261
  350.0 0.0 copy-done
  350.0 0.6 reshape.38
Async XLA Ops:
  322.2 27.8 %copy-start = (f32[16,8,128]{2,1,0:T(8,128)S(1)}, f32[16,8,128]{2,1,0:T(8,128)}, u32[]{:S(2)}) copy-start(f32[16,8,128]{2,1,0:T(8,128)} %get-tuple-element.38) | copy-start | bytes 196612
